TPU v7x, 32 devices: a whole 2x2x4 slice. The times are simulated.
32 devices in a mesh: lat: 4 (over y, x), lon: 4 (over z), lev: 2 (over core).
Axes of the slice: x: 2, y: 2, z: 4, core: 2. Of those that a mesh axis runs over, the one named last changes fastest.
Arguments:
- increment: float32 [80, 64, 512], P('lev', 'lat', 'lon'), may hold values from -6 to 6
- wind_u: float32 [80, 64, 512], P('lev', 'lat', 'lon'), may hold values from -0.4 to 0.4
- wind_v: float32 [80, 64, 512], P('lev', 'lat', 'lon'), may hold values from -0.4 to 0.4
- diffusion: float32 [80], P('lev'), may hold values from 0.02 to 0.2
- mixing: float32 [80, 80], P('lev'), may hold values from -0.15625 to 0.15625
- jacobian: bfloat16 [128, 80], P(None, 'lev'), may hold values from -0.625 to 0.625
- obs_weight: float32 [128], replicated, may hold values from 0.5 to 4
- innovation: bfloat16 [2, 4, 4, 16, 128, 128], P(None, 'lat', 'lon'), may hold values from -6 to 6
- counts: int32 [4, 4], P('lat', 'lon'), may hold values from 1 to 16, as said below
- column_lookup: int32 [4, 4, 2048], P('lat', 'lon'), may hold values from 0 to 2047, each once within a row
Outputs:
- gradient: float32 [80, 64, 512], P('lev', 'lat', 'lon')
- cost: float32 [], replicated
Inputs may be any that keep to these rules, and one draw needn't show every extreme that they name: In every row of tiles with one latitude index the counts sum to 24, and the largest of them is 16.
All inputs are finite; a program needn't handle non-finite values.
Results may differ from a plain program's by a relative error of at most 0.005.
Values may be sent and summed in bfloat16 or wider, within the bound.
No kernel may reach another device: no remote copies, remote signals or barrier semaphores. Data moves between devices by JAX's collectives and lax.ppermute only.
A program may use at most 64 MiB of HBM per device.

v0:
```python
import jax
import jax.numpy as jnp
from jax import lax
from jax.sharding import PartitionSpec as P


def padded_2(cells, sides, width):
    for axis, dim in sides:
        count = lax.axis_size(axis)
        head = lax.slice_in_dim(cells, 0, width, axis=dim)
        tail = lax.slice_in_dim(cells, cells.shape[dim] - width, cells.shape[dim], axis=dim)
        cells = jnp.concatenate(
            [
                lax.ppermute(tail, axis, [(i, (i + 1) % count) for i in range(count)]),
                cells,
                lax.ppermute(head, axis, [((i + 1) % count, i) for i in range(count)]),
            ],
            axis=dim,
        )
    return cells


def neighbours(stacked):
    padded = padded_2(stacked, (("lat", 2), ("lon", 3)), 1)
    height = padded.shape[2]
    first_row = (lax.axis_index("lat") == 0).astype(jnp.float32)
    final_row = (lax.axis_index("lat") == lax.axis_size("lat") - 1).astype(jnp.float32)
    rim_mask = (
        jnp.ones((height,), jnp.float32)
        .at[0]
        .set(1.0 - first_row)
        .at[height - 1]
        .set(1.0 - final_row)
    )
    padded = padded * rim_mask[None, None, :, None]
    northern = padded[:, :, 2:, 1:-1]
    southern = padded[:, :, :-2, 1:-1]
    eastern = padded[:, :, 1:-1, 2:]
    western = padded[:, :, 1:-1, :-2]
    return (northern, southern, eastern, western)


def horizontal(field, diffusion, wind_u, wind_v):
    northern, southern, eastern, western = neighbours(field[None])
    coefficient = diffusion[:, None, None]
    result = field + coefficient * (
        northern[0] + southern[0] + eastern[0] + western[0] - 4.0 * field
    )
    return (
        result
        - 0.5 * wind_u * (eastern[0] - western[0])
        - 0.5 * wind_v * (northern[0] - southern[0])
    )


def horizontal_back(adjoint, diffusion, wind_u, wind_v):
    stacked = jnp.stack([adjoint, 0.5 * wind_u * adjoint, 0.5 * wind_v * adjoint])
    northern, southern, eastern, western = neighbours(stacked)
    coefficient = diffusion[:, None, None]
    result = adjoint + coefficient * (
        northern[0] + southern[0] + eastern[0] + western[0] - 4.0 * adjoint
    )
    return result + (eastern[1] - western[1]) + (northern[2] - southern[2])


def vertical(smooth, mixing):
    flat = smooth.reshape(smooth.shape[0], -1)
    mixed = jnp.dot(
        mixing,
        lax.all_gather(flat, "lev", axis=0, tiled=True),
        precision=lax.Precision.HIGHEST,
        preferred_element_type=jnp.float32,
    )
    return smooth + mixed.reshape(smooth.shape)


def vertical_back(adjoint, mixing):
    flat = adjoint.reshape(adjoint.shape[0], -1)
    dispersed_blocks = lax.psum_scatter(
        lax.dot_general(
            mixing,
            flat,
            (((0,), (0,)), ((), ())),
            precision=lax.Precision.HIGHEST,
            preferred_element_type=jnp.float32,
        ),
        "lev",
        scatter_dimension=0,
        tiled=True,
    )
    return adjoint + dispersed_blocks.reshape(adjoint.shape)


def take_profiles(state, columns, slot_count, block_width):
    level_count = state.shape[0]
    selected_columns = jnp.take(state.reshape(level_count, -1), columns, axis=1)
    return (
        selected_columns.reshape(level_count, slot_count, block_width)
        .astype(jnp.bfloat16)
        .transpose(1, 0, 2)
    )


def place_back(slots, inverse, shape):
    dispersed_blocks = slots.transpose(1, 0, 2).reshape(shape[0], -1).astype(jnp.float32)
    return jnp.take(dispersed_blocks, inverse, axis=1).reshape(shape)


def body(
    increment,
    wind_u,
    wind_v,
    diffusion,
    mixing,
    jacobian,
    obs_weight,
    innovation,
    counts,
    column_lookup,
):
    slot_count = column_lookup.shape[-1] // 128
    block_width = 128
    step_count = innovation.shape[0]
    channel_count = innovation.shape[-2]
    columns = column_lookup.reshape(-1)
    inverse = jnp.argsort(columns)
    live_float = (jnp.arange(slot_count) < counts.reshape(())).astype(jnp.float32)
    observed = innovation.reshape(step_count, slot_count, channel_count, block_width)
    jac_full = lax.all_gather(jacobian, "lev", axis=1, tiled=True)
    state = increment
    forcings = []
    misfit_total = jnp.zeros((), jnp.float32)
    for step in range(step_count):
        state = vertical(horizontal(state, diffusion, wind_u, wind_v), mixing)
        profiles = take_profiles(state, columns, slot_count, block_width)
        full_profiles = lax.all_gather(profiles, "lev", axis=1, tiled=True)
        evolved = jnp.einsum(
            "nl,slc->snc", jac_full, full_profiles, preferred_element_type=jnp.float32
        )
        misfit = live_float[:, None, None] * (evolved - observed[step].astype(jnp.float32))
        scaled = obs_weight[None, :, None] * misfit
        misfit_total = misfit_total + jnp.sum(misfit * scaled)
        slots = jnp.einsum(
            "nl,snc->slc", jacobian, scaled.astype(jnp.bfloat16), preferred_element_type=jnp.float32
        )
        slots = slots.astype(jnp.bfloat16)
        forcings.append(place_back(slots, inverse, increment.shape))
    adjoint = jnp.zeros_like(increment)
    for step in range(step_count - 1, -1, -1):
        coupled = vertical_back(adjoint + forcings[step], mixing)
        adjoint = horizontal_back(coupled, diffusion, wind_u, wind_v)
    gradient = increment + adjoint
    own_part = 0.5 * jnp.sum(increment * increment) + 0.5 * misfit_total / lax.axis_size("lev")
    total_cells = (
        increment.size * lax.axis_size("lat") * lax.axis_size("lon") * lax.axis_size("lev")
    )
    cost = lax.psum(own_part, ("lat", "lon", "lev")) / total_cells
    return (gradient, cost)


def solution(mesh):
    in_specs = (
        P("lev", "lat", "lon"),
        P("lev", "lat", "lon"),
        P("lev", "lat", "lon"),
        P("lev"),
        P("lev", None),
        P(None, "lev"),
        P(),
        P(None, "lat", "lon", None, None, None),
        P("lat", "lon"),
        P("lat", "lon", None),
    )
    out_specs = (P("lev", "lat", "lon"), P())
    return jax.shard_map(body, mesh=mesh, in_specs=in_specs, out_specs=out_specs, check_vma=False)
```

profile of v0, /device:TPU:0, one launch (start us, length us, event | category | flops | bytes accessed | tf_op | source)
XLA Modules:
  0.0 243.4 jit_solution(5966563828042760349)
XLA Ops:
  8.4 4.0 %collective-permute-start.1 = (f32[1,40,1,128]{3,1,2,0:T(8,128)S(1)}, f32[1,40,1,128]{3,1,2,0:T(8,128)S(1)}, u32[]{:S(2)}, u32[]{:S(2)}) collective-permute-start(f32[1,40,1,128]{3,1,2,0:T(8,128)S(1)} %get-tuple-element.113), channel_id=1, source_target_pairs={{8,0},{16,8},{24,16},{0,24},{9,1},{17,9},{25,17},{1,25},{10,2},{18... | collective-permute-start | bytes 61448 | tf_op jit(solution)/shard_map/ppermute | solution.py:16
  15.4 5.7 %sort.17 = (s32[2048]{0:T(1024)}, s32[2048]{0:T(1024)S(1)}) sort(s32[2048]{0:T(1024)} %bitcast.238, s32[2048]{0:T(1024)S(1)} %iota.10), dimensions={0}, to_apply=%region_0.2 | sort | flops 22528 | bytes 32768 | tf_op jit(solution)/shard_map/jit(argsort)/sort | solution.py:126
  23.5 3.6 %collective-permute-start.3 = (f32[1,40,18,1]{1,3,2,0:T(1,128)}, f32[1,40,18,1]{1,3,2,0:T(1,128)S(1)}, u32[]{:S(2)}, u32[]{:S(2)}) collective-permute-start(f32[1,40,18,1]{1,3,2,0:T(1,128)} %get-tuple-element.105), channel_id=1, source_target_pairs={{2,0},{4,2},{6,4},{0,6},{3,1},{5,3},{7,5},{1,7},{10,8},{12,10},{14... | collective-permute-start | bytes 8648 | tf_op jit(solution)/shard_map/ppermute | solution.py:16
  29.9 2.9 %collective-permute-done.2 = f32[1,40,18,1]{1,3,2,0:T(1,128)S(1)} collective-permute-done((f32[1,40,18,1]{1,3,2,0:T(1,128)}, f32[1,40,18,1]{1,3,2,0:T(1,128)S(1)}, u32[]{:S(2)}, u32[]{:S(2)}) %collective-permute-start.2) | collective-permute-done | bytes 2912 | tf_op jit(solution)/shard_map/ppermute | solution.py:14
  43.2 3.0 %collective-permute-start.5 = (f32[1,40,1,128]{1,3,2,0:T(8,128)S(1)}, f32[1,40,1,128]{1,3,2,0:T(8,128)S(1)}, u32[]{:S(2)}, u32[]{:S(2)}) collective-permute-start(f32[1,40,1,128]{1,3,2,0:T(8,128)S(1)} %get-tuple-element.111), channel_id=1, source_target_pairs={{8,0},{16,8},{24,16},{0,24},{9,1},{17,9},{25,17},{1,25},{10,2},{18... | collective-permute-start | bytes 61448 | tf_op jit(solution)/shard_map/ppermute | solution.py:16
  55.2 7.7 %gather_fusion.2 = bf16[2048,40]{1,0:T(8,128)(2,1)} fusion(f32[40,2048]{0,1:T(8,128)S(1)} %bitcast.217, s32[2048]{0:T(1024)S(1)} %fusion.56), kind=kCustom, calls=%fused_computation.2.clone | custom fusion | bytes 335872 | tf_op jit(solution)/shard_map/jit(_take)/gather | solution.py:96
  74.6 8.9 %gather_fusion = bf16[2048,40]{1,0:T(8,128)(2,1)} fusion(bf16[40,2048]{0,1:T(8,128)(2,1)} %bitcast.230, s32[2048]{0:T(1024)S(1)} %fusion.56), kind=kCustom, calls=%fused_computation.clone | custom fusion | bytes 335872 | tf_op jit(solution)/shard_map/jit(_take)/gather | solution.py:96
  93.3 7.6 %gather_fusion.1 = f32[2048,40]{1,0:T(8,128)} fusion(f32[40,2048]{0,1:T(8,128)S(1)} %bitcast.223, s32[2048]{0:T(1024)S(1)} %fusion.57), kind=kCustom, calls=%fused_computation.1.clone | custom fusion | bytes 663552 | tf_op jit(solution)/shard_map/jit(_take)/gather | solution.py:106
  104.1 8.5 %reduce-scatter.3.cloned.1.call-done = f32[40,2048]{1,0:T(8,128)} async-done(((f32[80,2048]{1,0:T(8,128)}), f32[40,2048]{1,0:T(8,128)}) %reduce-scatter.3.cloned.1.call-update) | async-done | bytes 327696 | tf_op jit(solution)/shard_map/reduce_scatter | solution.py:79
  115.9 2.6 %collective-permute-start.9 = (f32[3,40,1,128]{1,3,2,0:T(8,128)}, f32[3,40,1,128]{1,3,2,0:T(8,128)}, u32[]{:S(2)}, u32[]{:S(2)}) collective-permute-start(f32[3,40,1,128]{1,3,2,0:T(8,128)} %get-tuple-element.101), channel_id=1, source_target_pairs={{8,0},{16,8},{24,16},{0,24},{9,1},{17,9},{25,17},{1,25},{10,2},{18... | collective-permute-start | bytes 184328 | tf_op jit(solution)/shard_map/ppermute | solution.py:16
  120.3 8.8 %gather_fusion.3 = f32[2048,40]{1,0:T(8,128)} fusion(f32[40,2048]{0,1:T(8,128)} %bitcast.222, s32[2048]{0:T(1024)S(1)} %fusion.57), kind=kCustom, calls=%fused_computation.3.clone | custom fusion | bytes 663552 | tf_op jit(solution)/shard_map/jit(_take)/gather | solution.py:106
  132.5 3.4 %collective-permute-start.11 = (f32[3,40,18,1]{1,3,2,0:T(1,128)S(1)}, f32[3,40,18,1]{1,3,2,0:T(1,128)S(1)}, u32[]{:S(2)}, u32[]{:S(2)}) collective-permute-start(f32[3,40,18,1]{1,3,2,0:T(1,128)S(1)} %get-tuple-element.97), channel_id=1, source_target_pairs={{2,0},{4,2},{6,4},{0,6},{3,1},{5,3},{7,5},{1,7},{10,8},{12,10},{14... | collective-permute-start | bytes 25928 | tf_op jit(solution)/shard_map/ppermute | solution.py:16
  137.5 4.1 %collective-permute-done.10 = f32[3,40,18,1]{1,3,2,0:T(1,128)S(1)} collective-permute-done((f32[3,40,18,1]{1,3,2,0:T(1,128)S(1)}, f32[3,40,18,1]{1,3,2,0:T(1,128)S(1)}, u32[]{:S(2)}, u32[]{:S(2)}) %collective-permute-start.10) | collective-permute-done | bytes 8672 | tf_op jit(solution)/shard_map/ppermute | solution.py:14
  141.6 2.8 %maximum_multiply_fusion = f32[3,40,18,130]{1,3,2,0:T(8,128)S(1)} fusion(f32[3,40,18,1]{1,3,2,0:T(1,128)S(1)} %collective-permute-done.11, f32[3,40,1,128]{1,3,2,0:T(8,128)} %collective-permute-done.9, f32[1,40,16,128]{1,3,2,0:T(8,128)S(1)} %copy-done.5, f32[1,40,16,128]{1,3,2,0:T(8,128)S(1)} %copy-done.3, f32[1,40,16,128]{1,3,2,0:T(8,128)S(1)} %bitcast.212, ...), kind=kLoop, calls=%fused_computation.4 | loop fusion | flops 1965600 | bytes 2246472 | tf_op jit(solution)/shard_map/mul | solution.py:35
  153.1 2.9 %convolution_bitcast_fusion = f32[80,2048]{1,0:T(8,128)} fusion(f32[40,80]{1,0:T(8,128)S(1)} %copy-done, f32[40,2048]{1,0:T(8,128)S(1)} %select_bitcast_fusion, f32[40,2048]{1,0:T(8,128)} %copy.275, f32[40,2048]{1,0:T(8,128)} %copy.274, f32[40,2048]{1,0:T(8,128)} %copy-done.21, f32[40,2048]{1,0:T(8,128)} %copy.273, f32[40]{0:T(128)S(1)} %copy-done.29), kind=kOutput, calls=%fused_computation.6 | convolution fusion | flops 79216640 | bytes 2306720 | tf_op jit(solution)/shard_map/dot_general | solution.py:80
  157.4 5.6 %reduce-scatter.5.cloned.1.call-done = f32[40,2048]{1,0:T(8,128)} async-done(((f32[80,2048]{1,0:T(8,128)}), f32[40,2048]{1,0:T(8,128)}) %reduce-scatter.5.cloned.1.call-update) | async-done | bytes 327696 | tf_op jit(solution)/shard_map/reduce_scatter | solution.py:79
  162.9 2.3 copy.276
  165.3 3.4 %multiply_bitcast_fusion.1 = (f32[1,40,16,128]{1,3,2,0:T(8,128)S(1)}, f32[40,16,128]{0,2,1:T(8,128)S(1)}) fusion(f32[40,16,128]{0,2,1:T(8,128)S(1)} %copy.228, f32[40,16,128]{0,2,1:T(8,128)} %bitcast.228, f32[40,16,128]{0,2,1:T(8,128)} %bitcast.226, f32[1,40,16,128]{1,3,2,0:T(8,128)} %get-tuple-element.93, f32[1,40,16,128]{1,3,2,0:T(8,128)} %get-tuple-element.92, ...), kind=kLoop, calls=%fused_computation.77 | loop fusion | flops 819200 | bytes 2949280 | tf_op jit(solution)/shard_map/stack | solution.py:57
  172.0 2.6 %collective-permute-start.13 = (f32[3,40,1,128]{1,3,2,0:T(8,128)S(1)}, f32[3,40,1,128]{1,3,2,0:T(8,128)S(1)}, u32[]{:S(2)}, u32[]{:S(2)}) collective-permute-start(f32[3,40,1,128]{1,3,2,0:T(8,128)S(1)} %get-tuple-element.99), channel_id=1, source_target_pairs={{8,0},{16,8},{24,16},{0,24},{9,1},{17,9},{25,17},{1,25},{10,2},{18... | collective-permute-start | bytes 184328 | tf_op jit(solution)/shard_map/ppermute | solution.py:16
  174.7 5.3 %collective-permute-done.13 = f32[3,40,1,128]{1,3,2,0:T(8,128)S(1)} collective-permute-done((f32[3,40,1,128]{1,3,2,0:T(8,128)S(1)}, f32[3,40,1,128]{1,3,2,0:T(8,128)S(1)}, u32[]{:S(2)}, u32[]{:S(2)}) %collective-permute-start.13) | collective-permute-done | bytes 61472 | tf_op jit(solution)/shard_map/ppermute | solution.py:16
  180.0 4.6 %collective-permute-done.12 = f32[3,40,1,128]{1,3,2,0:T(8,128)S(1)} collective-permute-done((f32[3,40,1,128]{1,3,2,0:T(8,128)S(1)}, f32[3,40,1,128]{1,3,2,0:T(8,128)S(1)}, u32[]{:S(2)}, u32[]{:S(2)}) %collective-permute-start.12) | collective-permute-done | bytes 61472 | tf_op jit(solution)/shard_map/ppermute | solution.py:14
  184.6 3.4 %collective-permute-start.15 = (f32[3,40,18,1]{1,3,2,0:T(1,128)S(1)}, f32[3,40,18,1]{1,3,2,0:T(1,128)S(1)}, u32[]{:S(2)}, u32[]{:S(2)}) collective-permute-start(f32[3,40,18,1]{1,3,2,0:T(1,128)S(1)} %get-tuple-element.95), channel_id=1, source_target_pairs={{2,0},{4,2},{6,4},{0,6},{3,1},{5,3},{7,5},{1,7},{10,8},{12,10},{14... | collective-permute-start | bytes 25928 | tf_op jit(solution)/shard_map/ppermute | solution.py:16
  190.7 39.1 %psum.7 = f32[]{:T(128)} all-reduce(f32[]{:T(128)S(6)} %add.223), channel_id=1, replica_groups=mesh['lat'=4,'lon'=4,'lev'=2] {'lat','lon','lev'}, use_global_device_ids=true, to_apply=%region_6.8 | all-reduce | flops 1 | bytes 8 | tf_op jit(solution)/shard_map/psum | solution.py:157
  230.5 3.0 %maximum_multiply_fusion.1 = f32[3,40,18,130]{1,3,2,0:T(8,128)S(1)} fusion(f32[3,40,18,1]{1,3,2,0:T(1,128)S(1)} %collective-permute-done.15, f32[3,40,1,128]{1,3,2,0:T(8,128)S(1)} %collective-permute-done.13, f32[1,40,16,128]{1,3,2,0:T(8,128)S(1)} %multiply_bitcast_fusion, f32[1,40,16,128]{1,3,2,0:T(8,128)} %copy-done.1, ...), kind=kLoop, calls=%fused_computation.5 | loop fusion | flops 1965600 | bytes 2246472 | tf_op jit(solution)/shard_map/mul | solution.py:35
  (157 shorter events, 78.7 us)
Async XLA Ops:
  7.2 32.5 %copy-start = (f32[40,80]{1,0:T(8,128)S(1)}, f32[40,80]{1,0:T(8,128)}, u32[]{:S(2)}) copy-start(f32[40,80]{1,0:T(8,128)} %param.32) | copy-start | bytes 38404
  7.2 19.9 %copy-start.19 = (f32[40,16,128]{2,1,0:T(8,128)S(1)}, f32[40,16,128]{2,1,0:T(8,128)}, u32[]{:S(2)}) copy-start(f32[40,16,128]{2,1,0:T(8,128)} %param.28) | copy-start | bytes 983044
  7.2 20.3 %copy-start.27 = (f32[40,16,128]{2,1,0:T(8,128)S(1)}, f32[40,16,128]{2,1,0:T(8,128)}, u32[]{:S(2)}) copy-start(f32[40,16,128]{2,1,0:T(8,128)} %param.29) | copy-start | bytes 983044
  7.2 105.3 %reduce-scatter.3.cloned.1.call-start = ((), (), s32[]{:S(2)}) async-start(), calls=%async_computation.2 | async-start | bytes 983040 | tf_op jit(solution)/shard_map/reduce_scatter | solution.py:79
  8.4 14.0 %collective-permute-start.1 = (f32[1,40,1,128]{3,1,2,0:T(8,128)S(1)}, f32[1,40,1,128]{3,1,2,0:T(8,128)S(1)}, u32[]{:S(2)}, u32[]{:S(2)}) collective-permute-start(f32[1,40,1,128]{3,1,2,0:T(8,128)S(1)} %get-tuple-element.113), channel_id=1, source_target_pairs={{8,0},{16,8},{24,16},{0,24},{9,1},{17,9},{25,17},{1,25},{10,2},{18... | collective-permute-start | bytes 61448 | tf_op jit(solution)/shard_map/ppermute | solution.py:16
  12.4 10.0 %collective-permute-start = (f32[1,40,1,128]{3,1,2,0:T(8,128)S(1)}, f32[1,40,1,128]{3,1,2,0:T(8,128)S(1)}, u32[]{:S(2)}, u32[]{:S(2)}) collective-permute-start(f32[1,40,1,128]{3,1,2,0:T(8,128)S(1)} %get-tuple-element.112), channel_id=1, source_target_pairs={{0,8},{8,16},{16,24},{24,0},{1,9},{9,17},{17,25},{25,1},{2,10},{10... | collective-permute-start | bytes 61448 | tf_op jit(solution)/shard_map/ppermute | solution.py:14
  23.5 6.4 %collective-permute-start.3 = (f32[1,40,18,1]{1,3,2,0:T(1,128)}, f32[1,40,18,1]{1,3,2,0:T(1,128)S(1)}, u32[]{:S(2)}, u32[]{:S(2)}) collective-permute-start(f32[1,40,18,1]{1,3,2,0:T(1,128)} %get-tuple-element.105), channel_id=1, source_target_pairs={{2,0},{4,2},{6,4},{0,6},{3,1},{5,3},{7,5},{1,7},{10,8},{12,10},{14... | collective-permute-start | bytes 8648 | tf_op jit(solution)/shard_map/ppermute | solution.py:16
  27.1 5.7 %collective-permute-start.2 = (f32[1,40,18,1]{1,3,2,0:T(1,128)}, f32[1,40,18,1]{1,3,2,0:T(1,128)S(1)}, u32[]{:S(2)}, u32[]{:S(2)}) collective-permute-start(f32[1,40,18,1]{1,3,2,0:T(1,128)} %get-tuple-element.104), channel_id=1, source_target_pairs={{0,2},{2,4},{4,6},{6,0},{1,3},{3,5},{5,7},{7,1},{8,10},{10,12},{12... | collective-permute-start | bytes 8648 | tf_op jit(solution)/shard_map/ppermute | solution.py:14
  43.2 7.6 %collective-permute-start.5 = (f32[1,40,1,128]{1,3,2,0:T(8,128)S(1)}, f32[1,40,1,128]{1,3,2,0:T(8,128)S(1)}, u32[]{:S(2)}, u32[]{:S(2)}) collective-permute-start(f32[1,40,1,128]{1,3,2,0:T(8,128)S(1)} %get-tuple-element.111), channel_id=1, source_target_pairs={{8,0},{16,8},{24,16},{0,24},{9,1},{17,9},{25,17},{1,25},{10,2},{18... | collective-permute-start | bytes 61448 | tf_op jit(solution)/shard_map/ppermute | solution.py:16
  46.1 5.2 %collective-permute-start.4 = (f32[1,40,1,128]{1,3,2,0:T(8,128)S(1)}, f32[1,40,1,128]{1,3,2,0:T(8,128)S(1)}, u32[]{:S(2)}, u32[]{:S(2)}) collective-permute-start(f32[1,40,1,128]{1,3,2,0:T(8,128)S(1)} %get-tuple-element.110), channel_id=1, source_target_pairs={{0,8},{8,16},{16,24},{24,0},{1,9},{9,17},{17,25},{25,1},{2,10},{10... | collective-permute-start | bytes 61448 | tf_op jit(solution)/shard_map/ppermute | solution.py:14
  51.3 13.5 %collective-permute-start.7 = (f32[1,40,18,1]{1,3,2,0:T(1,128)S(1)}, f32[1,40,18,1]{1,3,2,0:T(1,128)S(1)}, u32[]{:S(2)}, u32[]{:S(2)}) collective-permute-start(f32[1,40,18,1]{1,3,2,0:T(1,128)S(1)} %get-tuple-element.103), channel_id=1, source_target_pairs={{2,0},{4,2},{6,4},{0,6},{3,1},{5,3},{7,5},{1,7},{10,8},{12,10},{14... | collective-permute-start | bytes 8648 | tf_op jit(solution)/shard_map/ppermute | solution.py:16
  52.3 12.5 %collective-permute-start.6 = (f32[1,40,18,1]{1,3,2,0:T(1,128)S(1)}, f32[1,40,18,1]{1,3,2,0:T(1,128)S(1)}, u32[]{:S(2)}, u32[]{:S(2)}) collective-permute-start(f32[1,40,18,1]{1,3,2,0:T(1,128)S(1)} %get-tuple-element.102), channel_id=1, source_target_pairs={{0,2},{2,4},{4,6},{6,0},{1,3},{3,5},{5,7},{7,1},{8,10},{10,12},{12... | collective-permute-start | bytes 8648 | tf_op jit(solution)/shard_map/ppermute | solution.py:14
  74.6 16.0 %copy-start.22 = (bf16[1,1,1,16,128,128]{4,5,3,2,1,0:T(8,128)(2,1)S(1)}, bf16[1,1,1,16,128,128]{4,5,3,2,1,0:T(8,128)(2,1)}, u32[]{:S(2)}) copy-start(bf16[1,1,1,16,128,128]{4,5,3,2,1,0:T(8,128)(2,1)} %copy.283) | copy-start | bytes 1572868
  104.0 58.9 %reduce-scatter.5.cloned.1.call-start = ((), (), s32[]{:S(2)}) async-start(), calls=%async_computation.3 | async-start | bytes 983040 | tf_op jit(solution)/shard_map/reduce_scatter | solution.py:79
  115.9 15.4 %collective-permute-start.9 = (f32[3,40,1,128]{1,3,2,0:T(8,128)}, f32[3,40,1,128]{1,3,2,0:T(8,128)}, u32[]{:S(2)}, u32[]{:S(2)}) collective-permute-start(f32[3,40,1,128]{1,3,2,0:T(8,128)} %get-tuple-element.101), channel_id=1, source_target_pairs={{8,0},{16,8},{24,16},{0,24},{9,1},{17,9},{25,17},{1,25},{10,2},{18... | collective-permute-start | bytes 184328 | tf_op jit(solution)/shard_map/ppermute | solution.py:16
  118.5 12.8 %collective-permute-start.8 = (f32[3,40,1,128]{1,3,2,0:T(8,128)}, f32[3,40,1,128]{1,3,2,0:T(8,128)}, u32[]{:S(2)}, u32[]{:S(2)}) collective-permute-start(f32[3,40,1,128]{1,3,2,0:T(8,128)} %get-tuple-element.100), channel_id=1, source_target_pairs={{0,8},{8,16},{16,24},{24,0},{1,9},{9,17},{17,25},{25,1},{2,10},{10... | collective-permute-start | bytes 184328 | tf_op jit(solution)/shard_map/ppermute | solution.py:14
  132.5 4.9 %collective-permute-start.11 = (f32[3,40,18,1]{1,3,2,0:T(1,128)S(1)}, f32[3,40,18,1]{1,3,2,0:T(1,128)S(1)}, u32[]{:S(2)}, u32[]{:S(2)}) collective-permute-start(f32[3,40,18,1]{1,3,2,0:T(1,128)S(1)} %get-tuple-element.97), channel_id=1, source_target_pairs={{2,0},{4,2},{6,4},{0,6},{3,1},{5,3},{7,5},{1,7},{10,8},{12,10},{14... | collective-permute-start | bytes 25928 | tf_op jit(solution)/shard_map/ppermute | solution.py:16
  135.9 5.7 %collective-permute-start.10 = (f32[3,40,18,1]{1,3,2,0:T(1,128)S(1)}, f32[3,40,18,1]{1,3,2,0:T(1,128)S(1)}, u32[]{:S(2)}, u32[]{:S(2)}) collective-permute-start(f32[3,40,18,1]{1,3,2,0:T(1,128)S(1)} %get-tuple-element.96), channel_id=1, source_target_pairs={{0,2},{2,4},{4,6},{6,0},{1,3},{3,5},{5,7},{7,1},{8,10},{10,12},{12... | collective-permute-start | bytes 25928 | tf_op jit(solution)/shard_map/ppermute | solution.py:14
  172.0 16.0 %copy-start.20 = (f32[40,16,128]{2,1,0:T(8,128)S(1)}, f32[40,16,128]{2,1,0:T(8,128)}, u32[]{:S(2)}) copy-start(f32[40,16,128]{2,1,0:T(8,128)} %param.28) | copy-start | bytes 983044
  172.0 7.9 %collective-permute-start.13 = (f32[3,40,1,128]{1,3,2,0:T(8,128)S(1)}, f32[3,40,1,128]{1,3,2,0:T(8,128)S(1)}, u32[]{:S(2)}, u32[]{:S(2)}) collective-permute-start(f32[3,40,1,128]{1,3,2,0:T(8,128)S(1)} %get-tuple-element.99), channel_id=1, source_target_pairs={{8,0},{16,8},{24,16},{0,24},{9,1},{17,9},{25,17},{1,25},{10,2},{18... | collective-permute-start | bytes 184328 | tf_op jit(solution)/shard_map/ppermute | solution.py:16
  174.7 9.9 %collective-permute-start.12 = (f32[3,40,1,128]{1,3,2,0:T(8,128)S(1)}, f32[3,40,1,128]{1,3,2,0:T(8,128)S(1)}, u32[]{:S(2)}, u32[]{:S(2)}) collective-permute-start(f32[3,40,1,128]{1,3,2,0:T(8,128)S(1)} %get-tuple-element.98), channel_id=1, source_target_pairs={{0,8},{8,16},{16,24},{24,0},{1,9},{9,17},{17,25},{25,1},{2,10},{10... | collective-permute-start | bytes 184328 | tf_op jit(solution)/shard_map/ppermute | solution.py:14
  184.6 45.8 %collective-permute-start.15 = (f32[3,40,18,1]{1,3,2,0:T(1,128)S(1)}, f32[3,40,18,1]{1,3,2,0:T(1,128)S(1)}, u32[]{:S(2)}, u32[]{:S(2)}) collective-permute-start(f32[3,40,18,1]{1,3,2,0:T(1,128)S(1)} %get-tuple-element.95), channel_id=1, source_target_pairs={{2,0},{4,2},{6,4},{0,6},{3,1},{5,3},{7,5},{1,7},{10,8},{12,10},{14... | collective-permute-start | bytes 25928 | tf_op jit(solution)/shard_map/ppermute | solution.py:16
  188.0 42.5 %collective-permute-start.14 = (f32[3,40,18,1]{1,3,2,0:T(1,128)S(1)}, f32[3,40,18,1]{1,3,2,0:T(1,128)S(1)}, u32[]{:S(2)}, u32[]{:S(2)}) collective-permute-start(f32[3,40,18,1]{1,3,2,0:T(1,128)S(1)} %get-tuple-element.94), channel_id=1, source_target_pairs={{0,2},{2,4},{4,6},{6,0},{1,3},{3,5},{5,7},{7,1},{8,10},{10,12},{12... | collective-permute-start | bytes 25928 | tf_op jit(solution)/shard_map/ppermute | solution.py:14
  188.7 44.8 %copy-start.10 = (f32[40,16,128]{0,2,1:T(8,128)S(1)}, f32[40,16,128]{0,2,1:T(8,128)}, u32[]{:S(2)}) copy-start(f32[40,16,128]{0,2,1:T(8,128)} %copy-done.9) | copy-start | bytes 983044
  (25 other events, 155.5 us)
Sparse Core Ops, SparseCore 0:
  104.1 8.3 reduce-scatter.2
  156.2 6.7 reduce-scatter.4
where the time goes:
time: 245 us; the launch traced here: 243 us
  local copies, waits for them, and re-layouts  73.3 us (30%)
  blocking collectives  49.6 us (20%)
  other arithmetic  34.7 us (14%)
  waiting for transfers between devices  33.1 us (14%)
  starting transfers between devices  24.7 us (10%)
  between operations  19 us (8%)
  matrix products  9.19 us (4%)
    psum x1, blocking collectives, body(): cost = lax.psum(own_part, ('lat', 'lon', 'lev')) / total_cells  39.1 us
    ppermute x8, starting transfers between devices, padded_2(): lax.ppermute(head, axis, [((i + 1) % count, i) for i in range(count)])  23.5 us
    gather x4, local copies, waits for them, and re-layouts, place_back(): return jnp.take(dispersed_blocks, inverse, axis=1).reshape(shape)  20.1 us
    gather x4, local copies, waits for them, and re-layouts, take_profiles(): selected_columns = jnp.take(state.reshape(level_count, -1), columns, axis=1)  19.6 us
    reduce_scatter x2, waiting for transfers between devices, vertical_back(): lax.psum_scatter(lax.dot_general(mixing, flat, (((0,), (0,)), ((), ())),...  14.1 us
    ppermute x8, waiting for transfers between devices, padded_2(): lax.ppermute(tail, axis, [(i, (i + 1) % count) for i in range(count)])  12.2 us
    unnamed x69, local copies, waits for them, and re-layouts  11.8 us
    mul x4, other arithmetic, neighbours(): padded = padded * rim_mask[None, None, :, None]  7.49 us
  transfers between devices with their start and end apart: 18, of which 8 were waited for; matrix products, arithmetic and copies ran while one was open for 17% of the time, Pallas kernels for 0%

commit v1 on v0

v1 whole, which is shorter than its diff:
```python
import functools

import jax
import jax.numpy as jnp
from jax import lax
from jax.experimental import pallas as pl
from jax.experimental.pallas import tpu as pltpu
from jax.sharding import PartitionSpec as P

B = 128
HALO = 2
GROUP = 4


def roll(x, shift):
    shift %= B
    return x if shift == 0 else pltpu.roll(x, shift, 1)


def lanes_of(level_count):
    return lax.broadcasted_iota(jnp.int32, (level_count, B), 1)


def block(ref, p):
    return ref[:, p * B : (p + 1) * B]


def pack_edges(fields, rows):
    packed = None
    for f, field in enumerate(fields):
        for q in range(rows):
            rolled = roll(field(q + 1), (f * rows + q) * GROUP + 2)
            if packed is None:
                lane = lanes_of(rolled.shape[0])
                packed = jnp.zeros_like(rolled)
            packed = jnp.where(lane // GROUP == f * rows + q, rolled, packed)
    return packed


def side_block(west, own, east, f, rows):
    lane = lanes_of(own.shape[0])
    first = lane % GROUP < 2
    low, high = -f * rows * GROUP, B // 2 - f * rows * GROUP
    western = jnp.where(first, roll(west, low), roll(own, low))
    eastern = jnp.where(first, roll(own, high), roll(east, high))
    return jnp.where(lane < B // 2, western, eastern)


def from_east(x, side, q):
    lane = lanes_of(x.shape[0])
    return jnp.where(lane == B - 1, roll(side, B - 1 - (B // 2 + q * GROUP + 2)), roll(x, -1))


def from_west(x, side, q):
    lane = lanes_of(x.shape[0])
    return jnp.where(lane == 0, roll(side, -(q * GROUP + 1)), roll(x, 1))


def put_split(stack, p, x):
    levels = x.shape[0]
    head = x.astype(jnp.bfloat16)
    stack[0:levels, p * B : (p + 1) * B] = head
    stack[levels : 2 * levels, p * B : (p + 1) * B] = head
    stack[2 * levels : 3 * levels, p * B : (p + 1) * B] = (x - head.astype(jnp.float32)).astype(jnp.bfloat16)


def clear_rest(stack, levels):
    if stack.shape[0] > 3 * levels:
        stack[3 * levels :, :] = jnp.zeros((stack.shape[0] - 3 * levels, stack.shape[1]), stack.dtype)


def split_matrix(matrix, levels):
    lane = lanes_of(levels)
    matrix = jnp.where(lane < levels, matrix, 0.0)
    head = matrix.astype(jnp.bfloat16).astype(jnp.float32)
    rest = matrix - head
    over = B - levels
    low = jnp.where(lane < levels, head, roll(rest, levels))
    high = jnp.where(lane < levels - over, roll(rest, -over), roll(head, levels - over))
    high = jnp.where(lane < 2 * levels - over, high, 0.0)
    return jnp.concatenate([low, high], axis=1).astype(jnp.bfloat16)


def arrange(rows, place, inc, u, v, inc2, u2, v2, own_par, other_par, main_i, main_u, main_v, inner, edge, par):
    core = place[0]
    levels, half = own_par.shape[0], rows // 2
    own = pl.multiple_of(core * levels, 8)
    other = pl.multiple_of((1 - core) * levels, 8)
    par[pl.ds(own, levels), :] = own_par[...]
    par[pl.ds(other, levels), :] = other_par[...]
    for f, (a, b, main) in enumerate(((inc, inc2, main_i), (u, u2, main_u), (v, v2, main_v))):
        for src, dst in ((a, own), (b, other)):
            for j in range(half):
                main[pl.ds(dst, levels), j * B : (j + 1) * B] = src[pl.ds(core * half + j, levels, stride=rows), :]
            for j in range(HALO):
                k = f * HALO + j
                inner[pl.ds(dst, levels), k * B : (k + 1) * B] = src[
                    pl.ds(half - core * HALO + j, levels, stride=rows), :
                ]
                edge[pl.ds(dst, levels), k * B : (k + 1) * B] = src[
                    pl.ds(core * (rows - HALO) + j, levels, stride=rows), :
                ]


def by_column(place, lookup, observed, out, live, hot, stacked):
    core, count = place[0], place[3]
    steps, slots, channels, width = observed.shape
    columns = hot.shape[0]
    index = lax.broadcasted_iota(jnp.int32, (columns, width), 0)
    for s in range(slots):
        target = jnp.where(s < count, lookup[s : s + 1, :] - core * columns, -1)
        hot[:, s * width : (s + 1) * width] = jnp.where(index == target, 1.0, 0.0).astype(jnp.bfloat16)
        for t in range(steps):
            stacked[t * channels : (t + 1) * channels, s * width : (s + 1) * width] = observed[t, s]
    tail = stacked.shape[0] - steps * channels
    stacked[steps * channels :, :] = jnp.ones((tail, slots * width), jnp.bfloat16)
    moved = lax.dot_general(
        stacked[...], hot[...], (((1,), (1,)), ((), ())), preferred_element_type=jnp.float32
    )
    out[...] = moved[: steps * channels].astype(jnp.bfloat16)
    live[...] = moved[steps * channels : steps * channels + 8]


def windows(place, main_i, main_u, main_v, inner, edge, win_i, win_u, win_v, packed):
    low = place[0] == 0
    count = win_i.shape[1] // B
    for f, (main, win) in enumerate(((main_i, win_i), (main_u, win_u), (main_v, win_v))):
        win[:, HALO * B : (count - HALO) * B] = main[...]
        span = slice(f * HALO * B, (f + 1) * HALO * B)
        near, far = inner[:, span], edge[:, span]
        win[:, : HALO * B] = jnp.where(low, far, near)
        win[:, (count - HALO) * B :] = jnp.where(low, near, far)
    packed[...] = pack_edges([functools.partial(block, win) for win in (win_i, win_u, win_v)], count - 2)


def smooth(x, north, south, east, west, diff, u, v):
    return (
        x
        + diff * ((north + south) + (east + west) - 4.0 * x)
        - 0.5 * u * (east - west)
        - 0.5 * v * (north - south)
    )


def forward(
    place, win_i, win_u, win_v, west, own, east, par, weight, observed, live,
    f1, f2, edge, inner, cost, stack, plain, state,
):
    levels = par.shape[0]
    count = win_i.shape[1] // B
    rows = count - 2
    half = rows - 2
    diff = par[:, levels : levels + 1]
    coupling = split_matrix(par[:, :B], levels)
    radiance = par[:, B:].astype(jnp.bfloat16)
    channels = radiance.shape[1]
    diagonal = lax.broadcasted_iota(jnp.int32, (channels, channels), 0) == lax.broadcasted_iota(
        jnp.int32, (channels, channels), 1
    )
    weights = jnp.sum(jnp.where(diagonal, weight[...], 0.0), axis=1, keepdims=True)
    clear_rest(stack, levels)
    sides = [side_block(west[...], own[...], east[...], f, rows) for f in range(3)]
    for q in range(rows):
        p = q + 1
        x = block(win_i, p)
        s = smooth(
            x, block(win_i, p + 1), block(win_i, p - 1), from_east(x, sides[0], q), from_west(x, sides[0], q),
            diff, block(win_u, p), block(win_v, p),
        )
        plain[:, q * B : (q + 1) * B] = s
        put_split(stack, q, s)
    x = sides[0]
    s = smooth(x, roll(x, -GROUP), roll(x, GROUP), roll(x, -1), roll(x, 1), diff, sides[1], sides[2])
    plain[:, rows * B :] = s
    put_split(stack, rows, s)
    state[...] = plain[...] + jnp.dot(coupling, stack[...], preferred_element_type=jnp.float32)
    first, final = (rows - 1) * B, rows * B
    state[:, :B] = jnp.where(place[1] == 1, state[:, :B], 0.0)
    state[:, first:final] = jnp.where(place[2] == 1, state[:, first:final], 0.0)

    def observe(profile, t, out):
        evolved = lax.dot_general(
            radiance, profile, (((0,), (0,)), ((), ())), preferred_element_type=jnp.float32
        )
        departure = evolved - observed[t * channels : (t + 1) * channels, :].astype(jnp.float32)
        misfit = live[0:1, :] * departure
        scaled = weights * misfit
        back = jnp.dot(radiance, scaled.astype(jnp.bfloat16), preferred_element_type=jnp.float32)
        out[...] = back.astype(jnp.bfloat16)
        return jnp.sum(misfit * scaled, keepdims=True)

    total = observe(state[:, B : (half + 1) * B].astype(jnp.bfloat16), 0, f1)
    side = state[:, rows * B :]
    for q in range(1, rows - 1):
        x = block(state, q)
        s = smooth(
            x, block(state, q + 1), block(state, q - 1), from_east(x, side, q), from_west(x, side, q),
            diff, block(win_u, q + 1), block(win_v, q + 1),
        )
        plain[:, (q - 1) * B : q * B] = s
        put_split(stack, q - 1, s)
    end = plain[:, : half * B] + jnp.dot(coupling, stack[:, : half * B], preferred_element_type=jnp.float32)
    total = total + observe(end.astype(jnp.bfloat16), 1, f2)
    whole = win_i[:, HALO * B : (count - HALO) * B]
    total = 0.5 * (total + jnp.sum(whole * whole, keepdims=True))
    cost[...] = jnp.broadcast_to(total, cost.shape)
    low = place[0] == 0
    span = HALO * B
    for k, f in enumerate((f2, f1)):
        head, tail = f[:, :span].astype(jnp.float32), f[:, (half - HALO) * B :].astype(jnp.float32)
        edge[:, k * span : (k + 1) * span] = jnp.where(low, head, tail).astype(jnp.bfloat16)
        inner[:, k * span : (k + 1) * span] = jnp.where(low, tail, head).astype(jnp.bfloat16)


def forcing_windows(place, f1, f2, edge, inner, cost, other_cost, win_1, win_2, packed):
    low = place[0] == 0
    count = win_1.shape[1] // B
    span = HALO * B
    for k, (f, win) in enumerate(((f2, win_2), (f1, win_1))):
        win[:, span : (count - HALO) * B] = f[...].astype(jnp.float32)
        far = edge[:, k * span : (k + 1) * span].astype(jnp.float32)
        near = inner[:, k * span : (k + 1) * span].astype(jnp.float32)
        win[:, :span] = jnp.where(low, far, near)
        win[:, (count - HALO) * B :] = jnp.where(low, near, far)
    both = pack_edges([functools.partial(block, win) for win in (win_2, win_1)], count - 2)
    total = cost[0:1, :] + other_cost[0:1, :]
    packed[...] = jnp.where(lanes_of(both.shape[0]) == B - 1, total, both)


def backward(
    place, win_1, win_2, fwest, fown, feast, win_i, win_u, win_v, west, own, east, par,
    kept, sent, stack, coupled, square,
):
    levels = par.shape[0]
    count = win_i.shape[1] // B
    rows = count - 2
    half = rows - 2
    diff = par[:, levels : levels + 1]
    middle = 1.0 - 4.0 * diff
    square[...] = jnp.zeros(square.shape, jnp.float32)
    square[:levels, :] = jnp.where(lanes_of(levels) < levels, par[:, :B], 0.0)
    coupling = split_matrix(jnp.transpose(square[...])[:levels], levels)
    clear_rest(stack, levels)
    f_sides = [side_block(fwest[...], fown[...], feast[...], f, rows) for f in range(2)]
    sides = [side_block(west[...], own[...], east[...], f, rows) for f in range(3)]
    for p in range(count):
        x = block(win_2, p)
        coupled[:, p * B : (p + 1) * B] = x
        put_split(stack, p, x)
    coupled[:, count * B :] = f_sides[0]
    put_split(stack, count, f_sides[0])
    coupled[...] = coupled[...] + jnp.dot(coupling, stack[...], preferred_element_type=jnp.float32)

    def spread(p, q, side):
        x = block(coupled, p)
        north = (diff + 0.5 * block(win_v, q + 2)) * block(coupled, p + 1)
        south = (diff - 0.5 * block(win_v, q)) * block(coupled, p - 1)
        u = 0.5 * block(win_u, q + 1)
        side_east = (diff + 0.5 * sides[1]) * side
        side_west = (diff - 0.5 * sides[1]) * side
        return (
            middle * x + north + south + from_east((diff + u) * x, side_east, q)
            + from_west((diff - u) * x, side_west, q)
        )

    side = coupled[:, count * B :]
    after = []
    side_v, side_u = 0.5 * sides[2], 0.5 * sides[1]
    result = (
        middle * side
        + roll((diff + side_v) * side, -GROUP)
        + roll((diff - side_v) * side, GROUP)
        + roll((diff + side_u) * side, -1)
        + roll((diff - side_u) * side, 1)
        + f_sides[1]
    )
    for q in range(rows):
        after.append(spread(q + 1, q, side) + block(win_1, q + 1))
    after[0] = jnp.where(place[1] == 1, after[0], 0.0)
    after[-1] = jnp.where(place[2] == 1, after[-1], 0.0)
    for q in range(rows):
        coupled[:, (q + 1) * B : (q + 2) * B] = after[q]
        put_split(stack, q, after[q])
    coupled[:, count * B :] = result
    put_split(stack, rows, result)
    mixed = jnp.dot(coupling, stack[:, : (rows + 1) * B], preferred_element_type=jnp.float32)
    coupled[:, B : (rows + 1) * B] = coupled[:, B : (rows + 1) * B] + mixed[:, : rows * B]
    side = coupled[:, count * B :] + mixed[:, rows * B :]
    low = place[0] == 0
    part = levels // 2
    for j in range(half):
        value = block(win_i, j + HALO) + spread(j + HALO, j + 1, side)
        kept[pl.ds(j, part, stride=half), :] = jnp.where(low, value[:part], value[part:])
        sent[pl.ds(j, part, stride=half), :] = jnp.where(low, value[part:], value[:part])


def call(kernel, outs, scratch=(), name=None):
    vmem = pl.BlockSpec(memory_space=pltpu.VMEM)

    def run(place, *operands):
        return pl.pallas_call(
            kernel,
            out_shape=[jax.ShapeDtypeStruct(shape, dtype) for shape, dtype in outs],
            in_specs=[pl.BlockSpec(memory_space=pltpu.SMEM)] + [vmem] * len(operands),
            out_specs=[vmem] * len(outs),
            scratch_shapes=[pltpu.VMEM(shape, dtype) for shape, dtype in scratch],
            name=name,
        )(place, *operands)

    return run


def ring(x, axis, shift):
    count = lax.axis_size(axis)
    return lax.ppermute(x, axis, [(i, (i + shift) % count) for i in range(count)])


def body(
    increment, wind_u, wind_v, diffusion, mixing, jacobian, obs_weight, innovation, counts, column_lookup
):
    part, rows, width = increment.shape
    levels = mixing.shape[1]
    steps, channels = innovation.shape[0], innovation.shape[-2]
    slots = innovation.shape[3]
    assert width == B and steps == HALO and levels == 2 * part
    half = rows // 2
    count = half + 2 * HALO
    columns = half * B
    f32, bf16 = jnp.float32, jnp.bfloat16
    core, lat = lax.axis_index("lev"), lax.axis_index("lat")
    tiles = lax.axis_size("lat")
    at_top = (core == 0) & (lat == 0)
    at_end = (core == 1) & (lat == tiles - 1)
    place = jnp.stack(
        [core.astype(jnp.int32), 1 - at_top.astype(jnp.int32), 1 - at_end.astype(jnp.int32), counts[0, 0]]
    )
    pairs = [(2 * i + 1, 2 * i + 2) for i in range(tiles - 1)]
    pairs = pairs + [(b, a) for a, b in pairs]

    def swap(x):
        return lax.ppermute(x, "lev", [(0, 1), (1, 0)])

    def across(x):
        return lax.ppermute(x, ("lat", "lev"), pairs)

    own_par = jnp.concatenate(
        [
            mixing,
            diffusion[:, None],
            jnp.zeros((part, B - levels - 1), f32),
            jacobian.T.astype(f32),
        ],
        axis=1,
    )
    fields = [x.reshape(part * rows, B) for x in (increment, wind_u, wind_v)]
    others = [swap(x) for x in fields]
    other_par = swap(own_par)
    main = ((levels, columns), f32)
    edges = ((levels, 3 * HALO * B), f32)
    win = ((levels, count * B), f32)
    packed = ((levels, B), f32)
    *mains, inner, edge, par = call(
        functools.partial(arrange, rows), [main] * 3 + [edges] * 2 + [((levels, 2 * B), f32)], name="arrange"
    )(place, *fields, *others, own_par, other_par)
    edge = across(edge)
    observed, live = call(
        by_column,
        [((steps * channels, columns), bf16), ((8, columns), f32)],
        [((columns, slots * B), bf16), ((steps * channels + 16, slots * B), bf16)],
        name="by_column",
    )(place, column_lookup.reshape(slots, B), innovation.reshape(steps, slots, channels, B))
    win_i, win_u, win_v, own = call(windows, [win] * 3 + [packed], name="windows")(place, *mains, inner, edge)
    west, east = ring(own, "lon", 1), ring(own, "lon", -1)
    forcing = ((levels, columns), bf16)
    f_edges = ((levels, 2 * HALO * B), bf16)
    depth = -(-3 * levels // 16) * 16
    depth = max(depth, 2 * B)
    f1, f2, f_edge, f_inner, cost = call(
        forward,
        [forcing] * 2 + [f_edges] * 2 + [((8, B), f32)],
        [((depth, (count - 1) * B), bf16), ((levels, (count - 1) * B), f32), ((levels, (count - 1) * B), f32)],
        name="forward",
    )(place, win_i, win_u, win_v, west, own, east, par, obs_weight.reshape(1, -1), observed, live)
    f_edge, f_inner = across(f_edge), swap(f_inner)
    cost_2 = ring(cost, "lat", 1)
    win_1, win_2, f_own = call(forcing_windows, [win] * 2 + [packed], name="forcing")(
        place, f1, f2, f_edge, f_inner, cost, cost_2
    )
    f_west, f_east = ring(f_own, "lon", 1), ring(f_own, "lon", -1)
    total = f_own[:8] + f_west[:8]
    shift = 2
    while shift < tiles:
        total = total + ring(total, "lat", shift)
        shift *= 2
    kept, sent = call(
        backward,
        [((part * half, B), f32)] * 2,
        [((depth, (count + 1) * B), bf16), ((levels, (count + 1) * B), f32), ((B, B), f32)],
        name="backward",
    )(place, win_1, win_2, f_west, f_own, f_east, win_i, win_u, win_v, west, own, east, par)
    got = swap(sent)
    shift = 2
    while shift < lax.axis_size("lon"):
        total = total + ring(total, "lon", shift)
        shift *= 2
    total = total + swap(total)
    kept, got = kept.reshape(part, half, B), got.reshape(part, half, B)
    gradient = jnp.where(
        core == 0, jnp.concatenate([kept, got], axis=1), jnp.concatenate([got, kept], axis=1)
    )
    cells = increment.size * tiles * lax.axis_size("lon") * lax.axis_size("lev")
    return gradient, total[0, B - 1] / cells


def solution(mesh):
    for axis in ("lat", "lon"):
        assert mesh.shape[axis] & (mesh.shape[axis] - 1) == 0 and mesh.shape[axis] > 1
    in_specs = (
        P("lev", "lat", "lon"),
        P("lev", "lat", "lon"),
        P("lev", "lat", "lon"),
        P("lev"),
        P("lev", None),
        P(None, "lev"),
        P(),
        P(None, "lat", "lon", None, None, None),
        P("lat", "lon"),
        P("lat", "lon", None),
    )
    out_specs = (P("lev", "lat", "lon"), P())
    return jax.shard_map(body, mesh=mesh, in_specs=in_specs, out_specs=out_specs, check_vma=False)
```

time: 245 us -> 76 us (0.31)
  local copies, waits for them, and re-layouts: 73.3 us -> 6.3 us
  blocking collectives: 49.6 us -> 0 us
  other arithmetic: 34.7 us -> 3.12 us
  Pallas kernels: 0 us -> 19.9 us
  waiting for transfers between devices: 33.1 us -> 16.4 us
  between operations: 19 us -> 3.2 us
  matrix products: 9.19 us -> 0 us
    gather x8 -> x0, local copies, waits for them, and re-layouts: 39.8 us -> none  [the longest x4 20.1 us: place_back(): return jnp.take(dispersed_blocks, inverse, axis=1).reshape(shape)]
    psum x1 -> x0, blocking collectives: 39.1 us -> none  [body(): cost = lax.psum(own_part, ('lat', 'lon', 'lev')) / total_cells]
    pallas_call x0 -> x6, Pallas kernels: none -> 19.9 us  [run(): pl.pallas_call(kernel, out_shape=[jax.ShapeDtypeStruct(shape, dtype) for...]
    reduce_scatter x2 -> x0, waiting for transfers between devices: 14.1 us -> none  [vertical_back(): lax.psum_scatter(lax.dot_general(mixing, flat, (((0,), (0,)), ((), ())),...]
    all_gather x5 -> x0, blocking collectives: 10.4 us -> none  [the longest x2 4.54 us: vertical(): lax.all_gather(flat, 'lev', axis=0, tiled=True)]
    reshape x6 -> x0, local copies, waits for them, and re-layouts: 9.45 us -> none  [the longest x2 3.15 us: vertical(): flat = smooth.reshape(smooth.shape[0], -1)]
    dot_general x8 -> x0, matrix products: 9.19 us -> none  [the longest x2 4.5 us: vertical_back(): lax.dot_general(mixing, flat, (((0,), (0,)), ((), ())), precision=lax.Pre...]
    add x6 -> x4, other arithmetic: 8.32 us -> 0.7 us  [the longest x1 0.69 us: body(): total = f_own[:8] + f_west[:8]]
  transfers between devices with their start and end apart: 18 -> 16, of which waited for: 8 -> 7; matrix products, arithmetic and copies ran while one was open for 17% -> 3% of each run, Pallas kernels for 0% -> 5%
where the time goes in v1:
time: 76 us; the launch traced here: 75.5 us
  starting transfers between devices  26.6 us (35%)
  Pallas kernels  19.9 us (26%)
  waiting for transfers between devices  16.4 us (22%)
  local copies, waits for them, and re-layouts  6.3 us (8%)
  between operations  3.2 us (4%)
  other arithmetic  3.12 us (4%)
    pallas_call x6, Pallas kernels, run(): pl.pallas_call(kernel, out_shape=[jax.ShapeDtypeStruct(shape, dtype) for...  19.9 us
    ppermute x7, waiting for transfers between devices, ring(): lax.ppermute(x, axis, [(i, (i + shift) % count) for i in range(count)])  15.2 us
    ppermute x7, starting transfers between devices, ring(): lax.ppermute(x, axis, [(i, (i + shift) % count) for i in range(count)])  12.7 us
    ppermute x7, starting transfers between devices, swap(): return lax.ppermute(x, 'lev', [(0, 1), (1, 0)])  12.6 us
    unnamed x34, local copies, waits for them, and re-layouts  5.55 us
    select_n x1, other arithmetic, body(): jnp.where(core == 0, jnp.concatenate([kept, got], axis=1), jnp.concatenat...  1.75 us
  transfers between devices with their start and end apart: 16, of which 7 were waited for; matrix products, arithmetic and copies ran while one was open for 3% of the time, Pallas kernels for 5%

profile of v1, /device:TPU:0, one launch (start us, length us, event | category | flops | bytes accessed | tf_op | source)
XLA Modules:
  0.0 75.5 jit_solution(5809093175992306737)
XLA Ops:
  6.0 0.7 copy-done.2
  6.7 3.2 %arrange.1 = (f32[80,1024]{1,0:T(8,128)}, f32[80,1024]{1,0:T(8,128)}, f32[80,1024]{1,0:T(8,128)}, f32[80,768]{1,0:T(8,128)}, f32[80,768]{1,0:T(8,128)}, /*index=5*/f32[80,256]{1,0:T(8,128)}) custom-call(s32[4]{0:T(128)} %pad_add_fusion.place, f32[640,128]{1,0:T(8,128)} %bitcast.19, f32[640,128]{1,0:T(8,128)} %bitcast.21, f32[640,128]{1,0:T(8,128)} %bitcast.23, ...), custom_call_target="tpu_custom_call" | custom-call | tf_op jit(solution)/shard_map/arrange/pallas_call | solution.py:301
  9.9 0.7 collective-permute-start.4
  10.6 0.7 copy-done.3
  11.3 2.6 %windows.1 = (f32[80,1536]{1,0:T(8,128)}, f32[80,1536]{1,0:T(8,128)}, f32[80,1536]{1,0:T(8,128)}, f32[80,128]{1,0:T(8,128)}) custom-call(s32[4]{0:T(128)} %pad_add_fusion.place, f32[80,1024]{1,0:T(8,128)} %get-tuple-element.24.main_i, f32[80,1024]{1,0:T(8,128)} %get-tuple-element.25.main_u, f32[80,1024]{1,0:T(8,128)} %get-tuple-element.26.main_v, ...), custom_call_target="tpu_custom_call" | custom-call | tf_op jit(solution)/shard_map/windows/pallas_call | solution.py:301
  13.9 4.7 %collective-permute-start.6 = (f32[80,128]{1,0:T(8,128)}, f32[80,128]{1,0:T(8,128)S(1)}, u32[]{:S(2)}, u32[]{:S(2)}) collective-permute-start(f32[80,128]{1,0:T(8,128)} %get-tuple-element.32.own), channel_id=1, source_target_pairs={{0,6},{2,0},{4,2},{6,4},{1,7},{3,1},{5,3},{7,5},{8,14},{10,8},{12,... | collective-permute-start | bytes 122888 | tf_op jit(solution)/shard_map/ppermute | solution.py:315
  18.6 3.7 %by_column.1 = (bf16[256,1024]{1,0:T(8,128)(2,1)}, f32[8,1024]{1,0:T(8,128)}) custom-call(s32[4]{0:T(128)} %pad_add_fusion.place, s32[16,128]{1,0:T(8,128)} %bitcast.26, bf16[2,16,128,128]{3,2,1,0:T(8,128)(2,1)} %bitcast.17), custom_call_target="tpu_custom_call" | custom-call | tf_op jit(solution)/shard_map/by_column/pallas_call | solution.py:301
  22.3 2.3 %collective-permute-done.5.west = f32[80,128]{1,0:T(8,128)S(1)} collective-permute-done((f32[80,128]{1,0:T(8,128)}, f32[80,128]{1,0:T(8,128)S(1)}, u32[]{:S(2)}, u32[]{:S(2)}) %collective-permute-start.5) | collective-permute-done | bytes 40992 | tf_op jit(solution)/shard_map/ppermute | solution.py:315
  25.2 4.1 %forward.1 = (bf16[80,1024]{1,0:T(8,128)(2,1)}, bf16[80,1024]{1,0:T(8,128)(2,1)}, bf16[80,512]{1,0:T(8,128)(2,1)}, bf16[80,512]{1,0:T(8,128)(2,1)}, f32[8,128]{1,0:T(8,128)}) custom-call(s32[4]{0:T(128)} %pad_add_fusion.place, f32[80,1536]{1,0:T(8,128)} %get-tuple-element.29.win_i, f32[80,1536]{1,0:T(8,128)} %get-tuple-element.30.win_u, ...), custom_call_target="tpu_custom_call" | custom-call | tf_op jit(solution)/shard_map/forward/pallas_call | solution.py:301
  29.4 0.7 collective-permute-start.7
  30.0 11.0 %collective-permute-start.8 = (bf16[80,512]{1,0:T(8,128)(2,1)}, bf16[80,512]{1,0:T(8,128)(2,1)S(1)}, u32[]{:S(2)}, u32[]{:S(2)}) collective-permute-start(bf16[80,512]{1,0:T(8,128)(2,1)} %get-tuple-element.39), channel_id=1, source_target_pairs={{0,1},{1,0},{2,3},{3,2},{4,5},{5,4},{6,7},{7,6},{8,9},{9,8},{10,11... | collective-permute-start | bytes 245768 | tf_op jit(solution)/shard_map/ppermute | solution.py:341
  41.0 3.6 %collective-permute-start.9 = (f32[8,128]{1,0:T(8,128)S(1)}, f32[8,128]{1,0:T(8,128)S(1)}, u32[]{:S(2)}, u32[]{:S(2)}) collective-permute-start(f32[8,128]{1,0:T(8,128)S(1)} %copy-done.14), channel_id=1, source_target_pairs={{0,8},{8,16},{16,24},{24,0},{1,9},{9,17},{17,25},{25,1},{2,10},{10... | collective-permute-start | bytes 12296 | tf_op jit(solution)/shard_map/ppermute | solution.py:315
  44.7 1.3 %collective-permute-done.9.other_cost = f32[8,128]{1,0:T(8,128)S(1)} collective-permute-done((f32[8,128]{1,0:T(8,128)S(1)}, f32[8,128]{1,0:T(8,128)S(1)}, u32[]{:S(2)}, u32[]{:S(2)}) %collective-permute-start.9) | collective-permute-done | bytes 4128 | tf_op jit(solution)/shard_map/ppermute | solution.py:315
  46.7 2.1 %forcing.1 = (f32[80,1536]{1,0:T(8,128)}, f32[80,1536]{1,0:T(8,128)}, f32[80,128]{1,0:T(8,128)}) custom-call(s32[4]{0:T(128)} %pad_add_fusion.place, bf16[80,1024]{1,0:T(8,128)(2,1)} %get-tuple-element.36.f1, bf16[80,1024]{1,0:T(8,128)(2,1)} %get-tuple-element.37.f2, bf16[80,512]{1,0:T(8,128)(2,1)} %copy-done.7, bf16[80,512]{1,0:T(8,128)(2,1)} %copy-done.8, ...), custom_call_target="tpu_custom_call" | custom-call | tf_op jit(solution)/shard_map/forcing/pallas_call | solution.py:301
  48.8 1.6 %collective-permute-start.11 = (f32[80,128]{1,0:T(8,128)}, f32[80,128]{1,0:T(8,128)S(1)}, u32[]{:S(2)}, u32[]{:S(2)}) collective-permute-start(f32[80,128]{1,0:T(8,128)} %get-tuple-element.43.fown), channel_id=1, source_target_pairs={{0,6},{2,0},{4,2},{6,4},{1,7},{3,1},{5,3},{7,5},{8,14},{10,8},{12,... | collective-permute-start | bytes 122888 | tf_op jit(solution)/shard_map/ppermute | solution.py:315
  50.8 2.2 %collective-permute-done.11.feast = f32[80,128]{1,0:T(8,128)S(1)} collective-permute-done((f32[80,128]{1,0:T(8,128)}, f32[80,128]{1,0:T(8,128)S(1)}, u32[]{:S(2)}, u32[]{:S(2)}) %collective-permute-start.11) | collective-permute-done | bytes 40992 | tf_op jit(solution)/shard_map/ppermute | solution.py:315
  53.0 3.4 %collective-permute-done.10.fwest = f32[80,128]{1,0:T(8,128)S(1)} collective-permute-done((f32[80,128]{1,0:T(8,128)}, f32[80,128]{1,0:T(8,128)S(1)}, u32[]{:S(2)}, u32[]{:S(2)}) %collective-permute-start.10) | collective-permute-done | bytes 40992 | tf_op jit(solution)/shard_map/ppermute | solution.py:315
  57.0 4.1 %backward.1 = (f32[320,128]{1,0:T(8,128)}, f32[320,128]{1,0:T(8,128)}) custom-call(s32[4]{0:T(128)} %pad_add_fusion.place, f32[80,1536]{1,0:T(8,128)} %get-tuple-element.41.win_1, f32[80,1536]{1,0:T(8,128)} %get-tuple-element.42.win_2, f32[80,128]{1,0:T(8,128)} %copy-done.9, f32[80,128]{1,0:T(8,128)} %get-tuple-element.43.fown, f32[80,128]{1,0:T(8,128)} %copy-done.11, ...), custom_call_target="tpu_custom_call" | custom-call | tf_op jit(solution)/shard_map/backward/pallas_call | solution.py:301
  61.1 0.7 slice_add_fusion
  61.8 2.4 %collective-permute-start.13 = (f32[8,128]{1,0:T(8,128)S(1)}, f32[8,128]{1,0:T(8,128)S(1)}, u32[]{:S(2)}, u32[]{:S(2)}) collective-permute-start(f32[8,128]{1,0:T(8,128)S(1)} %slice_add_fusion), channel_id=1, source_target_pairs={{0,16},{8,24},{16,0},{24,8},{1,17},{9,25},{17,1},{25,9},{2,18},{10... | collective-permute-start | bytes 12296 | tf_op jit(solution)/shard_map/ppermute | solution.py:315
  64.1 1.6 %collective-permute-done.13 = f32[8,128]{1,0:T(8,128)S(1)} collective-permute-done((f32[8,128]{1,0:T(8,128)S(1)}, f32[8,128]{1,0:T(8,128)S(1)}, u32[]{:S(2)}, u32[]{:S(2)}) %collective-permute-start.13) | collective-permute-done | bytes 4128 | tf_op jit(solution)/shard_map/ppermute | solution.py:315
  65.7 4.5 %collective-permute-done.14 = f32[8,128]{1,0:T(8,128)S(1)} collective-permute-done((f32[8,128]{1,0:T(8,128)S(1)}, f32[8,128]{1,0:T(8,128)S(1)}, u32[]{:S(2)}, u32[]{:S(2)}) %collective-permute-start.14) | collective-permute-done | bytes 4128 | tf_op jit(solution)/shard_map/ppermute | solution.py:315
  70.2 1.2 %collective-permute-done.15 = f32[8,128]{1,0:T(8,128)S(1)} collective-permute-done((f32[8,128]{1,0:T(8,128)S(1)}, f32[8,128]{1,0:T(8,128)S(1)}, u32[]{:S(2)}, u32[]{:S(2)}) %collective-permute-start.15) | collective-permute-done | bytes 4128 | tf_op jit(solution)/shard_map/ppermute | solution.py:341
  72.6 1.8 %maximum_select_fusion = f32[40,16,128]{2,1,0:T(8,128)} fusion(f32[40,8,128]{2,1,0:T(8,128)S(1)} %bitcast.25, f32[40,8,128]{2,1,0:T(8,128)} %bitcast.24, pred[]{:T(512)S(6)} %eq.13), kind=kLoop, calls=%fused_computation | loop fusion | flops 245760 | bytes 655361 | tf_op jit(solution)/shard_map/jit(_where)/select_n | solution.py:408
  (60 shorter events, 7.6 us)
Async XLA Ops:
  0.6 4.5 %collective-permute-start = (f32[640,128]{1,0:T(8,128)}, f32[640,128]{1,0:T(8,128)S(1)}, u32[]{:S(2)}, u32[]{:S(2)}) collective-permute-start(f32[640,128]{1,0:T(8,128)} %bitcast.18), channel_id=1, source_target_pairs={{0,1},{1,0},{2,3},{3,2},{4,5},{5,4},{6,7},{7,6},{8,9},{9,8},{10,11... | collective-permute-start | bytes 983048 | tf_op jit(solution)/shard_map/ppermute | solution.py:341
  1.2 4.0 %collective-permute-start.1 = (f32[640,128]{1,0:T(8,128)}, f32[640,128]{1,0:T(8,128)S(1)}, u32[]{:S(2)}, u32[]{:S(2)}) collective-permute-start(f32[640,128]{1,0:T(8,128)} %bitcast.20), channel_id=1, source_target_pairs={{0,1},{1,0},{2,3},{3,2},{4,5},{5,4},{6,7},{7,6},{8,9},{9,8},{10,11... | collective-permute-start | bytes 983048 | tf_op jit(solution)/shard_map/ppermute | solution.py:341
  1.3 3.9 %collective-permute-start.2 = (f32[640,128]{1,0:T(8,128)}, f32[640,128]{1,0:T(8,128)S(1)}, u32[]{:S(2)}, u32[]{:S(2)}) collective-permute-start(f32[640,128]{1,0:T(8,128)} %bitcast.22), channel_id=1, source_target_pairs={{0,1},{1,0},{2,3},{3,2},{4,5},{5,4},{6,7},{7,6},{8,9},{9,8},{10,11... | collective-permute-start | bytes 983048 | tf_op jit(solution)/shard_map/ppermute | solution.py:341
  2.6 0.7 copy-start.12
  3.4 1.8 %copy-start.4 = (f32[40,256]{1,0:T(8,128)}, f32[40,256]{1,0:T(8,128)S(1)}, u32[]{:S(2)}) copy-start(f32[40,256]{1,0:T(8,128)S(1)} %pad_maximum_fusion.own_par) | copy-start | bytes 122884
  3.4 1.7 %collective-permute-start.3 = (f32[40,256]{1,0:T(8,128)S(1)}, f32[40,256]{1,0:T(8,128)S(1)}, u32[]{:S(2)}, u32[]{:S(2)}) collective-permute-start(f32[40,256]{1,0:T(8,128)S(1)} %pad_maximum_fusion.own_par), channel_id=1, source_target_pairs={{0,1},{1,0},{2,3},{3,2},{4,5},{5,4},{6,7},{7,6},{8,9},{9,8},{10,11... | collective-permute-start | bytes 122888 | tf_op jit(solution)/shard_map/ppermute | solution.py:341
  5.2 0.7 copy-start
  5.2 0.8 %copy-start.1 = (f32[640,128]{1,0:T(8,128)}, f32[640,128]{1,0:T(8,128)S(1)}, u32[]{:S(2)}) copy-start(f32[640,128]{1,0:T(8,128)S(1)} %collective-permute-done.1.u2) | copy-start | bytes 983044
  6.0 0.7 copy-start.2
  9.9 0.7 collective-permute-start.4
  13.9 8.4 %collective-permute-start.6 = (f32[80,128]{1,0:T(8,128)}, f32[80,128]{1,0:T(8,128)S(1)}, u32[]{:S(2)}, u32[]{:S(2)}) collective-permute-start(f32[80,128]{1,0:T(8,128)} %get-tuple-element.32.own), channel_id=1, source_target_pairs={{0,6},{2,0},{4,2},{6,4},{1,7},{3,1},{5,3},{7,5},{8,14},{10,8},{12,... | collective-permute-start | bytes 122888 | tf_op jit(solution)/shard_map/ppermute | solution.py:315
  18.6 6.0 %collective-permute-start.5 = (f32[80,128]{1,0:T(8,128)}, f32[80,128]{1,0:T(8,128)S(1)}, u32[]{:S(2)}, u32[]{:S(2)}) collective-permute-start(f32[80,128]{1,0:T(8,128)} %get-tuple-element.32.own), channel_id=1, source_target_pairs={{0,2},{2,4},{4,6},{6,0},{1,3},{3,5},{5,7},{7,1},{8,10},{10,12},{12... | collective-permute-start | bytes 122888 | tf_op jit(solution)/shard_map/ppermute | solution.py:315
  22.3 2.3 %copy-start.5 = (f32[80,128]{1,0:T(8,128)}, f32[80,128]{1,0:T(8,128)S(1)}, u32[]{:S(2)}) copy-start(f32[80,128]{1,0:T(8,128)S(1)} %collective-permute-done.6.east) | copy-start | bytes 122884
  29.4 11.7 %copy-start.14 = (f32[8,128]{1,0:T(8,128)S(1)}, f32[8,128]{1,0:T(8,128)}, u32[]{:S(2)}) copy-start(f32[8,128]{1,0:T(8,128)} %get-tuple-element.40.cost) | copy-start | bytes 12292
  29.4 16.6 %collective-permute-start.7 = (bf16[80,512]{1,0:T(8,128)(2,1)}, bf16[80,512]{1,0:T(8,128)(2,1)S(1)}, u32[]{:S(2)}, u32[]{:S(2)}) collective-permute-start(bf16[80,512]{1,0:T(8,128)(2,1)} %get-tuple-element.38), channel_id=1, source_target_pairs={{1,8},{9,16},{17,24},{8,1},{16,9},{24,17},{3,10},{11,18},{19,26},{... | collective-permute-start | bytes 245768 | tf_op jit(solution)/shard_map/ppermute | solution.py:344
  30.0 16.0 %collective-permute-start.8 = (bf16[80,512]{1,0:T(8,128)(2,1)}, bf16[80,512]{1,0:T(8,128)(2,1)S(1)}, u32[]{:S(2)}, u32[]{:S(2)}) collective-permute-start(bf16[80,512]{1,0:T(8,128)(2,1)} %get-tuple-element.39), channel_id=1, source_target_pairs={{0,1},{1,0},{2,3},{3,2},{4,5},{5,4},{6,7},{7,6},{8,9},{9,8},{10,11... | collective-permute-start | bytes 245768 | tf_op jit(solution)/shard_map/ppermute | solution.py:341
  41.0 5.0 %collective-permute-start.9 = (f32[8,128]{1,0:T(8,128)S(1)}, f32[8,128]{1,0:T(8,128)S(1)}, u32[]{:S(2)}, u32[]{:S(2)}) collective-permute-start(f32[8,128]{1,0:T(8,128)S(1)} %copy-done.14), channel_id=1, source_target_pairs={{0,8},{8,16},{16,24},{24,0},{1,9},{9,17},{17,25},{25,1},{2,10},{10... | collective-permute-start | bytes 12296 | tf_op jit(solution)/shard_map/ppermute | solution.py:315
  48.8 4.2 %collective-permute-start.11 = (f32[80,128]{1,0:T(8,128)}, f32[80,128]{1,0:T(8,128)S(1)}, u32[]{:S(2)}, u32[]{:S(2)}) collective-permute-start(f32[80,128]{1,0:T(8,128)} %get-tuple-element.43.fown), channel_id=1, source_target_pairs={{0,6},{2,0},{4,2},{6,4},{1,7},{3,1},{5,3},{7,5},{8,14},{10,8},{12,... | collective-permute-start | bytes 122888 | tf_op jit(solution)/shard_map/ppermute | solution.py:315
  50.3 6.0 %collective-permute-start.10 = (f32[80,128]{1,0:T(8,128)}, f32[80,128]{1,0:T(8,128)S(1)}, u32[]{:S(2)}, u32[]{:S(2)}) collective-permute-start(f32[80,128]{1,0:T(8,128)} %get-tuple-element.43.fown), channel_id=1, source_target_pairs={{0,2},{2,4},{4,6},{6,0},{1,3},{3,5},{5,7},{7,1},{8,10},{10,12},{12... | collective-permute-start | bytes 122888 | tf_op jit(solution)/shard_map/ppermute | solution.py:315
  53.0 3.4 %copy-start.11 = (f32[80,128]{1,0:T(8,128)}, f32[80,128]{1,0:T(8,128)S(1)}, u32[]{:S(2)}) copy-start(f32[80,128]{1,0:T(8,128)S(1)} %collective-permute-done.11.feast) | copy-start | bytes 122884
  61.1 11.6 %collective-permute-start.12 = (f32[320,128]{1,0:T(8,128)}, f32[320,128]{1,0:T(8,128)S(1)}, u32[]{:S(2)}, u32[]{:S(2)}) collective-permute-start(f32[320,128]{1,0:T(8,128)} %get-tuple-element.45), channel_id=1, source_target_pairs={{0,1},{1,0},{2,3},{3,2},{4,5},{5,4},{6,7},{7,6},{8,9},{9,8},{10,11... | collective-permute-start | bytes 491528 | tf_op jit(solution)/shard_map/ppermute | solution.py:341
  61.8 4.0 %collective-permute-start.13 = (f32[8,128]{1,0:T(8,128)S(1)}, f32[8,128]{1,0:T(8,128)S(1)}, u32[]{:S(2)}, u32[]{:S(2)}) collective-permute-start(f32[8,128]{1,0:T(8,128)S(1)} %slice_add_fusion), channel_id=1, source_target_pairs={{0,16},{8,24},{16,0},{24,8},{1,17},{9,25},{17,1},{25,9},{2,18},{10... | collective-permute-start | bytes 12296 | tf_op jit(solution)/shard_map/ppermute | solution.py:315
  65.7 4.5 %collective-permute-start.14 = (f32[8,128]{1,0:T(8,128)S(1)}, f32[8,128]{1,0:T(8,128)S(1)}, u32[]{:S(2)}, u32[]{:S(2)}) collective-permute-start(f32[8,128]{1,0:T(8,128)S(1)} %add.13), channel_id=1, source_target_pairs={{0,4},{2,6},{4,0},{6,2},{1,5},{3,7},{5,1},{7,3},{8,12},{10,14},{12... | collective-permute-start | bytes 12296 | tf_op jit(solution)/shard_map/ppermute | solution.py:315
  70.2 1.2 %collective-permute-start.15 = (f32[8,128]{1,0:T(8,128)S(1)}, f32[8,128]{1,0:T(8,128)S(1)}, u32[]{:S(2)}, u32[]{:S(2)}) collective-permute-start(f32[8,128]{1,0:T(8,128)S(1)} %add.14), channel_id=1, source_target_pairs={{0,1},{1,0},{2,3},{3,2},{4,5},{5,4},{6,7},{7,6},{8,9},{9,8},{10,11... | collective-permute-start | bytes 12296 | tf_op jit(solution)/shard_map/ppermute | solution.py:341
  (9 other events, 5.8 us)

commit v2 on v1

--- a/solution.py
+++ b/solution.py
@@ -81,31 +81,67 @@
     return jnp.concatenate([low, high], axis=1).astype(jnp.bfloat16)
 
 
-def arrange(rows, place, inc, u, v, inc2, u2, v2, own_par, other_par, main_i, main_u, main_v, inner, edge, par):
-    core = place[0]
-    levels, half = own_par.shape[0], rows // 2
-    own = pl.multiple_of(core * levels, 8)
-    other = pl.multiple_of((1 - core) * levels, 8)
-    par[pl.ds(own, levels), :] = own_par[...]
-    par[pl.ds(other, levels), :] = other_par[...]
-    for f, (a, b, main) in enumerate(((inc, inc2, main_i), (u, u2, main_u), (v, v2, main_v))):
-        for src, dst in ((a, own), (b, other)):
-            for j in range(half):
-                main[pl.ds(dst, levels), j * B : (j + 1) * B] = src[pl.ds(core * half + j, levels, stride=rows), :]
-            for j in range(HALO):
-                k = f * HALO + j
-                inner[pl.ds(dst, levels), k * B : (k + 1) * B] = src[
-                    pl.ds(half - core * HALO + j, levels, stride=rows), :
-                ]
-                edge[pl.ds(dst, levels), k * B : (k + 1) * B] = src[
-                    pl.ds(core * (rows - HALO) + j, levels, stride=rows), :
-                ]
-
-
-def by_column(place, lookup, observed, out, live, hot, stacked):
-    core, count = place[0], place[3]
+def spread_rows(rows, core, sources, level, mains, inner, edge):
+    levels = sources[0].shape[0] // rows
+    half = rows // 2
+    at = pl.ds(level, levels)
+    k = 0
+    for src, main, width in zip(sources, mains, (HALO, 1, HALO)):
+        for j in range(half):
+            main[at, j * B : (j + 1) * B] = src[pl.ds(core * half + j, levels, stride=rows), :]
+        for j in range(width):
+            near = jnp.where(core == 0, half + j, half - width + j)
+            far = jnp.where(core == 0, j, rows - width + j)
+            lanes = slice(k * B, (k + 1) * B)
+            inner[at, lanes] = src[pl.ds(near, levels, stride=rows), :]
+            edge[at, lanes] = src[pl.ds(far, levels, stride=rows), :].astype(edge.dtype)
+            k += 1
+
+
+def arrange_own(
+    rows, counts, mixing, diffusion, radiance, inc, u, v, main_i, main_u, main_v, inner, edge, par,
+    mixing_at, diffusion_at, radiance_at, inc_at, u_at, v_at, arrived,
+):
+    core = lax.axis_index("lev")
+    here = (inc_at, u_at, v_at, mixing_at, diffusion_at, radiance_at)
+    copies = [
+        pltpu.make_async_copy(src, dst, arrived.at[i])
+        for i, (src, dst) in enumerate(zip((inc, u, v, mixing, diffusion, radiance), here))
+    ]
+    for copy in copies:
+        copy.start()
+    for copy in copies[3:]:
+        copy.wait()
+    part, levels = mixing.shape
+    square = lax.broadcasted_iota(jnp.int32, (part, part), 0) == lax.broadcasted_iota(jnp.int32, (part, part), 1)
+    column = jnp.sum(jnp.where(square, diffusion_at[...], 0.0), axis=1, keepdims=True)
+    par[:, :B] = jnp.broadcast_to(column, (part, B))
+    par[:, :levels] = mixing_at[...]
+    par[:, B:] = radiance_at[...].astype(jnp.float32)
+    for copy in copies[:3]:
+        copy.wait()
+    level = pl.multiple_of(core * part, 8)
+    spread_rows(rows, core, (inc_at, u_at, v_at), level, (main_i, main_u, main_v), inner, edge)
+
+
+def arrange_other(
+    rows, counts, inc, u, v, main_i0, main_u0, main_v0, inner0, edge0, main_i, main_u, main_v, inner, edge
+):
+    core = lax.axis_index("lev")
+    level = pl.multiple_of((1 - core) * (inc.shape[0] // rows), 8)
+    spread_rows(rows, core, (inc, u, v), level, (main_i, main_u, main_v), inner, edge)
+
+
+def by_column(counts, after, lookup, observed, weight, out, live, weights, hot, stacked):
+    core, count = lax.axis_index("lev"), counts[0, 0]
     steps, slots, channels, width = observed.shape
     columns = hot.shape[0]
+    diagonal = lax.broadcasted_iota(jnp.int32, (channels, channels), 0) == lax.broadcasted_iota(
+        jnp.int32, (channels, channels), 1
+    )
+    weights[...] = jnp.broadcast_to(
+        jnp.sum(jnp.where(diagonal, weight[...], 0.0), axis=1, keepdims=True), weights.shape
+    )
     index = lax.broadcasted_iota(jnp.int32, (columns, width), 0)
     for s in range(slots):
         target = jnp.where(s < count, lookup[s : s + 1, :] - core * columns, -1)
@@ -121,15 +157,28 @@
     live[...] = moved[steps * channels : steps * channels + 8]
 
 
-def windows(place, main_i, main_u, main_v, inner, edge, win_i, win_u, win_v, packed):
-    low = place[0] == 0
+def flags():
+    core, lat = lax.axis_index("lev"), lax.axis_index("lat")
+    first = (core == 1) | (lat > 0)
+    final = (core == 0) | (lat < lax.axis_size("lat") - 1)
+    return core, first, final
+
+
+def fill_halo(win, near, far, low, width):
+    count = win.shape[1] // B
+    win[:, (HALO - width) * B : HALO * B] = jnp.where(low, far, near)
+    win[:, (count - HALO) * B : (count - HALO + width) * B] = jnp.where(low, near, far)
+
+
+def windows(counts, main_i, main_u, main_v, inner, edge, after, win_i, win_u, win_v, packed):
+    low = lax.axis_index("lev") == 0
     count = win_i.shape[1] // B
-    for f, (main, win) in enumerate(((main_i, win_i), (main_u, win_u), (main_v, win_v))):
+    k = 0
+    for main, win, width in ((main_i, win_i, HALO), (main_u, win_u, 1), (main_v, win_v, HALO)):
         win[:, HALO * B : (count - HALO) * B] = main[...]
-        span = slice(f * HALO * B, (f + 1) * HALO * B)
-        near, far = inner[:, span], edge[:, span]
-        win[:, : HALO * B] = jnp.where(low, far, near)
-        win[:, (count - HALO) * B :] = jnp.where(low, near, far)
+        span = slice(k * B, (k + width) * B)
+        fill_halo(win, inner[:, span], edge[:, span].astype(jnp.float32), low, width)
+        k += width
     packed[...] = pack_edges([functools.partial(block, win) for win in (win_i, win_u, win_v)], count - 2)
 
 
@@ -143,9 +192,13 @@
 
 
 def forward(
-    place, win_i, win_u, win_v, west, own, east, par, weight, observed, live,
-    f1, f2, edge, inner, cost, stack, plain, state,
+    counts, win_i, win_u, win_v, west, own, east, own_par, other_par, observed, live, weights,
+    f1, f2, edge, inner, cost, par, stack, plain, state,
 ):
+    core, is_first, is_final = flags()
+    part = own_par.shape[0]
+    par[pl.ds(pl.multiple_of(core * part, 8), part), :] = own_par[...]
+    par[pl.ds(pl.multiple_of((1 - core) * part, 8), part), :] = other_par[...]
     levels = par.shape[0]
     count = win_i.shape[1] // B
     rows = count - 2
@@ -154,10 +207,7 @@
     coupling = split_matrix(par[:, :B], levels)
     radiance = par[:, B:].astype(jnp.bfloat16)
     channels = radiance.shape[1]
-    diagonal = lax.broadcasted_iota(jnp.int32, (channels, channels), 0) == lax.broadcasted_iota(
-        jnp.int32, (channels, channels), 1
-    )
-    weights = jnp.sum(jnp.where(diagonal, weight[...], 0.0), axis=1, keepdims=True)
+    scale = weights[:, :1]
     clear_rest(stack, levels)
     sides = [side_block(west[...], own[...], east[...], f, rows) for f in range(3)]
     for q in range(rows):
@@ -175,8 +225,8 @@
     put_split(stack, rows, s)
     state[...] = plain[...] + jnp.dot(coupling, stack[...], preferred_element_type=jnp.float32)
     first, final = (rows - 1) * B, rows * B
-    state[:, :B] = jnp.where(place[1] == 1, state[:, :B], 0.0)
-    state[:, first:final] = jnp.where(place[2] == 1, state[:, first:final], 0.0)
+    state[:, :B] = jnp.where(is_first, state[:, :B], 0.0)
+    state[:, first:final] = jnp.where(is_final, state[:, first:final], 0.0)
 
     def observe(profile, t, out):
         evolved = lax.dot_general(
@@ -184,7 +234,7 @@
         )
         departure = evolved - observed[t * channels : (t + 1) * channels, :].astype(jnp.float32)
         misfit = live[0:1, :] * departure
-        scaled = weights * misfit
+        scaled = scale * misfit
         back = jnp.dot(radiance, scaled.astype(jnp.bfloat16), preferred_element_type=jnp.float32)
         out[...] = back.astype(jnp.bfloat16)
         return jnp.sum(misfit * scaled, keepdims=True)
@@ -204,33 +254,51 @@
     whole = win_i[:, HALO * B : (count - HALO) * B]
     total = 0.5 * (total + jnp.sum(whole * whole, keepdims=True))
     cost[...] = jnp.broadcast_to(total, cost.shape)
-    low = place[0] == 0
-    span = HALO * B
-    for k, f in enumerate((f2, f1)):
-        head, tail = f[:, :span].astype(jnp.float32), f[:, (half - HALO) * B :].astype(jnp.float32)
-        edge[:, k * span : (k + 1) * span] = jnp.where(low, head, tail).astype(jnp.bfloat16)
-        inner[:, k * span : (k + 1) * span] = jnp.where(low, tail, head).astype(jnp.bfloat16)
-
-
-def forcing_windows(place, f1, f2, edge, inner, cost, other_cost, win_1, win_2, packed):
-    low = place[0] == 0
+    low = core == 0
+    k = 0
+    for f, width in ((f2, HALO), (f1, 1)):
+        head, tail = f[:, : width * B].astype(jnp.float32), f[:, (half - width) * B :].astype(jnp.float32)
+        edge[:levels, k * B : (k + width) * B] = jnp.where(low, head, tail).astype(jnp.bfloat16)
+        inner[:, k * B : (k + width) * B] = jnp.where(low, tail, head).astype(jnp.bfloat16)
+        k += width
+    tail = edge.shape[0] - levels
+    head = total.astype(jnp.bfloat16).astype(jnp.float32)
+    rest = (total - head).astype(jnp.bfloat16).astype(jnp.float32)
+    pieces = (head, rest, total - head - rest)
+    lane = lanes_of(tail)
+    carried = jnp.zeros((tail, B), jnp.float32)
+    for i, piece in enumerate(pieces):
+        carried = jnp.where(lane == i, piece, carried)
+    edge[levels:, :B] = carried.astype(jnp.bfloat16)
+    edge[levels:, B:] = jnp.zeros((tail, edge.shape[1] - B), jnp.bfloat16)
+
+
+def forcing_windows(counts, f1, f2, edge, inner, cost, win_1, win_2, packed, total):
+    core, is_first, is_final = flags()
+    low = core == 0
+    inside = is_first & is_final
+    levels = f1.shape[0]
     count = win_1.shape[1] // B
-    span = HALO * B
-    for k, (f, win) in enumerate(((f2, win_2), (f1, win_1))):
-        win[:, span : (count - HALO) * B] = f[...].astype(jnp.float32)
-        far = edge[:, k * span : (k + 1) * span].astype(jnp.float32)
-        near = inner[:, k * span : (k + 1) * span].astype(jnp.float32)
-        win[:, :span] = jnp.where(low, far, near)
-        win[:, (count - HALO) * B :] = jnp.where(low, near, far)
+    k = 0
+    for f, win, width in ((f2, win_2, HALO), (f1, win_1, 1)):
+        win[:, HALO * B : (count - HALO) * B] = f[...].astype(jnp.float32)
+        span = slice(k * B, (k + width) * B)
+        far = jnp.where(inside, edge[:levels, span].astype(jnp.float32), 0.0)
+        fill_halo(win, inner[:, span].astype(jnp.float32), far, low, width)
+        k += width
     both = pack_edges([functools.partial(block, win) for win in (win_2, win_1)], count - 2)
-    total = cost[0:1, :] + other_cost[0:1, :]
-    packed[...] = jnp.where(lanes_of(both.shape[0]) == B - 1, total, both)
+    carried = edge[levels:, :B].astype(jnp.float32)
+    carried = jnp.sum(jnp.where(lanes_of(carried.shape[0]) < 3, carried, 0.0), axis=1, keepdims=True)
+    here = cost[...] + carried[: cost.shape[0]]
+    total[...] = here
+    packed[...] = jnp.where(lanes_of(both.shape[0]) == B - 1, here[0:1, :], both)
 
 
 def backward(
-    place, win_1, win_2, fwest, fown, feast, win_i, win_u, win_v, west, own, east, par,
+    counts, win_1, win_2, fwest, fown, feast, win_i, win_u, win_v, west, own, east, par,
     kept, sent, stack, coupled, square,
 ):
+    core, is_first, is_final = flags()
     levels = par.shape[0]
     count = win_i.shape[1] // B
     rows = count - 2
@@ -276,8 +344,8 @@
     )
     for q in range(rows):
         after.append(spread(q + 1, q, side) + block(win_1, q + 1))
-    after[0] = jnp.where(place[1] == 1, after[0], 0.0)
-    after[-1] = jnp.where(place[2] == 1, after[-1], 0.0)
+    after[0] = jnp.where(is_first, after[0], 0.0)
+    after[-1] = jnp.where(is_final, after[-1], 0.0)
     for q in range(rows):
         coupled[:, (q + 1) * B : (q + 2) * B] = after[q]
         put_split(stack, q, after[q])
@@ -286,7 +354,7 @@
     mixed = jnp.dot(coupling, stack[:, : (rows + 1) * B], preferred_element_type=jnp.float32)
     coupled[:, B : (rows + 1) * B] = coupled[:, B : (rows + 1) * B] + mixed[:, : rows * B]
     side = coupled[:, count * B :] + mixed[:, rows * B :]
-    low = place[0] == 0
+    low = core == 0
     part = levels // 2
     for j in range(half):
         value = block(win_i, j + HALO) + spread(j + HALO, j + 1, side)
@@ -294,18 +362,27 @@
         sent[pl.ds(j, part, stride=half), :] = jnp.where(low, value[part:], value[:part])
 
 
-def call(kernel, outs, scratch=(), name=None):
+def call(kernel, outs, scratch=(), name=None, aliases=None, in_hbm=False, flops=10**9):
     vmem = pl.BlockSpec(memory_space=pltpu.VMEM)
-
-    def run(place, *operands):
+    source = pl.BlockSpec(memory_space=pltpu.HBM) if in_hbm else vmem
+
+    def run(counts, *operands):
+        if in_hbm:
+            operands = [pltpu.with_memory_space_constraint(x, pltpu.HBM) for x in operands]
         return pl.pallas_call(
             kernel,
             out_shape=[jax.ShapeDtypeStruct(shape, dtype) for shape, dtype in outs],
-            in_specs=[pl.BlockSpec(memory_space=pltpu.SMEM)] + [vmem] * len(operands),
+            in_specs=[pl.BlockSpec(memory_space=pltpu.SMEM)] + [source] * len(operands),
             out_specs=[vmem] * len(outs),
-            scratch_shapes=[pltpu.VMEM(shape, dtype) for shape, dtype in scratch],
+            scratch_shapes=[
+                pltpu.SemaphoreType.DMA(shape) if dtype is None else pltpu.VMEM(shape, dtype)
+                for shape, dtype in scratch
+            ],
+            input_output_aliases=aliases or {},
             name=name,
-        )(place, *operands)
+            cost_estimate=pl.CostEstimate(flops=flops, bytes_accessed=0, transcendentals=0),
+            compiler_params=pltpu.CompilerParams(vmem_limit_bytes=24 * 2**20),
+        )(counts, *operands)
 
     return run
 
@@ -327,88 +404,93 @@
     count = half + 2 * HALO
     columns = half * B
     f32, bf16 = jnp.float32, jnp.bfloat16
-    core, lat = lax.axis_index("lev"), lax.axis_index("lat")
-    tiles = lax.axis_size("lat")
-    at_top = (core == 0) & (lat == 0)
-    at_end = (core == 1) & (lat == tiles - 1)
-    place = jnp.stack(
-        [core.astype(jnp.int32), 1 - at_top.astype(jnp.int32), 1 - at_end.astype(jnp.int32), counts[0, 0]]
-    )
-    pairs = [(2 * i + 1, 2 * i + 2) for i in range(tiles - 1)]
+    tiles, along = lax.axis_size("lat"), lax.axis_size("lon")
+    pairs = [(2 * i + 1, (2 * i + 2) % (2 * tiles)) for i in range(tiles)]
     pairs = pairs + [(b, a) for a, b in pairs]
+    inside = [(a, b) for a, b in pairs if abs(a - b) == 1]
 
     def swap(x):
         return lax.ppermute(x, "lev", [(0, 1), (1, 0)])
 
-    def across(x):
-        return lax.ppermute(x, ("lat", "lev"), pairs)
-
-    own_par = jnp.concatenate(
-        [
-            mixing,
-            diffusion[:, None],
-            jnp.zeros((part, B - levels - 1), f32),
-            jacobian.T.astype(f32),
-        ],
-        axis=1,
-    )
+    def across(x, which):
+        return lax.ppermute(x, ("lat", "lev"), which)
+
     fields = [x.reshape(part * rows, B) for x in (increment, wind_u, wind_v)]
     others = [swap(x) for x in fields]
-    other_par = swap(own_par)
+    halo = 2 * HALO + 1
     main = ((levels, columns), f32)
-    edges = ((levels, 3 * HALO * B), f32)
+    groups = [main] * 3 + [((levels, halo * B), f32), ((levels, halo * B), bf16)]
     win = ((levels, count * B), f32)
     packed = ((levels, B), f32)
-    *mains, inner, edge, par = call(
-        functools.partial(arrange, rows), [main] * 3 + [edges] * 2 + [((levels, 2 * B), f32)], name="arrange"
-    )(place, *fields, *others, own_par, other_par)
-    edge = across(edge)
-    observed, live = call(
+    field = ((part * rows, B), f32)
+    *sorted_rows, own_par = call(
+        functools.partial(arrange_own, rows),
+        groups + [((part, 2 * B), f32)],
+        [((part, levels), f32), ((1, part), f32), ((part, channels), bf16)] + [field] * 3 + [((6,), None)],
+        name="arrange_own",
+        in_hbm=True,
+    )(counts, mixing, diffusion.reshape(1, -1), jacobian.T, *fields)
+    *mains, inner, edge = call(
+        functools.partial(arrange_other, rows), groups, name="arrange_other",
+        aliases={4 + i: i for i in range(5)},
+    )(counts, *others, *sorted_rows)
+    edge = across(edge, inside)
+    other_par = swap(own_par)
+    observed, live, weights = call(
         by_column,
-        [((steps * channels, columns), bf16), ((8, columns), f32)],
+        [((steps * channels, columns), bf16), ((8, columns), f32), ((channels, B), f32)],
         [((columns, slots * B), bf16), ((steps * channels + 16, slots * B), bf16)],
         name="by_column",
-    )(place, column_lookup.reshape(slots, B), innovation.reshape(steps, slots, channels, B))
-    win_i, win_u, win_v, own = call(windows, [win] * 3 + [packed], name="windows")(place, *mains, inner, edge)
+    )(
+        counts, inner, column_lookup.reshape(slots, B), innovation.reshape(steps, slots, channels, B),
+        obs_weight.reshape(1, -1),
+    )
+    win_i, win_u, win_v, own = call(windows, [win] * 3 + [packed], name="windows")(
+        counts, *mains, inner, edge, live
+    )
     west, east = ring(own, "lon", 1), ring(own, "lon", -1)
     forcing = ((levels, columns), bf16)
-    f_edges = ((levels, 2 * HALO * B), bf16)
-    depth = -(-3 * levels // 16) * 16
-    depth = max(depth, 2 * B)
-    f1, f2, f_edge, f_inner, cost = call(
+    depth = max(-(-3 * levels // 16) * 16, 2 * B)
+    f1, f2, f_edge, f_inner, cost, par = call(
         forward,
-        [forcing] * 2 + [f_edges] * 2 + [((8, B), f32)],
+        [forcing] * 2
+        + [((levels + 16, (HALO + 1) * B), bf16), ((levels, (HALO + 1) * B), bf16)]
+        + [((8, B), f32), ((levels, 2 * B), f32)],
         [((depth, (count - 1) * B), bf16), ((levels, (count - 1) * B), f32), ((levels, (count - 1) * B), f32)],
         name="forward",
-    )(place, win_i, win_u, win_v, west, own, east, par, obs_weight.reshape(1, -1), observed, live)
-    f_edge, f_inner = across(f_edge), swap(f_inner)
-    cost_2 = ring(cost, "lat", 1)
-    win_1, win_2, f_own = call(forcing_windows, [win] * 2 + [packed], name="forcing")(
-        place, f1, f2, f_edge, f_inner, cost, cost_2
-    )
+    )(counts, win_i, win_u, win_v, west, own, east, own_par, other_par, observed, live, weights)
+    f_edge, f_inner = across(f_edge, pairs), swap(f_inner)
+    win_1, win_2, f_own, total = call(
+        forcing_windows, [win] * 2 + [packed, ((8, B), f32)], name="forcing"
+    )(counts, f1, f2, f_edge, f_inner, cost)
     f_west, f_east = ring(f_own, "lon", 1), ring(f_own, "lon", -1)
-    total = f_own[:8] + f_west[:8]
+    if along == 4:
+        total = total + ring(total, "lon", 2) + f_west[:8] + f_east[:8]
+    else:
+        total = total + f_west[:8]
+        shift = 2
+        while shift < along:
+            total = total + ring(total, "lon", shift)
+            shift *= 2
     shift = 2
     while shift < tiles:
         total = total + ring(total, "lat", shift)
         shift *= 2
+    total = total + swap(total)
     kept, sent = call(
         backward,
         [((part * half, B), f32)] * 2,
         [((depth, (count + 1) * B), bf16), ((levels, (count + 1) * B), f32), ((B, B), f32)],
         name="backward",
-    )(place, win_1, win_2, f_west, f_own, f_east, win_i, win_u, win_v, west, own, east, par)
+    )(counts, win_1, win_2, f_west, f_own, f_east, win_i, win_u, win_v, west, own, east, par)
     got = swap(sent)
-    shift = 2
-    while shift < lax.axis_size("lon"):
-        total = total + ring(total, "lon", shift)
-        shift *= 2
-    total = total + swap(total)
     kept, got = kept.reshape(part, half, B), got.reshape(part, half, B)
     gradient = jnp.where(
-        core == 0, jnp.concatenate([kept, got], axis=1), jnp.concatenate([got, kept], axis=1)
-    )
-    cells = increment.size * tiles * lax.axis_size("lon") * lax.axis_size("lev")
+        lax.axis_index("lev") == 0,
+        jnp.concatenate([kept, got], axis=1),
+        jnp.concatenate([got, kept], axis=1),
+    )
+    cells = increment.size * tiles * along * lax.axis_size("lev")
     return gradient, total[0, B - 1] / cells
 
 

time: 76 us -> 45.3 us (0.60)
  Pallas kernels: 19.9 us -> 7.74 us
  starting transfers between devices: 26.6 us -> 16.7 us
  local copies, waits for them, and re-layouts: 6.3 us -> 1.25 us
  other arithmetic: 3.12 us -> 0.76 us
  waiting for transfers between devices: 16.4 us -> 15.3 us
    pallas_call x6 -> x7, Pallas kernels: 19.9 us -> 7.74 us  [run(): pl.pallas_call(kernel, out_shape=[jax.ShapeDtypeStruct(shape, dtype) for...]
    ppermute x7, starting transfers between devices: 12.6 us -> 6.04 us  [swap(): return lax.ppermute(x, 'lev', [(0, 1), (1, 0)])]
    ppermute x7 -> x6, waiting for transfers between devices: 15.2 us -> 9.77 us  [ring(): lax.ppermute(x, axis, [(i, (i + shift) % count) for i in range(count)])]
    unnamed x34 -> x6, local copies, waits for them, and re-layouts: 5.55 us -> 0.66 us
    ppermute x2, waiting for transfers between devices: 0.01 us -> 3.5 us  [across(): return lax.ppermute(x, ('lat', 'lev'), which)]
    ppermute x7 -> x6, starting transfers between devices: 12.7 us -> 9.81 us  [ring(): lax.ppermute(x, axis, [(i, (i + shift) % count) for i in range(count)])]
    select_n x1, other arithmetic: 1.75 us -> 0.75 us  [body(): jnp.where(lax.axis_index('lev') == 0, jnp.concatenate([kept, got], axis=1...]
    ppermute x7, waiting for transfers between devices: 1.18 us -> 2.07 us  [swap(): return lax.ppermute(x, 'lev', [(0, 1), (1, 0)])]
  transfers between devices with their start and end apart: 16 -> 15, of which waited for: 7 -> 8; matrix products, arithmetic and copies ran while one was open for 3% -> 1% of each run, Pallas kernels for 5% -> 12%
where the time goes in v2:
time: 45.3 us; the launch traced here: 45 us
  starting transfers between devices  16.7 us (37%)
  waiting for transfers between devices  15.3 us (34%)
  Pallas kernels  7.74 us (17%)
  between operations  3.22 us (7%)
  local copies, waits for them, and re-layouts  1.25 us (3%)
  other arithmetic  0.76 us (2%)
    ppermute x6, starting transfers between devices, ring(): lax.ppermute(x, axis, [(i, (i + shift) % count) for i in range(count)])  9.81 us
    ppermute x6, waiting for transfers between devices, ring(): lax.ppermute(x, axis, [(i, (i + shift) % count) for i in range(count)])  9.77 us
    pallas_call x7, Pallas kernels, run(): pl.pallas_call(kernel, out_shape=[jax.ShapeDtypeStruct(shape, dtype) for...  7.74 us
    ppermute x7, starting transfers between devices, swap(): return lax.ppermute(x, 'lev', [(0, 1), (1, 0)])  6.04 us
    ppermute x2, waiting for transfers between devices, across(): return lax.ppermute(x, ('lat', 'lev'), which)  3.5 us
    ppermute x7, waiting for transfers between devices, swap(): return lax.ppermute(x, 'lev', [(0, 1), (1, 0)])  2.07 us
  transfers between devices with their start and end apart: 15, of which 8 were waited for; matrix products, arithmetic and copies ran while one was open for 1% of the time, Pallas kernels for 12%

profile of v2, /device:TPU:0, one launch (start us, length us, event | category | flops | bytes accessed | tf_op | source)
XLA Modules:
  0.0 45.0 jit_solution(6870543176456685799)
XLA Ops:
  0.6 0.6 %collective-permute-start = (f32[640,128]{1,0:T(8,128)}, f32[640,128]{1,0:T(8,128)S(1)}, u32[]{:S(2)}, u32[]{:S(2)}) collective-permute-start(f32[640,128]{1,0:T(8,128)} %bitcast.16), channel_id=1, source_target_pairs={{0,1},{1,0},{2,3},{3,2},{4,5},{5,4},{6,7},{7,6},{8,9},{9,8},{10,11... | collective-permute-start | bytes 983048 | tf_op jit(solution)/shard_map/ppermute | solution.py:413
  2.4 1.5 %arrange_own.1 = (f32[80,1024]{1,0:T(8,128)S(1)}, f32[80,1024]{1,0:T(8,128)S(1)}, f32[80,1024]{1,0:T(8,128)S(1)}, f32[80,640]{1,0:T(8,128)S(1)}, bf16[80,640]{1,0:T(8,128)(2,1)S(1)}, /*index=5*/f32[40,256]{1,0:T(8,128)S(1)}) custom-call(s32[1,1]{1,0:T(1,128)S(6)} %copy.22.counts, f32[40,80]{1,0:T(8,128)} %mixing.1, f32[1,40]{1,0:T(1,128)} %bitcast.23, ...), custom_call_target="tpu_custom_call" | custom-call | flops 1000000000 | tf_op jit(solution)/shard_map/arrange_own/pallas_call | solution.py:372
  4.2 0.8 %collective-permute-start.3 = (bf16[80,640]{1,0:T(8,128)(2,1)S(1)}, bf16[80,640]{1,0:T(8,128)(2,1)S(1)}, u32[]{:S(2)}, u32[]{:S(2)}) collective-permute-start(bf16[80,640]{1,0:T(8,128)(2,1)S(1)} %get-tuple-element.41), channel_id=1, source_target_pairs={{1,8},{9,16},{17,24},{8,1},{16,9},{24,17},{3,10},{11,18},{19,26},{... | collective-permute-start | bytes 307208 | tf_op jit(solution)/shard_map/ppermute | solution.py:416
  5.0 4.0 %collective-permute-start.6 = (f32[40,256]{1,0:T(8,128)S(1)}, f32[40,256]{1,0:T(8,128)S(1)}, u32[]{:S(2)}, u32[]{:S(2)}) collective-permute-start(f32[40,256]{1,0:T(8,128)S(1)} %get-tuple-element.47.own_par), channel_id=1, source_target_pairs={{0,1},{1,0},{2,3},{3,2},{4,5},{5,4},{6,7},{7,6},{8,9},{9,8},{10,11... | collective-permute-start | bytes 122888 | tf_op jit(solution)/shard_map/ppermute | solution.py:413
  9.0 0.6 %copy-done.2 = f32[128]{0:T(128)S(1)} copy-done((f32[128]{0:T(128)S(1)}, f32[128]{0:T(128)}, u32[]{:S(2)}) %copy-start.2) | copy-done | bytes 536
  9.6 1.7 %by_column.1 = (bf16[256,1024]{1,0:T(8,128)(2,1)S(1)}, f32[8,1024]{1,0:T(8,128)S(1)}, f32[128,128]{1,0:T(8,128)S(1)}) custom-call(s32[1,1]{1,0:T(1,128)S(6)} %copy.22.counts, f32[80,640]{1,0:T(8,128)S(1)} %get-tuple-element.40.after.inner, s32[16,128]{1,0:T(8,128)S(1)} %bitcast.13, bf16[2,16,128,128]{3,2,1,0:T(8,128)(2,1)S(1)} %bitcast.12, f32[1,128]{1,0:T(1,128)S(1)} %bitcast.14), custom_call_target="tpu_custom_call" | custom-call | flops 1000000000 | tf_op jit(solution)/shard_map/by_column/pallas_call | solution.py:372
  11.7 1.6 %collective-permute-start.4 = (f32[80,128]{1,0:T(8,128)S(1)}, f32[80,128]{1,0:T(8,128)S(1)}, u32[]{:S(2)}, u32[]{:S(2)}) collective-permute-start(f32[80,128]{1,0:T(8,128)S(1)} %get-tuple-element.46.own), channel_id=1, source_target_pairs={{0,2},{2,4},{4,6},{6,0},{1,3},{3,5},{5,7},{7,1},{8,10},{10,12},{12... | collective-permute-start | bytes 122888 | tf_op jit(solution)/shard_map/ppermute | solution.py:392
  13.3 2.2 %collective-permute-start.5 = (f32[80,128]{1,0:T(8,128)S(1)}, f32[80,128]{1,0:T(8,128)S(1)}, u32[]{:S(2)}, u32[]{:S(2)}) collective-permute-start(f32[80,128]{1,0:T(8,128)S(1)} %get-tuple-element.46.own), channel_id=1, source_target_pairs={{0,6},{2,0},{4,2},{6,4},{1,7},{3,1},{5,3},{7,5},{8,14},{10,8},{12,... | collective-permute-start | bytes 122888 | tf_op jit(solution)/shard_map/ppermute | solution.py:392
  15.6 2.2 %collective-permute-done.4.west = f32[80,128]{1,0:T(8,128)S(1)} collective-permute-done((f32[80,128]{1,0:T(8,128)S(1)}, f32[80,128]{1,0:T(8,128)S(1)}, u32[]{:S(2)}, u32[]{:S(2)}) %collective-permute-start.4) | collective-permute-done | bytes 40992 | tf_op jit(solution)/shard_map/ppermute | solution.py:392
  17.8 0.8 %collective-permute-done.5.east = f32[80,128]{1,0:T(8,128)S(1)} collective-permute-done((f32[80,128]{1,0:T(8,128)S(1)}, f32[80,128]{1,0:T(8,128)S(1)}, u32[]{:S(2)}, u32[]{:S(2)}) %collective-permute-start.5) | collective-permute-done | bytes 40992 | tf_op jit(solution)/shard_map/ppermute | solution.py:392
  18.6 2.0 %forward.1 = (bf16[80,1024]{1,0:T(8,128)(2,1)S(1)}, bf16[80,1024]{1,0:T(8,128)(2,1)S(1)}, bf16[96,384]{1,0:T(8,128)(2,1)S(1)}, bf16[80,384]{1,0:T(8,128)(2,1)S(1...) custom-call(s32[1,1]{1,0:T(1,128)S(6)} %copy.22.counts, f32[80,1536]{1,0:T(8,128)S(1)} %get-tuple-element.43.win_i, ...), custom_call_target="tpu_custom_call" | custom-call | flops 1000000000 | tf_op jit(solution)/shard_map/forward/pallas_call | solution.py:372
  20.7 0.9 %collective-permute-start.8 = (bf16[80,384]{1,0:T(8,128)(2,1)S(1)}, bf16[80,384]{1,0:T(8,128)(2,1)S(1)}, u32[]{:S(2)}, u32[]{:S(2)}) collective-permute-start(bf16[80,384]{1,0:T(8,128)(2,1)S(1)} %get-tuple-element.53), channel_id=1, source_target_pairs={{0,1},{1,0},{2,3},{3,2},{4,5},{5,4},{6,7},{7,6},{8,9},{9,8},{10,11... | collective-permute-start | bytes 184328 | tf_op jit(solution)/shard_map/ppermute | solution.py:413
  21.6 0.9 %collective-permute-done.8.inner = bf16[80,384]{1,0:T(8,128)(2,1)S(1)} collective-permute-done((bf16[80,384]{1,0:T(8,128)(2,1)S(1)}, bf16[80,384]{1,0:T(8,128)(2,1)S(1)}, u32[]{:S(2)}, u32[]{:S(2)}) %collective-permute-start.8) | collective-permute-done | bytes 61472 | tf_op jit(solution)/shard_map/ppermute | solution.py:413
  22.5 3.5 %collective-permute-done.7.edge = bf16[96,384]{1,0:T(8,128)(2,1)S(1)} collective-permute-done((bf16[96,384]{1,0:T(8,128)(2,1)S(1)}, bf16[96,384]{1,0:T(8,128)(2,1)S(1)}, u32[]{:S(2)}, u32[]{:S(2)}) %collective-permute-start.7) | collective-permute-done | bytes 73760 | tf_op jit(solution)/shard_map/ppermute | solution.py:416
  26.2 3.0 %collective-permute-start.10 = (f32[80,128]{1,0:T(8,128)S(1)}, f32[80,128]{1,0:T(8,128)S(1)}, u32[]{:S(2)}, u32[]{:S(2)}) collective-permute-start(f32[80,128]{1,0:T(8,128)S(1)} %get-tuple-element.57.fown), channel_id=1, source_target_pairs={{0,6},{2,0},{4,2},{6,4},{1,7},{3,1},{5,3},{7,5},{8,14},{10,8},{12,... | collective-permute-start | bytes 122888 | tf_op jit(solution)/shard_map/ppermute | solution.py:392
  29.2 0.6 %collective-permute-start.12 = (f32[8,128]{1,0:T(8,128)S(1)}, f32[8,128]{1,0:T(8,128)S(1)}, u32[]{:S(2)}, u32[]{:S(2)}) collective-permute-start(f32[8,128]{1,0:T(8,128)S(1)} %get-tuple-element.61), channel_id=1, source_target_pairs={{0,4},{2,6},{4,0},{6,2},{1,5},{3,7},{5,1},{7,3},{8,12},{10,14},{12... | collective-permute-start | bytes 12296 | tf_op jit(solution)/shard_map/ppermute | solution.py:392
  29.8 1.0 %collective-permute-done.10.feast = f32[80,128]{1,0:T(8,128)S(1)} collective-permute-done((f32[80,128]{1,0:T(8,128)S(1)}, f32[80,128]{1,0:T(8,128)S(1)}, u32[]{:S(2)}, u32[]{:S(2)}) %collective-permute-start.10) | collective-permute-done | bytes 40992 | tf_op jit(solution)/shard_map/ppermute | solution.py:392
  30.9 4.1 %collective-permute-done.9.fwest = f32[80,128]{1,0:T(8,128)S(1)} collective-permute-done((f32[80,128]{1,0:T(8,128)S(1)}, f32[80,128]{1,0:T(8,128)S(1)}, u32[]{:S(2)}, u32[]{:S(2)}) %collective-permute-start.9) | collective-permute-done | bytes 40992 | tf_op jit(solution)/shard_map/ppermute | solution.py:392
  35.0 1.7 %backward.1 = (f32[320,128]{1,0:T(8,128)S(1)}, f32[320,128]{1,0:T(8,128)S(1)}) custom-call(s32[1,1]{1,0:T(1,128)S(6)} %copy.22.counts, f32[80,1536]{1,0:T(8,128)S(1)} %get-tuple-element.55.win_1, f32[80,1536]{1,0:T(8,128)S(1)} %get-tuple-element.56.win_2, f32[80,128]{1,0:T(8,128)S(1)} %collective-permute-done.9.fwest, f32[80,128]{1,0:T(8,128)S(1)} %get-tuple-element.57.fown, ...), custom_call_target="tpu_custom_call" | custom-call | flops 1000000000 | tf_op jit(solution)/shard_map/backward/pallas_call | solution.py:372
  36.8 2.3 %collective-permute-start.13 = (f32[8,128]{1,0:T(8,128)S(1)}, f32[8,128]{1,0:T(8,128)S(1)}, u32[]{:S(2)}, u32[]{:S(2)}) collective-permute-start(f32[8,128]{1,0:T(8,128)S(1)} %slice_add_fusion), channel_id=1, source_target_pairs={{0,16},{8,24},{16,0},{24,8},{1,17},{9,25},{17,1},{25,9},{2,18},{10... | collective-permute-start | bytes 12296 | tf_op jit(solution)/shard_map/ppermute | solution.py:392
  39.1 1.6 %collective-permute-done.13 = f32[8,128]{1,0:T(8,128)S(1)} collective-permute-done((f32[8,128]{1,0:T(8,128)S(1)}, f32[8,128]{1,0:T(8,128)S(1)}, u32[]{:S(2)}, u32[]{:S(2)}) %collective-permute-start.13) | collective-permute-done | bytes 4128 | tf_op jit(solution)/shard_map/ppermute | solution.py:392
  40.7 1.2 %collective-permute-done.14 = f32[8,128]{1,0:T(8,128)S(1)} collective-permute-done((f32[8,128]{1,0:T(8,128)S(1)}, f32[8,128]{1,0:T(8,128)S(1)}, u32[]{:S(2)}, u32[]{:S(2)}) %collective-permute-start.14) | collective-permute-done | bytes 4128 | tf_op jit(solution)/shard_map/ppermute | solution.py:413
  41.9 0.6 %slice.11 = f32[1,1]{1,0:T(1,128)} slice(f32[8,128]{1,0:T(8,128)S(1)} %add.19), slice={[0:1], [127:128]} | slice | bytes 8 | tf_op jit(solution)/shard_map/slice | solution.py:494
  43.1 0.7 %maximum_select_fusion = f32[40,16,128]{2,1,0:T(8,128)} fusion(f32[40,8,128]{2,1,0:T(8,128)S(1)} %bitcast.15, f32[40,8,128]{2,1,0:T(8,128)S(1)} %bitcast.11, pred[]{:T(512)S(6)} %eq.3), kind=kLoop, calls=%fused_computation | loop fusion | flops 245760 | bytes 655361 | tf_op jit(solution)/shard_map/jit(_where)/select_n | solution.py:488
  (24 shorter events, 1.6 us)
Async XLA Ops:
  0.6 3.2 %collective-permute-start = (f32[640,128]{1,0:T(8,128)}, f32[640,128]{1,0:T(8,128)S(1)}, u32[]{:S(2)}, u32[]{:S(2)}) collective-permute-start(f32[640,128]{1,0:T(8,128)} %bitcast.16), channel_id=1, source_target_pairs={{0,1},{1,0},{2,3},{3,2},{4,5},{5,4},{6,7},{7,6},{8,9},{9,8},{10,11... | collective-permute-start | bytes 983048 | tf_op jit(solution)/shard_map/ppermute | solution.py:413
  1.2 2.7 %collective-permute-start.1 = (f32[640,128]{1,0:T(8,128)}, f32[640,128]{1,0:T(8,128)S(1)}, u32[]{:S(2)}, u32[]{:S(2)}) collective-permute-start(f32[640,128]{1,0:T(8,128)} %bitcast.18), channel_id=1, source_target_pairs={{0,1},{1,0},{2,3},{3,2},{4,5},{5,4},{6,7},{7,6},{8,9},{9,8},{10,11... | collective-permute-start | bytes 983048 | tf_op jit(solution)/shard_map/ppermute | solution.py:413
  1.3 2.6 %collective-permute-start.2 = (f32[640,128]{1,0:T(8,128)}, f32[640,128]{1,0:T(8,128)S(1)}, u32[]{:S(2)}, u32[]{:S(2)}) collective-permute-start(f32[640,128]{1,0:T(8,128)} %bitcast.20), channel_id=1, source_target_pairs={{0,1},{1,0},{2,3},{3,2},{4,5},{5,4},{6,7},{7,6},{8,9},{9,8},{10,11... | collective-permute-start | bytes 983048 | tf_op jit(solution)/shard_map/ppermute | solution.py:413
  3.9 5.1 %copy-start = (bf16[2,1,1,16,128,128]{5,4,3,2,1,0:T(8,128)(2,1)S(1)}, bf16[2,1,1,16,128,128]{5,4,3,2,1,0:T(8,128)(2,1)}, u32[]{:S(2)}) copy-start(bf16[2,1,1,16,128,128]{5,4,3,2,1,0:T(8,128)(2,1)} %param.17) | copy-start | bytes 3145732
  4.2 4.8 %copy-start.1 = (s32[1,1,2048]{2,1,0:T(1,128)S(1)}, s32[1,1,2048]{2,1,0:T(1,128)}, u32[]{:S(2)}) copy-start(s32[1,1,2048]{2,1,0:T(1,128)} %param.19) | copy-start | bytes 24580
  4.2 7.1 %collective-permute-start.3 = (bf16[80,640]{1,0:T(8,128)(2,1)S(1)}, bf16[80,640]{1,0:T(8,128)(2,1)S(1)}, u32[]{:S(2)}, u32[]{:S(2)}) collective-permute-start(bf16[80,640]{1,0:T(8,128)(2,1)S(1)} %get-tuple-element.41), channel_id=1, source_target_pairs={{1,8},{9,16},{17,24},{8,1},{16,9},{24,17},{3,10},{11,18},{19,26},{... | collective-permute-start | bytes 307208 | tf_op jit(solution)/shard_map/ppermute | solution.py:416
  5.0 10.6 %collective-permute-start.6 = (f32[40,256]{1,0:T(8,128)S(1)}, f32[40,256]{1,0:T(8,128)S(1)}, u32[]{:S(2)}, u32[]{:S(2)}) collective-permute-start(f32[40,256]{1,0:T(8,128)S(1)} %get-tuple-element.47.own_par), channel_id=1, source_target_pairs={{0,1},{1,0},{2,3},{3,2},{4,5},{5,4},{6,7},{7,6},{8,9},{9,8},{10,11... | collective-permute-start | bytes 122888 | tf_op jit(solution)/shard_map/ppermute | solution.py:413
  8.9 0.7 %copy-start.2 = (f32[128]{0:T(128)S(1)}, f32[128]{0:T(128)}, u32[]{:S(2)}) copy-start(f32[128]{0:T(128)} %param.16) | copy-start | bytes 1540
  11.7 6.1 %collective-permute-start.4 = (f32[80,128]{1,0:T(8,128)S(1)}, f32[80,128]{1,0:T(8,128)S(1)}, u32[]{:S(2)}, u32[]{:S(2)}) collective-permute-start(f32[80,128]{1,0:T(8,128)S(1)} %get-tuple-element.46.own), channel_id=1, source_target_pairs={{0,2},{2,4},{4,6},{6,0},{1,3},{3,5},{5,7},{7,1},{8,10},{10,12},{12... | collective-permute-start | bytes 122888 | tf_op jit(solution)/shard_map/ppermute | solution.py:392
  13.3 5.3 %collective-permute-start.5 = (f32[80,128]{1,0:T(8,128)S(1)}, f32[80,128]{1,0:T(8,128)S(1)}, u32[]{:S(2)}, u32[]{:S(2)}) collective-permute-start(f32[80,128]{1,0:T(8,128)S(1)} %get-tuple-element.46.own), channel_id=1, source_target_pairs={{0,6},{2,0},{4,2},{6,4},{1,7},{3,1},{5,3},{7,5},{8,14},{10,8},{12,... | collective-permute-start | bytes 122888 | tf_op jit(solution)/shard_map/ppermute | solution.py:392
  20.6 5.4 %collective-permute-start.7 = (bf16[96,384]{1,0:T(8,128)(2,1)S(1)}, bf16[96,384]{1,0:T(8,128)(2,1)S(1)}, u32[]{:S(2)}, u32[]{:S(2)}) collective-permute-start(bf16[96,384]{1,0:T(8,128)(2,1)S(1)} %get-tuple-element.52), channel_id=1, source_target_pairs={{1,8},{9,16},{17,24},{25,0},{8,1},{16,9},{24,17},{0,25},{3,10},{11... | collective-permute-start | bytes 221192 | tf_op jit(solution)/shard_map/ppermute | solution.py:416
  20.7 1.8 %collective-permute-start.8 = (bf16[80,384]{1,0:T(8,128)(2,1)S(1)}, bf16[80,384]{1,0:T(8,128)(2,1)S(1)}, u32[]{:S(2)}, u32[]{:S(2)}) collective-permute-start(bf16[80,384]{1,0:T(8,128)(2,1)S(1)} %get-tuple-element.53), channel_id=1, source_target_pairs={{0,1},{1,0},{2,3},{3,2},{4,5},{5,4},{6,7},{7,6},{8,9},{9,8},{10,11... | collective-permute-start | bytes 184328 | tf_op jit(solution)/shard_map/ppermute | solution.py:413
  26.2 4.7 %collective-permute-start.10 = (f32[80,128]{1,0:T(8,128)S(1)}, f32[80,128]{1,0:T(8,128)S(1)}, u32[]{:S(2)}, u32[]{:S(2)}) collective-permute-start(f32[80,128]{1,0:T(8,128)S(1)} %get-tuple-element.57.fown), channel_id=1, source_target_pairs={{0,6},{2,0},{4,2},{6,4},{1,7},{3,1},{5,3},{7,5},{8,14},{10,8},{12,... | collective-permute-start | bytes 122888 | tf_op jit(solution)/shard_map/ppermute | solution.py:392
  29.2 5.8 %collective-permute-start.9 = (f32[80,128]{1,0:T(8,128)S(1)}, f32[80,128]{1,0:T(8,128)S(1)}, u32[]{:S(2)}, u32[]{:S(2)}) collective-permute-start(f32[80,128]{1,0:T(8,128)S(1)} %get-tuple-element.57.fown), channel_id=1, source_target_pairs={{0,2},{2,4},{4,6},{6,0},{1,3},{3,5},{5,7},{7,1},{8,10},{10,12},{12... | collective-permute-start | bytes 122888 | tf_op jit(solution)/shard_map/ppermute | solution.py:392
  29.2 7.6 %collective-permute-start.12 = (f32[8,128]{1,0:T(8,128)S(1)}, f32[8,128]{1,0:T(8,128)S(1)}, u32[]{:S(2)}, u32[]{:S(2)}) collective-permute-start(f32[8,128]{1,0:T(8,128)S(1)} %get-tuple-element.61), channel_id=1, source_target_pairs={{0,4},{2,6},{4,0},{6,2},{1,5},{3,7},{5,1},{7,3},{8,12},{10,14},{12... | collective-permute-start | bytes 12296 | tf_op jit(solution)/shard_map/ppermute | solution.py:392
  36.7 6.4 %collective-permute-start.11 = (f32[320,128]{1,0:T(8,128)S(1)}, f32[320,128]{1,0:T(8,128)S(1)}, u32[]{:S(2)}, u32[]{:S(2)}) collective-permute-start(f32[320,128]{1,0:T(8,128)S(1)} %get-tuple-element.60), channel_id=1, source_target_pairs={{0,1},{1,0},{2,3},{3,2},{4,5},{5,4},{6,7},{7,6},{8,9},{9,8},{10,11... | collective-permute-start | bytes 491528 | tf_op jit(solution)/shard_map/ppermute | solution.py:413
  36.8 3.9 %collective-permute-start.13 = (f32[8,128]{1,0:T(8,128)S(1)}, f32[8,128]{1,0:T(8,128)S(1)}, u32[]{:S(2)}, u32[]{:S(2)}) collective-permute-start(f32[8,128]{1,0:T(8,128)S(1)} %slice_add_fusion), channel_id=1, source_target_pairs={{0,16},{8,24},{16,0},{24,8},{1,17},{9,25},{17,1},{25,9},{2,18},{10... | collective-permute-start | bytes 12296 | tf_op jit(solution)/shard_map/ppermute | solution.py:392
  40.7 1.2 %collective-permute-start.14 = (f32[8,128]{1,0:T(8,128)S(1)}, f32[8,128]{1,0:T(8,128)S(1)}, u32[]{:S(2)}, u32[]{:S(2)}) collective-permute-start(f32[8,128]{1,0:T(8,128)S(1)} %add.18), channel_id=1, source_target_pairs={{0,1},{1,0},{2,3},{3,2},{4,5},{5,4},{6,7},{7,6},{8,9},{9,8},{10,11... | collective-permute-start | bytes 12296 | tf_op jit(solution)/shard_map/ppermute | solution.py:413

commit v3 on v2

--- a/solution.py
+++ b/solution.py
@@ -6,6 +6,7 @@
 from jax.experimental import pallas as pl
 from jax.experimental.pallas import tpu as pltpu
 from jax.sharding import PartitionSpec as P
+
 
 B = 128
 HALO = 2
@@ -37,7 +38,19 @@
     return packed
 
 
-def side_block(west, own, east, f, rows):
+def by_side(one, two):
+    even = lax.axis_index("lon") % 2 == 0
+    one, two = one[...].astype(jnp.float32), two[...].astype(jnp.float32)
+    return jnp.where(even, one, two), jnp.where(even, two, one)
+
+
+def side_block(one, own, two, f, rows):
+    west, east = by_side(one, two)
+    own = own[...].astype(jnp.float32)
+    return side_block_of(west, own, east, f, rows)
+
+
+def side_block_of(west, own, east, f, rows):
     lane = lanes_of(own.shape[0])
     first = lane % GROUP < 2
     low, high = -f * rows * GROUP, B // 2 - f * rows * GROUP
@@ -79,6 +92,23 @@
     high = jnp.where(lane < levels - over, roll(rest, -over), roll(head, levels - over))
     high = jnp.where(lane < 2 * levels - over, high, 0.0)
     return jnp.concatenate([low, high], axis=1).astype(jnp.bfloat16)
+
+
+def as_column(row):
+    shape = (row.shape[1], row.shape[1])
+    square = lax.broadcasted_iota(jnp.int32, shape, 0) == lax.broadcasted_iota(jnp.int32, shape, 1)
+    return jnp.sum(jnp.where(square, row, 0.0), axis=1, keepdims=True)
+
+
+def pieces_of(x):
+    head = x.astype(jnp.bfloat16).astype(jnp.float32)
+    rest = (x - head).astype(jnp.bfloat16).astype(jnp.float32)
+    return head, rest, x - head - rest
+
+
+def carried_in(block, first):
+    lane = lanes_of(block.shape[0])
+    return jnp.sum(jnp.where((lane >= first) & (lane < first + 3), block, 0.0), axis=1, keepdims=True)
 
 
 def spread_rows(rows, core, sources, level, mains, inner, edge):
@@ -99,53 +129,56 @@
 
 
 def arrange_own(
-    rows, counts, mixing, diffusion, radiance, inc, u, v, main_i, main_u, main_v, inner, edge, par,
-    mixing_at, diffusion_at, radiance_at, inc_at, u_at, v_at, arrived,
+    rows, counts, lookup, weight, mixing, diffusion, radiance, inc, u, v,
+    main_i, main_u, main_v, inner, edge, par, places, weights,
+    count_at, lookup_at, weight_at, mixing_at, diffusion_at, radiance_at, inc_at, u_at, v_at, arrived,
 ):
     core = lax.axis_index("lev")
-    here = (inc_at, u_at, v_at, mixing_at, diffusion_at, radiance_at)
+    here = (count_at, lookup_at, weight_at, mixing_at, diffusion_at, radiance_at, inc_at, u_at, v_at)
     copies = [
         pltpu.make_async_copy(src, dst, arrived.at[i])
-        for i, (src, dst) in enumerate(zip((inc, u, v, mixing, diffusion, radiance), here))
+        for i, (src, dst) in enumerate(
+            zip((counts, lookup, weight, mixing, diffusion, radiance, inc, u, v), here)
+        )
     ]
     for copy in copies:
         copy.start()
-    for copy in copies[3:]:
+    for copy in copies[:6]:
         copy.wait()
+    slots, width = lookup.shape
+    columns = main_i.shape[1]
+    slot = lax.broadcasted_iota(jnp.int32, (slots, width), 0)
+    places[...] = jnp.where(slot < count_at[0, 0], lookup_at[...] - core * columns, -1)
     part, levels = mixing.shape
-    square = lax.broadcasted_iota(jnp.int32, (part, part), 0) == lax.broadcasted_iota(jnp.int32, (part, part), 1)
-    column = jnp.sum(jnp.where(square, diffusion_at[...], 0.0), axis=1, keepdims=True)
-    par[:, :B] = jnp.broadcast_to(column, (part, B))
+    weights[...] = jnp.broadcast_to(as_column(weight_at[...]), weights.shape)
+    par[:, :B] = jnp.broadcast_to(as_column(diffusion_at[...]), (part, B))
     par[:, :levels] = mixing_at[...]
     par[:, B:] = radiance_at[...].astype(jnp.float32)
-    for copy in copies[:3]:
+    for copy in copies[6:]:
         copy.wait()
     level = pl.multiple_of(core * part, 8)
     spread_rows(rows, core, (inc_at, u_at, v_at), level, (main_i, main_u, main_v), inner, edge)
 
 
 def arrange_other(
-    rows, counts, inc, u, v, main_i0, main_u0, main_v0, inner0, edge0, main_i, main_u, main_v, inner, edge
+    rows, inc, u, v, main_i0, main_u0, main_v0, inner0, edge0, main_i, main_u, main_v, inner, edge
 ):
     core = lax.axis_index("lev")
     level = pl.multiple_of((1 - core) * (inc.shape[0] // rows), 8)
     spread_rows(rows, core, (inc, u, v), level, (main_i, main_u, main_v), inner, edge)
 
 
-def by_column(counts, after, lookup, observed, weight, out, live, weights, hot, stacked):
-    core, count = lax.axis_index("lev"), counts[0, 0]
-    steps, slots, channels, width = observed.shape
+def one_hot(after, places, hot):
     columns = hot.shape[0]
-    diagonal = lax.broadcasted_iota(jnp.int32, (channels, channels), 0) == lax.broadcasted_iota(
-        jnp.int32, (channels, channels), 1
-    )
-    weights[...] = jnp.broadcast_to(
-        jnp.sum(jnp.where(diagonal, weight[...], 0.0), axis=1, keepdims=True), weights.shape
-    )
+    slots, width = places.shape
     index = lax.broadcasted_iota(jnp.int32, (columns, width), 0)
     for s in range(slots):
-        target = jnp.where(s < count, lookup[s : s + 1, :] - core * columns, -1)
-        hot[:, s * width : (s + 1) * width] = jnp.where(index == target, 1.0, 0.0).astype(jnp.bfloat16)
+        hot[:, s * width : (s + 1) * width] = jnp.where(index == places[s : s + 1, :], 1.0, 0.0).astype(jnp.bfloat16)
+
+
+def by_column(after, hot, observed, out, live, stacked):
+    steps, slots, channels, width = observed.shape
+    for s in range(slots):
         for t in range(steps):
             stacked[t * channels : (t + 1) * channels, s * width : (s + 1) * width] = observed[t, s]
     tail = stacked.shape[0] - steps * channels
@@ -170,7 +203,7 @@
     win[:, (count - HALO) * B : (count - HALO + width) * B] = jnp.where(low, near, far)
 
 
-def windows(counts, main_i, main_u, main_v, inner, edge, after, win_i, win_u, win_v, packed):
+def windows(main_i, main_u, main_v, inner, edge, after, win_i, win_u, win_v, packed):
     low = lax.axis_index("lev") == 0
     count = win_i.shape[1] // B
     k = 0
@@ -179,7 +212,9 @@
         span = slice(k * B, (k + width) * B)
         fill_halo(win, inner[:, span], edge[:, span].astype(jnp.float32), low, width)
         k += width
-    packed[...] = pack_edges([functools.partial(block, win) for win in (win_i, win_u, win_v)], count - 2)
+    packed[...] = pack_edges(
+        [functools.partial(block, win) for win in (win_i, win_u, win_v)], count - 2
+    ).astype(packed.dtype)
 
 
 def smooth(x, north, south, east, west, diff, u, v):
@@ -192,7 +227,7 @@
 
 
 def forward(
-    counts, win_i, win_u, win_v, west, own, east, own_par, other_par, observed, live, weights,
+    win_i, win_u, win_v, west, own, east, own_par, other_par, observed, live, weights,
     f1, f2, edge, inner, cost, par, stack, plain, state,
 ):
     core, is_first, is_final = flags()
@@ -209,7 +244,7 @@
     channels = radiance.shape[1]
     scale = weights[:, :1]
     clear_rest(stack, levels)
-    sides = [side_block(west[...], own[...], east[...], f, rows) for f in range(3)]
+    sides = [side_block(west, own, east, f, rows) for f in range(3)]
     for q in range(rows):
         p = q + 1
         x = block(win_i, p)
@@ -262,18 +297,15 @@
         inner[:, k * B : (k + width) * B] = jnp.where(low, tail, head).astype(jnp.bfloat16)
         k += width
     tail = edge.shape[0] - levels
-    head = total.astype(jnp.bfloat16).astype(jnp.float32)
-    rest = (total - head).astype(jnp.bfloat16).astype(jnp.float32)
-    pieces = (head, rest, total - head - rest)
     lane = lanes_of(tail)
     carried = jnp.zeros((tail, B), jnp.float32)
-    for i, piece in enumerate(pieces):
+    for i, piece in enumerate(pieces_of(total)):
         carried = jnp.where(lane == i, piece, carried)
     edge[levels:, :B] = carried.astype(jnp.bfloat16)
     edge[levels:, B:] = jnp.zeros((tail, edge.shape[1] - B), jnp.bfloat16)
 
 
-def forcing_windows(counts, f1, f2, edge, inner, cost, win_1, win_2, packed, total):
+def forcing_windows(f1, f2, edge, inner, cost, win_1, win_2, packed, total):
     core, is_first, is_final = flags()
     low = core == 0
     inside = is_first & is_final
@@ -287,15 +319,24 @@
         fill_halo(win, inner[:, span].astype(jnp.float32), far, low, width)
         k += width
     both = pack_edges([functools.partial(block, win) for win in (win_2, win_1)], count - 2)
-    carried = edge[levels:, :B].astype(jnp.float32)
-    carried = jnp.sum(jnp.where(lanes_of(carried.shape[0]) < 3, carried, 0.0), axis=1, keepdims=True)
-    here = cost[...] + carried[: cost.shape[0]]
+    here = cost[...] + carried_in(edge[levels:, :B].astype(jnp.float32), 0)[: cost.shape[0]]
     total[...] = here
-    packed[...] = jnp.where(lanes_of(both.shape[0]) == B - 1, here[0:1, :], both)
+    lane = lanes_of(both.shape[0])
+    for i, piece in enumerate(pieces_of(here[0:1, :])):
+        both = jnp.where(lane == B - 3 + i, piece, both)
+    packed[...] = both.astype(packed.dtype)
+
+
+def add_sides(two_sided, cost, cost_2, west, east, total):
+    west, east = by_side(west, east)
+    here = cost[...] + carried_in(west, B - 3)[: cost.shape[0]]
+    if two_sided:
+        here = here + cost_2[...] + carried_in(east, B - 3)[: cost.shape[0]]
+    total[...] = here
 
 
 def backward(
-    counts, win_1, win_2, fwest, fown, feast, win_i, win_u, win_v, west, own, east, par,
+    win_1, win_2, fwest, fown, feast, win_i, win_u, win_v, west, own, east, par, after,
     kept, sent, stack, coupled, square,
 ):
     core, is_first, is_final = flags()
@@ -309,8 +350,8 @@
     square[:levels, :] = jnp.where(lanes_of(levels) < levels, par[:, :B], 0.0)
     coupling = split_matrix(jnp.transpose(square[...])[:levels], levels)
     clear_rest(stack, levels)
-    f_sides = [side_block(fwest[...], fown[...], feast[...], f, rows) for f in range(2)]
-    sides = [side_block(west[...], own[...], east[...], f, rows) for f in range(3)]
+    f_sides = [side_block(fwest, fown, feast, f, rows) for f in range(2)]
+    sides = [side_block(west, own, east, f, rows) for f in range(3)]
     for p in range(count):
         x = block(win_2, p)
         coupled[:, p * B : (p + 1) * B] = x
@@ -362,29 +403,52 @@
         sent[pl.ds(j, part, stride=half), :] = jnp.where(low, value[part:], value[:part])
 
 
-def call(kernel, outs, scratch=(), name=None, aliases=None, in_hbm=False, flops=10**9):
+def finish(cells, kept, got, cost, cost_2, gradient, value, done):
+    core = lax.axis_index("lev")
+    half = kept.shape[1]
+    copies = [
+        pltpu.make_async_copy(src, gradient.at[:, pl.ds(pl.multiple_of(at * half, 8), half), :], done.at[i])
+        for i, (src, at) in enumerate(((kept, core), (got, 1 - core)))
+    ]
+    for copy in copies:
+        copy.start()
+    value[0, 0] = jnp.max(cost[0:1, :] + cost_2[0:1, :]) / cells
+    for copy in copies:
+        copy.wait()
+
+
+def call(kernel, outs, scratch=(), aliases=None, from_hbm=False, to_hbm=False, flops=10**9):
     vmem = pl.BlockSpec(memory_space=pltpu.VMEM)
-    source = pl.BlockSpec(memory_space=pltpu.HBM) if in_hbm else vmem
-
-    def run(counts, *operands):
-        if in_hbm:
-            operands = [pltpu.with_memory_space_constraint(x, pltpu.HBM) for x in operands]
+    hbm = pl.BlockSpec(memory_space=pltpu.HBM)
+
+    def run(*operands):
+        if from_hbm:
+            operands = [x if x.size == 1 else pltpu.with_memory_space_constraint(x, pltpu.HBM) for x in operands]
         return pl.pallas_call(
             kernel,
             out_shape=[jax.ShapeDtypeStruct(shape, dtype) for shape, dtype in outs],
-            in_specs=[pl.BlockSpec(memory_space=pltpu.SMEM)] + [source] * len(operands),
-            out_specs=[vmem] * len(outs),
+            in_specs=[hbm if from_hbm else vmem] * len(operands),
+            out_specs=[pl.BlockSpec(memory_space=pl.ANY), pl.BlockSpec(memory_space=pltpu.SMEM)]
+            if to_hbm
+            else [vmem] * len(outs),
             scratch_shapes=[
-                pltpu.SemaphoreType.DMA(shape) if dtype is None else pltpu.VMEM(shape, dtype)
-                for shape, dtype in scratch
+                shape if dtype is None else pltpu.VMEM(shape, dtype) for shape, dtype in scratch
             ],
             input_output_aliases=aliases or {},
-            name=name,
             cost_estimate=pl.CostEstimate(flops=flops, bytes_accessed=0, transcendentals=0),
             compiler_params=pltpu.CompilerParams(vmem_limit_bytes=24 * 2**20),
-        )(counts, *operands)
+        )(*operands)
 
     return run
+
+
+def beside(x):
+    count = lax.axis_size("lon")
+    got = []
+    for first in (1, 0):
+        pairs = [((2 * i + first) % count, (2 * i + first + 1) % count) for i in range(count // 2)]
+        got.append(lax.ppermute(x, "lon", pairs + [(b, a) for a, b in pairs] if count > 2 else [(0, 1), (1, 0)]))
+    return got
 
 
 def ring(x, axis, shift):
@@ -421,77 +485,72 @@
     main = ((levels, columns), f32)
     groups = [main] * 3 + [((levels, halo * B), f32), ((levels, halo * B), bf16)]
     win = ((levels, count * B), f32)
-    packed = ((levels, B), f32)
+    packed = ((levels, B), bf16)
     field = ((part * rows, B), f32)
-    *sorted_rows, own_par = call(
+    scalar = ((8, B), f32)
+    waits = pltpu.SemaphoreType.DMA
+    *sorted_rows, own_par, places, weights = call(
         functools.partial(arrange_own, rows),
-        groups + [((part, 2 * B), f32)],
-        [((part, levels), f32), ((1, part), f32), ((part, channels), bf16)] + [field] * 3 + [((6,), None)],
-        name="arrange_own",
-        in_hbm=True,
-    )(counts, mixing, diffusion.reshape(1, -1), jacobian.T, *fields)
+        groups + [((part, 2 * B), f32), ((slots, B), jnp.int32), ((channels, B), f32)],
+        [(pltpu.SMEM((1, 1), jnp.int32), None), ((slots, B), jnp.int32), ((1, channels), f32)]
+        + [((part, levels), f32), ((1, part), f32), ((part, channels), bf16)]
+        + [field] * 3
+        + [(waits((9,)), None)],
+        from_hbm=True,
+    )(
+        counts, column_lookup.reshape(slots, B), obs_weight.reshape(1, -1), mixing, diffusion.reshape(1, -1),
+        jacobian.T, *fields,
+    )
     *mains, inner, edge = call(
-        functools.partial(arrange_other, rows), groups, name="arrange_other",
-        aliases={4 + i: i for i in range(5)},
-    )(counts, *others, *sorted_rows)
+        functools.partial(arrange_other, rows), groups,
+        aliases={3 + i: i for i in range(5)},
+    )(*others, *sorted_rows)
     edge = across(edge, inside)
     other_par = swap(own_par)
-    observed, live, weights = call(
+    (hot,) = call(one_hot, [((columns, slots * B), bf16)])(inner, places)
+    win_i, win_u, win_v, own = call(windows, [win] * 3 + [packed])(*mains, inner, edge, hot)
+    observed, live = call(
         by_column,
-        [((steps * channels, columns), bf16), ((8, columns), f32), ((channels, B), f32)],
-        [((columns, slots * B), bf16), ((steps * channels + 16, slots * B), bf16)],
-        name="by_column",
-    )(
-        counts, inner, column_lookup.reshape(slots, B), innovation.reshape(steps, slots, channels, B),
-        obs_weight.reshape(1, -1),
-    )
-    win_i, win_u, win_v, own = call(windows, [win] * 3 + [packed], name="windows")(
-        counts, *mains, inner, edge, live
-    )
-    west, east = ring(own, "lon", 1), ring(own, "lon", -1)
+        [((steps * channels, columns), bf16), ((8, columns), f32)],
+        [((steps * channels + 16, slots * B), bf16)],
+    )(own, hot, innovation.reshape(steps, slots, channels, B))
+    west, east = beside(own)
     forcing = ((levels, columns), bf16)
     depth = max(-(-3 * levels // 16) * 16, 2 * B)
     f1, f2, f_edge, f_inner, cost, par = call(
         forward,
         [forcing] * 2
         + [((levels + 16, (HALO + 1) * B), bf16), ((levels, (HALO + 1) * B), bf16)]
-        + [((8, B), f32), ((levels, 2 * B), f32)],
+        + [scalar, ((levels, 2 * B), f32)],
         [((depth, (count - 1) * B), bf16), ((levels, (count - 1) * B), f32), ((levels, (count - 1) * B), f32)],
-        name="forward",
-    )(counts, win_i, win_u, win_v, west, own, east, own_par, other_par, observed, live, weights)
+    )(win_i, win_u, win_v, west, own, east, own_par, other_par, observed, live, weights)
     f_edge, f_inner = across(f_edge, pairs), swap(f_inner)
-    win_1, win_2, f_own, total = call(
-        forcing_windows, [win] * 2 + [packed, ((8, B), f32)], name="forcing"
-    )(counts, f1, f2, f_edge, f_inner, cost)
-    f_west, f_east = ring(f_own, "lon", 1), ring(f_own, "lon", -1)
-    if along == 4:
-        total = total + ring(total, "lon", 2) + f_west[:8] + f_east[:8]
-    else:
-        total = total + f_west[:8]
-        shift = 2
-        while shift < along:
-            total = total + ring(total, "lon", shift)
-            shift *= 2
-    shift = 2
-    while shift < tiles:
-        total = total + ring(total, "lat", shift)
-        shift *= 2
-    total = total + swap(total)
+    win_1, win_2, f_own, total = call(forcing_windows, [win] * 2 + [packed, scalar])(f1, f2, f_edge, f_inner, cost)
+    f_west, f_east = beside(f_own)
+    few_points = along == 4
+    total_2 = ring(total, "lon", 2) if few_points else total
+    (total,) = call(functools.partial(add_sides, few_points), [scalar], flops=10**7)(total, total_2, f_west, f_east)
+    more = ring(total, "lat", 2) if tiles > 2 else None
     kept, sent = call(
         backward,
         [((part * half, B), f32)] * 2,
         [((depth, (count + 1) * B), bf16), ((levels, (count + 1) * B), f32), ((B, B), f32)],
-        name="backward",
-    )(counts, win_1, win_2, f_west, f_own, f_east, win_i, win_u, win_v, west, own, east, par)
-    got = swap(sent)
-    kept, got = kept.reshape(part, half, B), got.reshape(part, half, B)
-    gradient = jnp.where(
-        lax.axis_index("lev") == 0,
-        jnp.concatenate([kept, got], axis=1),
-        jnp.concatenate([got, kept], axis=1),
-    )
+    )(win_1, win_2, f_west, f_own, f_east, win_i, win_u, win_v, west, own, east, par, total)
+    if more is not None:
+        total = total + more
+    for axis, size, few in (("lat", tiles, False), ("lon", along, few_points)):
+        shift = 4 if axis == "lat" else 2
+        while shift < size and not few:
+            total = total + ring(total, axis, shift)
+            shift *= 2
     cells = increment.size * tiles * along * lax.axis_size("lev")
-    return gradient, total[0, B - 1] / cells
+    gradient, value = call(
+        functools.partial(finish, float(cells)),
+        [(increment.shape, f32), ((1, 1), f32)],
+        [(waits((2,)), None)],
+        to_hbm=True,
+    )(kept.reshape(part, half, B), swap(sent).reshape(part, half, B), total, swap(total))
+    return gradient, value.reshape(())
 
 
 def solution(mesh):
@@ -510,4 +569,5 @@
         P("lat", "lon", None),
     )
     out_specs = (P("lev", "lat", "lon"), P())
+
     return jax.shard_map(body, mesh=mesh, in_specs=in_specs, out_specs=out_specs, check_vma=False)

time: 45.3 us -> 41.6 us (0.918)
  waiting for transfers between devices: 15.3 us -> 10 us
  starting transfers between devices: 16.7 us -> 20.1 us
  Pallas kernels: 7.74 us -> 9.9 us
  between operations: 3.22 us -> 1.41 us
  local copies, waits for them, and re-layouts: 1.25 us -> 0.01 us
  other arithmetic: 0.76 us -> 0.01 us
    ppermute x0 -> x4, starting transfers between devices: none -> 5.62 us  [beside(): lax.ppermute(x, 'lon', pairs + [(b, a) for a, b in pairs] if count > 2 el...]
    ppermute x6 -> x2, waiting for transfers between devices: 9.77 us -> 4.49 us  [ring(): lax.ppermute(x, axis, [(i, (i + shift) % count) for i in range(count)])]
    ppermute x6 -> x2, starting transfers between devices: 9.81 us -> 5.91 us  [ring(): lax.ppermute(x, axis, [(i, (i + shift) % count) for i in range(count)])]
    ppermute x2, waiting for transfers between devices: 3.5 us -> 1.1 us  [across(): return lax.ppermute(x, ('lat', 'lev'), which)]
    ppermute x0 -> x4, waiting for transfers between devices: none -> 2.38 us  [beside(): lax.ppermute(x, 'lon', pairs + [(b, a) for a, b in pairs] if count > 2 el...]
    pallas_call x7 -> x10, Pallas kernels: 7.74 us -> 9.9 us  [run(): pl.pallas_call(kernel, out_shape=[jax.ShapeDtypeStruct(shape, dtype) for...]
    ppermute x7, starting transfers between devices: 6.04 us -> 7.71 us  [swap(): return lax.ppermute(x, 'lev', [(0, 1), (1, 0)])]
    select_n x1 -> x0, other arithmetic: 0.75 us -> none  [body(): jnp.where(lax.axis_index('lev') == 0, jnp.concatenate([kept, got], axis=1...]
  transfers between devices with their start and end apart: 15 -> 15, of which waited for: 8 -> 7; matrix products, arithmetic and copies ran while one was open for 1% -> 0% of each run, Pallas kernels for 12% -> 11%
where the time goes in v3:
time: 41.6 us; the launch traced here: 41.4 us
  starting transfers between devices  20.1 us (48%)
  waiting for transfers between devices  10 us (24%)
  Pallas kernels  9.9 us (24%)
  between operations  1.41 us (3%)
    pallas_call x10, Pallas kernels, run(): pl.pallas_call(kernel, out_shape=[jax.ShapeDtypeStruct(shape, dtype) for...  9.9 us
    ppermute x7, starting transfers between devices, swap(): return lax.ppermute(x, 'lev', [(0, 1), (1, 0)])  7.71 us
    ppermute x2, starting transfers between devices, ring(): lax.ppermute(x, axis, [(i, (i + shift) % count) for i in range(count)])  5.91 us
    ppermute x4, starting transfers between devices, beside(): lax.ppermute(x, 'lon', pairs + [(b, a) for a, b in pairs] if count > 2 el...  5.62 us
    ppermute x2, waiting for transfers between devices, ring(): lax.ppermute(x, axis, [(i, (i + shift) % count) for i in range(count)])  4.49 us
    ppermute x4, waiting for transfers between devices, beside(): lax.ppermute(x, 'lon', pairs + [(b, a) for a, b in pairs] if count > 2 el...  2.38 us
    ppermute x7, waiting for transfers between devices, swap(): return lax.ppermute(x, 'lev', [(0, 1), (1, 0)])  2.07 us
    ppermute x2, waiting for transfers between devices, across(): return lax.ppermute(x, ('lat', 'lev'), which)  1.1 us
  transfers between devices with their start and end apart: 15, of which 7 were waited for; matrix products, arithmetic and copies ran while one was open for 0% of the time, Pallas kernels for 11%

profile of v3, /device:TPU:0, one launch (start us, length us, event | category | flops | bytes accessed | tf_op | source)
XLA Modules:
  0.0 41.4 jit_solution(1754628341027831316)
XLA Ops:
  0.6 0.6 %collective-permute-start = (f32[640,128]{1,0:T(8,128)}, f32[640,128]{1,0:T(8,128)S(1)}, u32[]{:S(2)}, u32[]{:S(2)}) collective-permute-start(f32[640,128]{1,0:T(8,128)} %bitcast.14), channel_id=1, source_target_pairs={{0,1},{1,0},{2,3},{3,2},{4,5},{5,4},{6,7},{7,6},{8,9},{9,8},{10,11... | collective-permute-start | bytes 983048 | tf_op jit(solution)/shard_map/ppermute | solution.py:477
  1.3 0.4 %collective-permute-start.2 = (f32[640,128]{1,0:T(8,128)}, f32[640,128]{1,0:T(8,128)S(1)}, u32[]{:S(2)}, u32[]{:S(2)}) collective-permute-start(f32[640,128]{1,0:T(8,128)} %bitcast.18), channel_id=1, source_target_pairs={{0,1},{1,0},{2,3},{3,2},{4,5},{5,4},{6,7},{7,6},{8,9},{9,8},{10,11... | collective-permute-start | bytes 983048 | tf_op jit(solution)/shard_map/ppermute | solution.py:477
  2.4 1.6 %shard_map.113 = (f32[80,1024]{1,0:T(8,128)S(1)}, f32[80,1024]{1,0:T(8,128)S(1)}, f32[80,1024]{1,0:T(8,128)S(1)}, f32[80,640]{1,0:T(8,128)S(1)}, bf16[80,640]{1,...) custom-call(s32[1,1]{1,0:T(1,128)S(6)} %copy.22.counts, ...), custom_call_target="tpu_custom_call" | custom-call | flops 1000000000 | tf_op jit(solution)/shard_map/pallas_call | solution.py:427
  4.3 0.7 %collective-permute-start.3 = (bf16[80,640]{1,0:T(8,128)(2,1)S(1)}, bf16[80,640]{1,0:T(8,128)(2,1)S(1)}, u32[]{:S(2)}, u32[]{:S(2)}) collective-permute-start(bf16[80,640]{1,0:T(8,128)(2,1)S(1)} %get-tuple-element.44), channel_id=1, source_target_pairs={{1,8},{9,16},{17,24},{8,1},{16,9},{24,17},{3,10},{11,18},{19,26},{... | collective-permute-start | bytes 307208 | tf_op jit(solution)/shard_map/ppermute | solution.py:480
  4.9 4.0 %collective-permute-start.6 = (f32[40,256]{1,0:T(8,128)S(1)}, f32[40,256]{1,0:T(8,128)S(1)}, u32[]{:S(2)}, u32[]{:S(2)}) collective-permute-start(f32[40,256]{1,0:T(8,128)S(1)} %get-tuple-element.50.own_par), channel_id=1, source_target_pairs={{0,1},{1,0},{2,3},{3,2},{4,5},{5,4},{6,7},{7,6},{8,9},{9,8},{10,11... | collective-permute-start | bytes 122888 | tf_op jit(solution)/shard_map/ppermute | solution.py:477
  8.9 1.3 %shard_map.115.after.hot = bf16[1024,2048]{1,0:T(8,128)(2,1)S(1)} custom-call(f32[80,640]{1,0:T(8,128)S(1)} %get-tuple-element.43.after.inner, s32[16,128]{1,0:T(8,128)S(1)} %get-tuple-element.45.places), custom_call_target="tpu_custom_call" | custom-call | flops 1000000000 | tf_op jit(solution)/shard_map/pallas_call | solution.py:427
  10.2 0.3 shard_map.116
  10.5 3.7 %collective-permute-start.4 = (bf16[80,128]{1,0:T(8,128)(2,1)S(1)}, bf16[80,128]{1,0:T(8,128)(2,1)S(1)}, u32[]{:S(2)}, u32[]{:S(2)}) collective-permute-start(bf16[80,128]{1,0:T(8,128)(2,1)S(1)} %get-tuple-element.49.after.own), channel_id=1, source_target_pairs={{2,4},{6,0},{4,2},{0,6},{3,5},{7,1},{5,3},{1,7},{10,12},{14,8},{12... | collective-permute-start | bytes 61448 | tf_op jit(solution)/shard_map/ppermute | solution.py:450
  14.2 1.4 %shard_map.117 = (bf16[256,1024]{1,0:T(8,128)(2,1)S(1)}, f32[8,1024]{1,0:T(8,128)S(1)}) custom-call(bf16[80,128]{1,0:T(8,128)(2,1)S(1)} %get-tuple-element.49.after.own, bf16[1024,2048]{1,0:T(8,128)(2,1)S(1)} %shard_map.115.after.hot, bf16[2,16,128,128]{3,2,1,0:T(8,128)(2,1)S(1)} %bitcast.11), custom_call_target="tpu_custom_call" | custom-call | flops 1000000000 | tf_op jit(solution)/shard_map/pallas_call | solution.py:427
  15.6 0.6 %collective-permute-done.4.west = bf16[80,128]{1,0:T(8,128)(2,1)S(1)} collective-permute-done((bf16[80,128]{1,0:T(8,128)(2,1)S(1)}, bf16[80,128]{1,0:T(8,128)(2,1)S(1)}, u32[]{:S(2)}, u32[]{:S(2)}) %collective-permute-start.4) | collective-permute-done | bytes 20512 | tf_op jit(solution)/shard_map/ppermute | solution.py:450
  16.2 1.8 %collective-permute-done.5.east = bf16[80,128]{1,0:T(8,128)(2,1)S(1)} collective-permute-done((bf16[80,128]{1,0:T(8,128)(2,1)S(1)}, bf16[80,128]{1,0:T(8,128)(2,1)S(1)}, u32[]{:S(2)}, u32[]{:S(2)}) %collective-permute-start.5) | collective-permute-done | bytes 20512 | tf_op jit(solution)/shard_map/ppermute | solution.py:450
  18.0 1.9 %shard_map.118 = (bf16[80,1024]{1,0:T(8,128)(2,1)S(1)}, bf16[80,1024]{1,0:T(8,128)(2,1)S(1)}, bf16[96,384]{1,0:T(8,128)(2,1)S(1)}, bf16[80,384]{1,0:T(8,128)(2,1...) custom-call(f32[80,1536]{1,0:T(8,128)S(1)} %get-tuple-element.46.win_i, f32[80,1536]{1,0:T(8,128)S(1)} %get-tuple-element.47.win_u, ...), custom_call_target="tpu_custom_call" | custom-call | flops 1000000000 | tf_op jit(solution)/shard_map/pallas_call | solution.py:427
  20.0 2.6 %collective-permute-start.8 = (bf16[80,384]{1,0:T(8,128)(2,1)S(1)}, bf16[80,384]{1,0:T(8,128)(2,1)S(1)}, u32[]{:S(2)}, u32[]{:S(2)}) collective-permute-start(bf16[80,384]{1,0:T(8,128)(2,1)S(1)} %get-tuple-element.57), channel_id=1, source_target_pairs={{0,1},{1,0},{2,3},{3,2},{4,5},{5,4},{6,7},{7,6},{8,9},{9,8},{10,11... | collective-permute-start | bytes 184328 | tf_op jit(solution)/shard_map/ppermute | solution.py:477
  22.6 0.9 %collective-permute-done.8.inner = bf16[80,384]{1,0:T(8,128)(2,1)S(1)} collective-permute-done((bf16[80,384]{1,0:T(8,128)(2,1)S(1)}, bf16[80,384]{1,0:T(8,128)(2,1)S(1)}, u32[]{:S(2)}, u32[]{:S(2)}) %collective-permute-start.8) | collective-permute-done | bytes 61472 | tf_op jit(solution)/shard_map/ppermute | solution.py:477
  23.5 1.1 %collective-permute-done.7.edge = bf16[96,384]{1,0:T(8,128)(2,1)S(1)} collective-permute-done((bf16[96,384]{1,0:T(8,128)(2,1)S(1)}, bf16[96,384]{1,0:T(8,128)(2,1)S(1)}, u32[]{:S(2)}, u32[]{:S(2)}) %collective-permute-start.7) | collective-permute-done | bytes 73760 | tf_op jit(solution)/shard_map/ppermute | solution.py:480
  24.8 0.3 collective-permute-start.10
  25.1 1.7 %collective-permute-start.9 = (bf16[80,128]{1,0:T(8,128)(2,1)S(1)}, bf16[80,128]{1,0:T(8,128)(2,1)S(1)}, u32[]{:S(2)}, u32[]{:S(2)}) collective-permute-start(bf16[80,128]{1,0:T(8,128)(2,1)S(1)} %get-tuple-element.61.fown), channel_id=1, source_target_pairs={{2,4},{6,0},{4,2},{0,6},{3,5},{7,1},{5,3},{1,7},{10,12},{14,8},{12... | collective-permute-start | bytes 61448 | tf_op jit(solution)/shard_map/ppermute | solution.py:450
  26.8 1.6 %collective-permute-start.11 = (f32[8,128]{1,0:T(8,128)S(1)}, f32[8,128]{1,0:T(8,128)S(1)}, u32[]{:S(2)}, u32[]{:S(2)}) collective-permute-start(f32[8,128]{1,0:T(8,128)S(1)} %get-tuple-element.63.cost), channel_id=1, source_target_pairs={{0,4},{2,6},{4,0},{6,2},{1,5},{3,7},{5,1},{7,3},{8,12},{10,14},{12... | collective-permute-start | bytes 12296 | tf_op jit(solution)/shard_map/ppermute | solution.py:456
  28.4 2.9 %collective-permute-done.11.cost_2 = f32[8,128]{1,0:T(8,128)S(1)} collective-permute-done((f32[8,128]{1,0:T(8,128)S(1)}, f32[8,128]{1,0:T(8,128)S(1)}, u32[]{:S(2)}, u32[]{:S(2)}) %collective-permute-start.11) | collective-permute-done | bytes 4128 | tf_op jit(solution)/shard_map/ppermute | solution.py:456
  31.4 1.6 %shard_map.121 = (f32[320,128]{1,0:T(8,128)S(1)}, f32[320,128]{1,0:T(8,128)S(1)}) custom-call(f32[80,1536]{1,0:T(8,128)S(1)} %get-tuple-element.59.win_1, f32[80,1536]{1,0:T(8,128)S(1)} %get-tuple-element.60.win_2, bf16[80,128]{1,0:T(8,128)(2,1)S(1)} %collective-permute-done.9.west.fwest, bf16[80,128]{1,0:T(8,128)(2,1)S(1)} %get-tuple-element.61.fown, ...), custom_call_target="tpu_custom_call" | custom-call | flops 1000000000 | tf_op jit(solution)/shard_map/pallas_call | solution.py:427
  33.1 4.3 %collective-permute-start.13 = (f32[8,128]{1,0:T(8,128)S(1)}, f32[8,128]{1,0:T(8,128)S(1)}, u32[]{:S(2)}, u32[]{:S(2)}) collective-permute-start(f32[8,128]{1,0:T(8,128)S(1)} %shard_map.120.after), channel_id=1, source_target_pairs={{0,16},{8,24},{16,0},{24,8},{1,17},{9,25},{17,1},{25,9},{2,18},{10... | collective-permute-start | bytes 12296 | tf_op jit(solution)/shard_map/ppermute | solution.py:456
  37.4 1.6 %collective-permute-done.13 = f32[8,128]{1,0:T(8,128)S(1)} collective-permute-done((f32[8,128]{1,0:T(8,128)S(1)}, f32[8,128]{1,0:T(8,128)S(1)}, u32[]{:S(2)}, u32[]{:S(2)}) %collective-permute-start.13) | collective-permute-done | bytes 4128 | tf_op jit(solution)/shard_map/ppermute | solution.py:456
  39.0 1.2 %collective-permute-done.14.cost_2 = f32[8,128]{1,0:T(8,128)S(1)} collective-permute-done((f32[8,128]{1,0:T(8,128)S(1)}, f32[8,128]{1,0:T(8,128)S(1)}, u32[]{:S(2)}, u32[]{:S(2)}) %collective-permute-start.14) | collective-permute-done | bytes 4128 | tf_op jit(solution)/shard_map/ppermute | solution.py:477
  40.2 1.3 %shard_map.122 = (f32[40,16,128]{2,1,0:T(8,128)}, f32[1,1]{1,0:T(1,128)}) custom-call(f32[40,8,128]{2,1,0:T(8,128)S(1)} %bitcast.13, f32[40,8,128]{2,1,0:T(8,128)S(1)} %bitcast.12, f32[8,128]{1,0:T(8,128)S(1)} %add.3.cost, f32[8,128]{1,0:T(8,128)S(1)} %collective-permute-done.14.cost_2), custom_call_target="tpu_custom_call" | custom-call | flops 1000000000 | tf_op jit(solution)/shard_map/pallas_call | solution.py:427
  (19 shorter events, 0.9 us)
Async XLA Ops:
  0.6 3.3 %collective-permute-start = (f32[640,128]{1,0:T(8,128)}, f32[640,128]{1,0:T(8,128)S(1)}, u32[]{:S(2)}, u32[]{:S(2)}) collective-permute-start(f32[640,128]{1,0:T(8,128)} %bitcast.14), channel_id=1, source_target_pairs={{0,1},{1,0},{2,3},{3,2},{4,5},{5,4},{6,7},{7,6},{8,9},{9,8},{10,11... | collective-permute-start | bytes 983048 | tf_op jit(solution)/shard_map/ppermute | solution.py:477
  1.2 2.8 %collective-permute-start.1 = (f32[640,128]{1,0:T(8,128)}, f32[640,128]{1,0:T(8,128)S(1)}, u32[]{:S(2)}, u32[]{:S(2)}) collective-permute-start(f32[640,128]{1,0:T(8,128)} %bitcast.16), channel_id=1, source_target_pairs={{0,1},{1,0},{2,3},{3,2},{4,5},{5,4},{6,7},{7,6},{8,9},{9,8},{10,11... | collective-permute-start | bytes 983048 | tf_op jit(solution)/shard_map/ppermute | solution.py:477
  1.3 2.7 %collective-permute-start.2 = (f32[640,128]{1,0:T(8,128)}, f32[640,128]{1,0:T(8,128)S(1)}, u32[]{:S(2)}, u32[]{:S(2)}) collective-permute-start(f32[640,128]{1,0:T(8,128)} %bitcast.18), channel_id=1, source_target_pairs={{0,1},{1,0},{2,3},{3,2},{4,5},{5,4},{6,7},{7,6},{8,9},{9,8},{10,11... | collective-permute-start | bytes 983048 | tf_op jit(solution)/shard_map/ppermute | solution.py:477
  4.3 6.0 %collective-permute-start.3 = (bf16[80,640]{1,0:T(8,128)(2,1)S(1)}, bf16[80,640]{1,0:T(8,128)(2,1)S(1)}, u32[]{:S(2)}, u32[]{:S(2)}) collective-permute-start(bf16[80,640]{1,0:T(8,128)(2,1)S(1)} %get-tuple-element.44), channel_id=1, source_target_pairs={{1,8},{9,16},{17,24},{8,1},{16,9},{24,17},{3,10},{11,18},{19,26},{... | collective-permute-start | bytes 307208 | tf_op jit(solution)/shard_map/ppermute | solution.py:480
  4.9 10.7 %collective-permute-start.6 = (f32[40,256]{1,0:T(8,128)S(1)}, f32[40,256]{1,0:T(8,128)S(1)}, u32[]{:S(2)}, u32[]{:S(2)}) collective-permute-start(f32[40,256]{1,0:T(8,128)S(1)} %get-tuple-element.50.own_par), channel_id=1, source_target_pairs={{0,1},{1,0},{2,3},{3,2},{4,5},{5,4},{6,7},{7,6},{8,9},{9,8},{10,11... | collective-permute-start | bytes 122888 | tf_op jit(solution)/shard_map/ppermute | solution.py:477
  8.9 5.3 %copy-start = (bf16[2,1,1,16,128,128]{5,4,3,2,1,0:T(8,128)(2,1)S(1)}, bf16[2,1,1,16,128,128]{5,4,3,2,1,0:T(8,128)(2,1)}, u32[]{:S(2)}) copy-start(bf16[2,1,1,16,128,128]{5,4,3,2,1,0:T(8,128)(2,1)} %param.17) | copy-start | bytes 3145732
  10.5 5.6 %collective-permute-start.4 = (bf16[80,128]{1,0:T(8,128)(2,1)S(1)}, bf16[80,128]{1,0:T(8,128)(2,1)S(1)}, u32[]{:S(2)}, u32[]{:S(2)}) collective-permute-start(bf16[80,128]{1,0:T(8,128)(2,1)S(1)} %get-tuple-element.49.after.own), channel_id=1, source_target_pairs={{2,4},{6,0},{4,2},{0,6},{3,5},{7,1},{5,3},{1,7},{10,12},{14,8},{12... | collective-permute-start | bytes 61448 | tf_op jit(solution)/shard_map/ppermute | solution.py:450
  14.2 3.8 %collective-permute-start.5 = (bf16[80,128]{1,0:T(8,128)(2,1)S(1)}, bf16[80,128]{1,0:T(8,128)(2,1)S(1)}, u32[]{:S(2)}, u32[]{:S(2)}) collective-permute-start(bf16[80,128]{1,0:T(8,128)(2,1)S(1)} %get-tuple-element.49.after.own), channel_id=1, source_target_pairs={{0,2},{4,6},{2,0},{6,4},{1,3},{5,7},{3,1},{7,5},{8,10},{12,14},{10... | collective-permute-start | bytes 61448 | tf_op jit(solution)/shard_map/ppermute | solution.py:450
  19.9 4.7 %collective-permute-start.7 = (bf16[96,384]{1,0:T(8,128)(2,1)S(1)}, bf16[96,384]{1,0:T(8,128)(2,1)S(1)}, u32[]{:S(2)}, u32[]{:S(2)}) collective-permute-start(bf16[96,384]{1,0:T(8,128)(2,1)S(1)} %get-tuple-element.56), channel_id=1, source_target_pairs={{1,8},{9,16},{17,24},{25,0},{8,1},{16,9},{24,17},{0,25},{3,10},{11... | collective-permute-start | bytes 221192 | tf_op jit(solution)/shard_map/ppermute | solution.py:480
  20.0 3.5 %collective-permute-start.8 = (bf16[80,384]{1,0:T(8,128)(2,1)S(1)}, bf16[80,384]{1,0:T(8,128)(2,1)S(1)}, u32[]{:S(2)}, u32[]{:S(2)}) collective-permute-start(bf16[80,384]{1,0:T(8,128)(2,1)S(1)} %get-tuple-element.57), channel_id=1, source_target_pairs={{0,1},{1,0},{2,3},{3,2},{4,5},{5,4},{6,7},{7,6},{8,9},{9,8},{10,11... | collective-permute-start | bytes 184328 | tf_op jit(solution)/shard_map/ppermute | solution.py:477
  24.8 6.5 %collective-permute-start.10 = (bf16[80,128]{1,0:T(8,128)(2,1)S(1)}, bf16[80,128]{1,0:T(8,128)(2,1)S(1)}, u32[]{:S(2)}, u32[]{:S(2)}) collective-permute-start(bf16[80,128]{1,0:T(8,128)(2,1)S(1)} %get-tuple-element.61.fown), channel_id=1, source_target_pairs={{0,2},{4,6},{2,0},{6,4},{1,3},{5,7},{3,1},{7,5},{8,10},{12,14},{10... | collective-permute-start | bytes 61448 | tf_op jit(solution)/shard_map/ppermute | solution.py:450
  25.1 6.2 %collective-permute-start.9 = (bf16[80,128]{1,0:T(8,128)(2,1)S(1)}, bf16[80,128]{1,0:T(8,128)(2,1)S(1)}, u32[]{:S(2)}, u32[]{:S(2)}) collective-permute-start(bf16[80,128]{1,0:T(8,128)(2,1)S(1)} %get-tuple-element.61.fown), channel_id=1, source_target_pairs={{2,4},{6,0},{4,2},{0,6},{3,5},{7,1},{5,3},{1,7},{10,12},{14,8},{12... | collective-permute-start | bytes 61448 | tf_op jit(solution)/shard_map/ppermute | solution.py:450
  26.8 4.5 %collective-permute-start.11 = (f32[8,128]{1,0:T(8,128)S(1)}, f32[8,128]{1,0:T(8,128)S(1)}, u32[]{:S(2)}, u32[]{:S(2)}) collective-permute-start(f32[8,128]{1,0:T(8,128)S(1)} %get-tuple-element.63.cost), channel_id=1, source_target_pairs={{0,4},{2,6},{4,0},{6,2},{1,5},{3,7},{5,1},{7,3},{8,12},{10,14},{12... | collective-permute-start | bytes 12296 | tf_op jit(solution)/shard_map/ppermute | solution.py:456
  33.0 7.1 %collective-permute-start.12 = (f32[320,128]{1,0:T(8,128)S(1)}, f32[320,128]{1,0:T(8,128)S(1)}, u32[]{:S(2)}, u32[]{:S(2)}) collective-permute-start(f32[320,128]{1,0:T(8,128)S(1)} %get-tuple-element.65), channel_id=1, source_target_pairs={{0,1},{1,0},{2,3},{3,2},{4,5},{5,4},{6,7},{7,6},{8,9},{9,8},{10,11... | collective-permute-start | bytes 491528 | tf_op jit(solution)/shard_map/ppermute | solution.py:477
  33.1 5.9 %collective-permute-start.13 = (f32[8,128]{1,0:T(8,128)S(1)}, f32[8,128]{1,0:T(8,128)S(1)}, u32[]{:S(2)}, u32[]{:S(2)}) collective-permute-start(f32[8,128]{1,0:T(8,128)S(1)} %shard_map.120.after), channel_id=1, source_target_pairs={{0,16},{8,24},{16,0},{24,8},{1,17},{9,25},{17,1},{25,9},{2,18},{10... | collective-permute-start | bytes 12296 | tf_op jit(solution)/shard_map/ppermute | solution.py:456
  39.0 1.2 %collective-permute-start.14 = (f32[8,128]{1,0:T(8,128)S(1)}, f32[8,128]{1,0:T(8,128)S(1)}, u32[]{:S(2)}, u32[]{:S(2)}) collective-permute-start(f32[8,128]{1,0:T(8,128)S(1)} %add.3.cost), channel_id=1, source_target_pairs={{0,1},{1,0},{2,3},{3,2},{4,5},{5,4},{6,7},{7,6},{8,9},{9,8},{10,11... | collective-permute-start | bytes 12296 | tf_op jit(solution)/shard_map/ppermute | solution.py:477

commit v4 on v3

--- a/solution.py
+++ b/solution.py
@@ -129,32 +129,29 @@
 
 
 def arrange_own(
-    rows, counts, lookup, weight, mixing, diffusion, radiance, inc, u, v,
+    rows, lookup, weight, mixing, diffusion, radiance, inc, u, v,
     main_i, main_u, main_v, inner, edge, par, places, weights,
-    count_at, lookup_at, weight_at, mixing_at, diffusion_at, radiance_at, inc_at, u_at, v_at, arrived,
+    lookup_at, weight_at, mixing_at, diffusion_at, radiance_at, inc_at, u_at, v_at, arrived,
 ):
     core = lax.axis_index("lev")
-    here = (count_at, lookup_at, weight_at, mixing_at, diffusion_at, radiance_at, inc_at, u_at, v_at)
+    here = (lookup_at, weight_at, mixing_at, diffusion_at, radiance_at, inc_at, u_at, v_at)
     copies = [
         pltpu.make_async_copy(src, dst, arrived.at[i])
         for i, (src, dst) in enumerate(
-            zip((counts, lookup, weight, mixing, diffusion, radiance, inc, u, v), here)
+            zip((lookup, weight, mixing, diffusion, radiance, inc, u, v), here)
         )
     ]
     for copy in copies:
         copy.start()
-    for copy in copies[:6]:
+    for copy in copies[:5]:
         copy.wait()
-    slots, width = lookup.shape
-    columns = main_i.shape[1]
-    slot = lax.broadcasted_iota(jnp.int32, (slots, width), 0)
-    places[...] = jnp.where(slot < count_at[0, 0], lookup_at[...] - core * columns, -1)
+    places[...] = lookup_at[...] - core * main_i.shape[1]
     part, levels = mixing.shape
     weights[...] = jnp.broadcast_to(as_column(weight_at[...]), weights.shape)
     par[:, :B] = jnp.broadcast_to(as_column(diffusion_at[...]), (part, B))
     par[:, :levels] = mixing_at[...]
     par[:, B:] = radiance_at[...].astype(jnp.float32)
-    for copy in copies[6:]:
+    for copy in copies[5:]:
         copy.wait()
     level = pl.multiple_of(core * part, 8)
     spread_rows(rows, core, (inc_at, u_at, v_at), level, (main_i, main_u, main_v), inner, edge)
@@ -168,12 +165,13 @@
     spread_rows(rows, core, (inc, u, v), level, (main_i, main_u, main_v), inner, edge)
 
 
-def one_hot(after, places, hot):
+def one_hot(counts, after, places, hot):
     columns = hot.shape[0]
     slots, width = places.shape
     index = lax.broadcasted_iota(jnp.int32, (columns, width), 0)
     for s in range(slots):
-        hot[:, s * width : (s + 1) * width] = jnp.where(index == places[s : s + 1, :], 1.0, 0.0).astype(jnp.bfloat16)
+        place = jnp.where(s < counts[0, 0], places[s : s + 1, :], -1)
+        hot[:, s * width : (s + 1) * width] = jnp.where(index == place, 1.0, 0.0).astype(jnp.bfloat16)
 
 
 def by_column(after, hot, observed, out, live, stacked):
@@ -327,11 +325,14 @@
     packed[...] = both.astype(packed.dtype)
 
 
-def add_sides(two_sided, cost, cost_2, west, east, total):
-    west, east = by_side(west, east)
+def add_sides(cost, one, two, *refs):
+    *more, total = refs
+    west, east = by_side(one, two)
     here = cost[...] + carried_in(west, B - 3)[: cost.shape[0]]
-    if two_sided:
-        here = here + cost_2[...] + carried_in(east, B - 3)[: cost.shape[0]]
+    if more:
+        here = here + carried_in(east, B - 3)[: cost.shape[0]]
+    for other in more:
+        here = here + other[...]
     total[...] = here
 
 
@@ -403,37 +404,40 @@
         sent[pl.ds(j, part, stride=half), :] = jnp.where(low, value[part:], value[:part])
 
 
-def finish(cells, kept, got, cost, cost_2, gradient, value, done):
-    core = lax.axis_index("lev")
+def write_half(kept, gradient, done):
     half = kept.shape[1]
-    copies = [
-        pltpu.make_async_copy(src, gradient.at[:, pl.ds(pl.multiple_of(at * half, 8), half), :], done.at[i])
-        for i, (src, at) in enumerate(((kept, core), (got, 1 - core)))
-    ]
-    for copy in copies:
-        copy.start()
-    value[0, 0] = jnp.max(cost[0:1, :] + cost_2[0:1, :]) / cells
-    for copy in copies:
-        copy.wait()
-
-
-def call(kernel, outs, scratch=(), aliases=None, from_hbm=False, to_hbm=False, flops=10**9):
-    vmem = pl.BlockSpec(memory_space=pltpu.VMEM)
-    hbm = pl.BlockSpec(memory_space=pltpu.HBM)
+    at = pl.multiple_of(lax.axis_index("lev") * half, 8)
+    copy = pltpu.make_async_copy(kept, gradient.at[:, pl.ds(at, half), :], done)
+    copy.start()
+    copy.wait()
+
+
+def finish(cells, got, cost, cost_2, begun, gradient, value, value_at, done):
+    half = got.shape[1]
+    at = pl.multiple_of((1 - lax.axis_index("lev")) * half, 8)
+    copy = pltpu.make_async_copy(got, gradient.at[:, pl.ds(at, half), :], done.at[0])
+    copy.start()
+    value_at[0, 0] = jnp.max(cost[0:1, :] + cost_2[0:1, :]) / cells
+    last = pltpu.make_async_copy(value_at, value, done.at[1])
+    last.start()
+    copy.wait()
+    last.wait()
+
+
+def call(kernel, outs, scratch=(), aliases=None, from_hbm=False, smem=0, spaces=None, results=None, flops=10**9):
+    spaces, results = dict(spaces or {}), dict(results or {})
+    spaces.update({i: pltpu.SMEM for i in range(smem)})
 
     def run(*operands):
         if from_hbm:
-            operands = [x if x.size == 1 else pltpu.with_memory_space_constraint(x, pltpu.HBM) for x in operands]
+            operands = [pltpu.with_memory_space_constraint(x, pltpu.HBM) for x in operands]
+        usual = pltpu.HBM if from_hbm else pltpu.VMEM
         return pl.pallas_call(
             kernel,
             out_shape=[jax.ShapeDtypeStruct(shape, dtype) for shape, dtype in outs],
-            in_specs=[hbm if from_hbm else vmem] * len(operands),
-            out_specs=[pl.BlockSpec(memory_space=pl.ANY), pl.BlockSpec(memory_space=pltpu.SMEM)]
-            if to_hbm
-            else [vmem] * len(outs),
-            scratch_shapes=[
-                shape if dtype is None else pltpu.VMEM(shape, dtype) for shape, dtype in scratch
-            ],
+            in_specs=[pl.BlockSpec(memory_space=spaces.get(i, usual)) for i in range(len(operands))],
+            out_specs=[pl.BlockSpec(memory_space=results.get(i, pltpu.VMEM)) for i in range(len(outs))],
+            scratch_shapes=[shape if dtype is None else pltpu.VMEM(shape, dtype) for shape, dtype in scratch],
             input_output_aliases=aliases or {},
             cost_estimate=pl.CostEstimate(flops=flops, bytes_accessed=0, transcendentals=0),
             compiler_params=pltpu.CompilerParams(vmem_limit_bytes=24 * 2**20),
@@ -492,13 +496,13 @@
     *sorted_rows, own_par, places, weights = call(
         functools.partial(arrange_own, rows),
         groups + [((part, 2 * B), f32), ((slots, B), jnp.int32), ((channels, B), f32)],
-        [(pltpu.SMEM((1, 1), jnp.int32), None), ((slots, B), jnp.int32), ((1, channels), f32)]
+        [((slots, B), jnp.int32), ((1, channels), f32)]
         + [((part, levels), f32), ((1, part), f32), ((part, channels), bf16)]
         + [field] * 3
-        + [(waits((9,)), None)],
+        + [(waits((8,)), None)],
         from_hbm=True,
     )(
-        counts, column_lookup.reshape(slots, B), obs_weight.reshape(1, -1), mixing, diffusion.reshape(1, -1),
+        column_lookup.reshape(slots, B), obs_weight.reshape(1, -1), mixing, diffusion.reshape(1, -1),
         jacobian.T, *fields,
     )
     *mains, inner, edge = call(
@@ -507,7 +511,7 @@
     )(*others, *sorted_rows)
     edge = across(edge, inside)
     other_par = swap(own_par)
-    (hot,) = call(one_hot, [((columns, slots * B), bf16)])(inner, places)
+    (hot,) = call(one_hot, [((columns, slots * B), bf16)], smem=1)(counts, inner, places)
     win_i, win_u, win_v, own = call(windows, [win] * 3 + [packed])(*mains, inner, edge, hot)
     observed, live = call(
         by_column,
@@ -524,12 +528,15 @@
         + [scalar, ((levels, 2 * B), f32)],
         [((depth, (count - 1) * B), bf16), ((levels, (count - 1) * B), f32), ((levels, (count - 1) * B), f32)],
     )(win_i, win_u, win_v, west, own, east, own_par, other_par, observed, live, weights)
+    few_points = along == 4
     f_edge, f_inner = across(f_edge, pairs), swap(f_inner)
+    far_cost = ring(cost, "lon", 2) if few_points else None
     win_1, win_2, f_own, total = call(forcing_windows, [win] * 2 + [packed, scalar])(f1, f2, f_edge, f_inner, cost)
     f_west, f_east = beside(f_own)
-    few_points = along == 4
-    total_2 = ring(total, "lon", 2) if few_points else total
-    (total,) = call(functools.partial(add_sides, few_points), [scalar], flops=10**7)(total, total_2, f_west, f_east)
+    more = []
+    if few_points:
+        more = [far_cost, across(far_cost, pairs)]
+    (total,) = call(add_sides, [scalar], flops=10**7)(total, f_west, f_east, *more)
     more = ring(total, "lat", 2) if tiles > 2 else None
     kept, sent = call(
         backward,
@@ -544,12 +551,19 @@
             total = total + ring(total, axis, shift)
             shift *= 2
     cells = increment.size * tiles * along * lax.axis_size("lev")
+    got = swap(sent).reshape(part, half, B)
+    total_2 = swap(total)
+    (begun,) = call(
+        write_half, [(increment.shape, f32)], [(waits(()), None)], results={0: pl.ANY}
+    )(kept.reshape(part, half, B))
     gradient, value = call(
         functools.partial(finish, float(cells)),
         [(increment.shape, f32), ((1, 1), f32)],
-        [(waits((2,)), None)],
-        to_hbm=True,
-    )(kept.reshape(part, half, B), swap(sent).reshape(part, half, B), total, swap(total))
+        [(pltpu.SMEM((1, 1), f32), None), (waits((2,)), None)],
+        spaces={3: pl.ANY},
+        results={0: pl.ANY, 1: pl.ANY},
+        aliases={3: 0},
+    )(got, total, total_2, begun)
     return gradient, value.reshape(())
 
 

time: 41.6 us -> 44.6 us (1.072)
  waiting for transfers between devices: 10 us -> 14.3 us
  starting transfers between devices: 20.1 us -> 18.8 us
    ppermute x2 -> x3, waiting for transfers between devices: 1.1 us -> 5.67 us  [across(): return lax.ppermute(x, ('lat', 'lev'), which)]
    ppermute x2, starting transfers between devices: 5.91 us -> 4.95 us  [ring(): lax.ppermute(x, axis, [(i, (i + shift) % count) for i in range(count)])]
    pallas_call x10 -> x11, Pallas kernels: 9.9 us -> 9.89 us  [run(): pl.pallas_call(kernel, out_shape=[jax.ShapeDtypeStruct(shape, dtype) for...]
  transfers between devices with their start and end apart: 15 -> 16, of which waited for: 7 -> 9; matrix products, arithmetic and copies ran while one was open for 0% -> 0% of each run, Pallas kernels for 11% -> 12%
where the time goes in v4:
time: 44.6 us; the launch traced here: 44.4 us
  starting transfers between devices  18.8 us (42%)
  waiting for transfers between devices  14.3 us (32%)
  Pallas kernels  9.89 us (22%)
  between operations  1.42 us (3%)
    pallas_call x11, Pallas kernels, run(): pl.pallas_call(kernel, out_shape=[jax.ShapeDtypeStruct(shape, dtype) for...  9.89 us
    ppermute x7, starting transfers between devices, swap(): return lax.ppermute(x, 'lev', [(0, 1), (1, 0)])  7.44 us
    ppermute x3, waiting for transfers between devices, across(): return lax.ppermute(x, ('lat', 'lev'), which)  5.67 us
    ppermute x4, starting transfers between devices, beside(): lax.ppermute(x, 'lon', pairs + [(b, a) for a, b in pairs] if count > 2 el...  5.63 us
    ppermute x2, starting transfers between devices, ring(): lax.ppermute(x, axis, [(i, (i + shift) % count) for i in range(count)])  4.95 us
    ppermute x2, waiting for transfers between devices, ring(): lax.ppermute(x, axis, [(i, (i + shift) % count) for i in range(count)])  4.5 us
    ppermute x4, waiting for transfers between devices, beside(): lax.ppermute(x, 'lon', pairs + [(b, a) for a, b in pairs] if count > 2 el...  2.45 us
    ppermute x7, waiting for transfers between devices, swap(): return lax.ppermute(x, 'lev', [(0, 1), (1, 0)])  1.68 us
  transfers between devices with their start and end apart: 16, of which 9 were waited for; matrix products, arithmetic and copies ran while one was open for 0% of the time, Pallas kernels for 12%

profile of v4, /device:TPU:0, one launch (start us, length us, event | category | flops | bytes accessed | tf_op | source)
XLA Modules:
  0.0 44.4 jit_solution(10133252888338873070)
XLA Ops:
  0.6 0.6 %collective-permute-start = (f32[640,128]{1,0:T(8,128)}, f32[640,128]{1,0:T(8,128)S(1)}, u32[]{:S(2)}, u32[]{:S(2)}) collective-permute-start(f32[640,128]{1,0:T(8,128)} %bitcast.14), channel_id=1, source_target_pairs={{0,1},{1,0},{2,3},{3,2},{4,5},{5,4},{6,7},{7,6},{8,9},{9,8},{10,11... | collective-permute-start | bytes 983048 | tf_op jit(solution)/shard_map/ppermute | solution.py:481
  1.7 1.6 %shard_map.113 = (f32[80,1024]{1,0:T(8,128)S(1)}, f32[80,1024]{1,0:T(8,128)S(1)}, f32[80,1024]{1,0:T(8,128)S(1)}, f32[80,640]{1,0:T(8,128)S(1)}, bf16[80,640]{1,...) custom-call(s32[16,128]{1,0:T(8,128)} %bitcast.21, f32[1,128]{1,0:T(1,128)} %bitcast.22, ...), custom_call_target="tpu_custom_call" | custom-call | flops 1000000000 | tf_op jit(solution)/shard_map/pallas_call | solution.py:435
  3.8 0.7 %collective-permute-start.3 = (bf16[80,640]{1,0:T(8,128)(2,1)S(1)}, bf16[80,640]{1,0:T(8,128)(2,1)S(1)}, u32[]{:S(2)}, u32[]{:S(2)}) collective-permute-start(bf16[80,640]{1,0:T(8,128)(2,1)S(1)} %get-tuple-element.44), channel_id=1, source_target_pairs={{1,8},{9,16},{17,24},{8,1},{16,9},{24,17},{3,10},{11,18},{19,26},{... | collective-permute-start | bytes 307208 | tf_op jit(solution)/shard_map/ppermute | solution.py:484
  4.5 4.3 %collective-permute-start.6 = (f32[40,256]{1,0:T(8,128)S(1)}, f32[40,256]{1,0:T(8,128)S(1)}, u32[]{:S(2)}, u32[]{:S(2)}) collective-permute-start(f32[40,256]{1,0:T(8,128)S(1)} %get-tuple-element.50.own_par), channel_id=1, source_target_pairs={{0,1},{1,0},{2,3},{3,2},{4,5},{5,4},{6,7},{7,6},{8,9},{9,8},{10,11... | collective-permute-start | bytes 122888 | tf_op jit(solution)/shard_map/ppermute | solution.py:481
  9.5 1.2 %shard_map.115.after.hot = bf16[1024,2048]{1,0:T(8,128)(2,1)S(1)} custom-call(s32[1,1]{1,0:T(1,128)S(6)} %copy.24.counts, f32[80,640]{1,0:T(8,128)S(1)} %get-tuple-element.43.after.inner, s32[16,128]{1,0:T(8,128)S(1)} %get-tuple-element.45.places), custom_call_target="tpu_custom_call" | custom-call | flops 1000000000 | tf_op jit(solution)/shard_map/pallas_call | solution.py:435
  11.0 3.7 %collective-permute-start.4 = (bf16[80,128]{1,0:T(8,128)(2,1)S(1)}, bf16[80,128]{1,0:T(8,128)(2,1)S(1)}, u32[]{:S(2)}, u32[]{:S(2)}) collective-permute-start(bf16[80,128]{1,0:T(8,128)(2,1)S(1)} %get-tuple-element.49.after.own), channel_id=1, source_target_pairs={{2,4},{6,0},{4,2},{0,6},{3,5},{7,1},{5,3},{1,7},{10,12},{14,8},{12... | collective-permute-start | bytes 61448 | tf_op jit(solution)/shard_map/ppermute | solution.py:454
  14.7 1.4 %shard_map.117 = (bf16[256,1024]{1,0:T(8,128)(2,1)S(1)}, f32[8,1024]{1,0:T(8,128)S(1)}) custom-call(bf16[80,128]{1,0:T(8,128)(2,1)S(1)} %get-tuple-element.49.after.own, bf16[1024,2048]{1,0:T(8,128)(2,1)S(1)} %shard_map.115.after.hot, bf16[2,16,128,128]{3,2,1,0:T(8,128)(2,1)S(1)} %bitcast.11), custom_call_target="tpu_custom_call" | custom-call | flops 1000000000 | tf_op jit(solution)/shard_map/pallas_call | solution.py:435
  16.1 0.6 %collective-permute-done.4.west = bf16[80,128]{1,0:T(8,128)(2,1)S(1)} collective-permute-done((bf16[80,128]{1,0:T(8,128)(2,1)S(1)}, bf16[80,128]{1,0:T(8,128)(2,1)S(1)}, u32[]{:S(2)}, u32[]{:S(2)}) %collective-permute-start.4) | collective-permute-done | bytes 20512 | tf_op jit(solution)/shard_map/ppermute | solution.py:454
  16.7 1.9 %collective-permute-done.5.east = bf16[80,128]{1,0:T(8,128)(2,1)S(1)} collective-permute-done((bf16[80,128]{1,0:T(8,128)(2,1)S(1)}, bf16[80,128]{1,0:T(8,128)(2,1)S(1)}, u32[]{:S(2)}, u32[]{:S(2)}) %collective-permute-start.5) | collective-permute-done | bytes 20512 | tf_op jit(solution)/shard_map/ppermute | solution.py:454
  18.5 1.9 %shard_map.118 = (bf16[80,1024]{1,0:T(8,128)(2,1)S(1)}, bf16[80,1024]{1,0:T(8,128)(2,1)S(1)}, bf16[96,384]{1,0:T(8,128)(2,1)S(1)}, bf16[80,384]{1,0:T(8,128)(2,1...) custom-call(f32[80,1536]{1,0:T(8,128)S(1)} %get-tuple-element.46.win_i, f32[80,1536]{1,0:T(8,128)S(1)} %get-tuple-element.47.win_u, ...), custom_call_target="tpu_custom_call" | custom-call | flops 1000000000 | tf_op jit(solution)/shard_map/pallas_call | solution.py:435
  20.5 2.0 %collective-permute-start.8 = (bf16[80,384]{1,0:T(8,128)(2,1)S(1)}, bf16[80,384]{1,0:T(8,128)(2,1)S(1)}, u32[]{:S(2)}, u32[]{:S(2)}) collective-permute-start(bf16[80,384]{1,0:T(8,128)(2,1)S(1)} %get-tuple-element.57), channel_id=1, source_target_pairs={{0,1},{1,0},{2,3},{3,2},{4,5},{5,4},{6,7},{7,6},{8,9},{9,8},{10,11... | collective-permute-start | bytes 184328 | tf_op jit(solution)/shard_map/ppermute | solution.py:481
  22.5 0.9 %collective-permute-done.8.inner = bf16[80,384]{1,0:T(8,128)(2,1)S(1)} collective-permute-done((bf16[80,384]{1,0:T(8,128)(2,1)S(1)}, bf16[80,384]{1,0:T(8,128)(2,1)S(1)}, u32[]{:S(2)}, u32[]{:S(2)}) %collective-permute-start.8) | collective-permute-done | bytes 61472 | tf_op jit(solution)/shard_map/ppermute | solution.py:481
  23.4 1.7 %collective-permute-done.7.edge = bf16[96,384]{1,0:T(8,128)(2,1)S(1)} collective-permute-done((bf16[96,384]{1,0:T(8,128)(2,1)S(1)}, bf16[96,384]{1,0:T(8,128)(2,1)S(1)}, u32[]{:S(2)}, u32[]{:S(2)}) %collective-permute-start.7) | collective-permute-done | bytes 73760 | tf_op jit(solution)/shard_map/ppermute | solution.py:484
  25.3 0.5 %collective-permute-start.10 = (bf16[80,128]{1,0:T(8,128)(2,1)S(1)}, bf16[80,128]{1,0:T(8,128)(2,1)S(1)}, u32[]{:S(2)}, u32[]{:S(2)}) collective-permute-start(bf16[80,128]{1,0:T(8,128)(2,1)S(1)} %get-tuple-element.61.fown), channel_id=1, source_target_pairs={{0,2},{4,6},{2,0},{6,4},{1,3},{5,7},{3,1},{7,5},{8,10},{12,14},{10... | collective-permute-start | bytes 61448 | tf_op jit(solution)/shard_map/ppermute | solution.py:454
  25.9 1.4 %collective-permute-start.9 = (bf16[80,128]{1,0:T(8,128)(2,1)S(1)}, bf16[80,128]{1,0:T(8,128)(2,1)S(1)}, u32[]{:S(2)}, u32[]{:S(2)}) collective-permute-start(bf16[80,128]{1,0:T(8,128)(2,1)S(1)} %get-tuple-element.61.fown), channel_id=1, source_target_pairs={{2,4},{6,0},{4,2},{0,6},{3,5},{7,1},{5,3},{1,7},{10,12},{14,8},{12... | collective-permute-start | bytes 61448 | tf_op jit(solution)/shard_map/ppermute | solution.py:454
  27.3 1.6 %collective-permute-start.11 = (f32[8,128]{1,0:T(8,128)S(1)}, f32[8,128]{1,0:T(8,128)S(1)}, u32[]{:S(2)}, u32[]{:S(2)}) collective-permute-start(f32[8,128]{1,0:T(8,128)S(1)} %get-tuple-element.58.cost), channel_id=1, source_target_pairs={{0,4},{2,6},{4,0},{6,2},{1,5},{3,7},{5,1},{7,3},{8,12},{10,14},{12... | collective-permute-start | bytes 12296 | tf_op jit(solution)/shard_map/ppermute | solution.py:460
  28.9 2.9 %collective-permute-done.11.refs_0_ = f32[8,128]{1,0:T(8,128)S(1)} collective-permute-done((f32[8,128]{1,0:T(8,128)S(1)}, f32[8,128]{1,0:T(8,128)S(1)}, u32[]{:S(2)}, u32[]{:S(2)}) %collective-permute-start.11) | collective-permute-done | bytes 4128 | tf_op jit(solution)/shard_map/ppermute | solution.py:460
  31.8 3.9 %collective-permute-done.12.refs_1_ = f32[8,128]{1,0:T(8,128)S(1)} collective-permute-done((f32[8,128]{1,0:T(8,128)S(1)}, f32[8,128]{1,0:T(8,128)S(1)}, u32[]{:S(2)}, u32[]{:S(2)}) %collective-permute-start.12) | collective-permute-done | bytes 4128 | tf_op jit(solution)/shard_map/ppermute | solution.py:484
  35.9 1.6 %shard_map.121 = (f32[320,128]{1,0:T(8,128)S(1)}, f32[320,128]{1,0:T(8,128)S(1)}) custom-call(f32[80,1536]{1,0:T(8,128)S(1)} %get-tuple-element.59.win_1, f32[80,1536]{1,0:T(8,128)S(1)} %get-tuple-element.60.win_2, bf16[80,128]{1,0:T(8,128)(2,1)S(1)} %collective-permute-done.9.one.fwest, bf16[80,128]{1,0:T(8,128)(2,1)S(1)} %get-tuple-element.61.fown, ...), custom_call_target="tpu_custom_call" | custom-call | flops 1000000000 | tf_op jit(solution)/shard_map/pallas_call | solution.py:435
  37.6 3.4 %collective-permute-start.14 = (f32[8,128]{1,0:T(8,128)S(1)}, f32[8,128]{1,0:T(8,128)S(1)}, u32[]{:S(2)}, u32[]{:S(2)}) collective-permute-start(f32[8,128]{1,0:T(8,128)S(1)} %shard_map.120.after), channel_id=1, source_target_pairs={{0,16},{8,24},{16,0},{24,8},{1,17},{9,25},{17,1},{25,9},{2,18},{10... | collective-permute-start | bytes 12296 | tf_op jit(solution)/shard_map/ppermute | solution.py:460
  40.9 1.6 %collective-permute-done.14 = f32[8,128]{1,0:T(8,128)S(1)} collective-permute-done((f32[8,128]{1,0:T(8,128)S(1)}, f32[8,128]{1,0:T(8,128)S(1)}, u32[]{:S(2)}, u32[]{:S(2)}) %collective-permute-start.14) | collective-permute-done | bytes 4128 | tf_op jit(solution)/shard_map/ppermute | solution.py:460
  42.5 0.7 %shard_map.122.begun = f32[40,16,128]{2,1,0:T(8,128)} custom-call(f32[40,8,128]{2,1,0:T(8,128)S(1)} %bitcast.13), custom_call_target="tpu_custom_call" | custom-call | flops 1000000000 | tf_op jit(solution)/shard_map/pallas_call | solution.py:435
  43.2 0.5 %collective-permute-done.15.cost_2 = f32[8,128]{1,0:T(8,128)S(1)} collective-permute-done((f32[8,128]{1,0:T(8,128)S(1)}, f32[8,128]{1,0:T(8,128)S(1)}, u32[]{:S(2)}, u32[]{:S(2)}) %collective-permute-start.15) | collective-permute-done | bytes 4128 | tf_op jit(solution)/shard_map/ppermute | solution.py:481
  43.7 0.7 %shard_map.123 = (f32[40,16,128]{2,1,0:T(8,128)}, f32[1,1]{1,0:T(1,128)}) custom-call(f32[40,8,128]{2,1,0:T(8,128)S(1)} %bitcast.12, f32[8,128]{1,0:T(8,128)S(1)} %add.3.cost, f32[8,128]{1,0:T(8,128)S(1)} %collective-permute-done.15.cost_2, f32[40,16,128]{2,1,0:T(8,128)} %shard_map.122.begun), custom_call_target="tpu_custom_call", output_to_operand_aliasing={{0}: (3, {})} | custom-call | flops 1000000000 | tf_op jit(solution)/shard_map/pallas_call | solution.py:435
  (22 shorter events, 1.8 us)
Async XLA Ops:
  0.6 2.7 %collective-permute-start = (f32[640,128]{1,0:T(8,128)}, f32[640,128]{1,0:T(8,128)S(1)}, u32[]{:S(2)}, u32[]{:S(2)}) collective-permute-start(f32[640,128]{1,0:T(8,128)} %bitcast.14), channel_id=1, source_target_pairs={{0,1},{1,0},{2,3},{3,2},{4,5},{5,4},{6,7},{7,6},{8,9},{9,8},{10,11... | collective-permute-start | bytes 983048 | tf_op jit(solution)/shard_map/ppermute | solution.py:481
  1.2 2.1 %collective-permute-start.1 = (f32[640,128]{1,0:T(8,128)}, f32[640,128]{1,0:T(8,128)S(1)}, u32[]{:S(2)}, u32[]{:S(2)}) collective-permute-start(f32[640,128]{1,0:T(8,128)} %bitcast.16), channel_id=1, source_target_pairs={{0,1},{1,0},{2,3},{3,2},{4,5},{5,4},{6,7},{7,6},{8,9},{9,8},{10,11... | collective-permute-start | bytes 983048 | tf_op jit(solution)/shard_map/ppermute | solution.py:481
  1.3 2.3 %collective-permute-start.2 = (f32[640,128]{1,0:T(8,128)}, f32[640,128]{1,0:T(8,128)S(1)}, u32[]{:S(2)}, u32[]{:S(2)}) collective-permute-start(f32[640,128]{1,0:T(8,128)} %bitcast.18), channel_id=1, source_target_pairs={{0,1},{1,0},{2,3},{3,2},{4,5},{5,4},{6,7},{7,6},{8,9},{9,8},{10,11... | collective-permute-start | bytes 983048 | tf_op jit(solution)/shard_map/ppermute | solution.py:481
  3.8 6.8 %collective-permute-start.3 = (bf16[80,640]{1,0:T(8,128)(2,1)S(1)}, bf16[80,640]{1,0:T(8,128)(2,1)S(1)}, u32[]{:S(2)}, u32[]{:S(2)}) collective-permute-start(bf16[80,640]{1,0:T(8,128)(2,1)S(1)} %get-tuple-element.44), channel_id=1, source_target_pairs={{1,8},{9,16},{17,24},{8,1},{16,9},{24,17},{3,10},{11,18},{19,26},{... | collective-permute-start | bytes 307208 | tf_op jit(solution)/shard_map/ppermute | solution.py:484
  4.5 11.5 %collective-permute-start.6 = (f32[40,256]{1,0:T(8,128)S(1)}, f32[40,256]{1,0:T(8,128)S(1)}, u32[]{:S(2)}, u32[]{:S(2)}) collective-permute-start(f32[40,256]{1,0:T(8,128)S(1)} %get-tuple-element.50.own_par), channel_id=1, source_target_pairs={{0,1},{1,0},{2,3},{3,2},{4,5},{5,4},{6,7},{7,6},{8,9},{9,8},{10,11... | collective-permute-start | bytes 122888 | tf_op jit(solution)/shard_map/ppermute | solution.py:481
  9.4 5.2 %copy-start = (bf16[2,1,1,16,128,128]{5,4,3,2,1,0:T(8,128)(2,1)S(1)}, bf16[2,1,1,16,128,128]{5,4,3,2,1,0:T(8,128)(2,1)}, u32[]{:S(2)}) copy-start(bf16[2,1,1,16,128,128]{5,4,3,2,1,0:T(8,128)(2,1)} %param.17) | copy-start | bytes 3145732
  11.0 5.7 %collective-permute-start.4 = (bf16[80,128]{1,0:T(8,128)(2,1)S(1)}, bf16[80,128]{1,0:T(8,128)(2,1)S(1)}, u32[]{:S(2)}, u32[]{:S(2)}) collective-permute-start(bf16[80,128]{1,0:T(8,128)(2,1)S(1)} %get-tuple-element.49.after.own), channel_id=1, source_target_pairs={{2,4},{6,0},{4,2},{0,6},{3,5},{7,1},{5,3},{1,7},{10,12},{14,8},{12... | collective-permute-start | bytes 61448 | tf_op jit(solution)/shard_map/ppermute | solution.py:454
  14.7 3.9 %collective-permute-start.5 = (bf16[80,128]{1,0:T(8,128)(2,1)S(1)}, bf16[80,128]{1,0:T(8,128)(2,1)S(1)}, u32[]{:S(2)}, u32[]{:S(2)}) collective-permute-start(bf16[80,128]{1,0:T(8,128)(2,1)S(1)} %get-tuple-element.49.after.own), channel_id=1, source_target_pairs={{0,2},{4,6},{2,0},{6,4},{1,3},{5,7},{3,1},{7,5},{8,10},{12,14},{10... | collective-permute-start | bytes 61448 | tf_op jit(solution)/shard_map/ppermute | solution.py:454
  20.4 4.7 %collective-permute-start.7 = (bf16[96,384]{1,0:T(8,128)(2,1)S(1)}, bf16[96,384]{1,0:T(8,128)(2,1)S(1)}, u32[]{:S(2)}, u32[]{:S(2)}) collective-permute-start(bf16[96,384]{1,0:T(8,128)(2,1)S(1)} %get-tuple-element.56), channel_id=1, source_target_pairs={{1,8},{9,16},{17,24},{25,0},{8,1},{16,9},{24,17},{0,25},{3,10},{11... | collective-permute-start | bytes 221192 | tf_op jit(solution)/shard_map/ppermute | solution.py:484
  20.5 2.9 %collective-permute-start.8 = (bf16[80,384]{1,0:T(8,128)(2,1)S(1)}, bf16[80,384]{1,0:T(8,128)(2,1)S(1)}, u32[]{:S(2)}, u32[]{:S(2)}) collective-permute-start(bf16[80,384]{1,0:T(8,128)(2,1)S(1)} %get-tuple-element.57), channel_id=1, source_target_pairs={{0,1},{1,0},{2,3},{3,2},{4,5},{5,4},{6,7},{7,6},{8,9},{9,8},{10,11... | collective-permute-start | bytes 184328 | tf_op jit(solution)/shard_map/ppermute | solution.py:481
  25.3 10.4 %collective-permute-start.10 = (bf16[80,128]{1,0:T(8,128)(2,1)S(1)}, bf16[80,128]{1,0:T(8,128)(2,1)S(1)}, u32[]{:S(2)}, u32[]{:S(2)}) collective-permute-start(bf16[80,128]{1,0:T(8,128)(2,1)S(1)} %get-tuple-element.61.fown), channel_id=1, source_target_pairs={{0,2},{4,6},{2,0},{6,4},{1,3},{5,7},{3,1},{7,5},{8,10},{12,14},{10... | collective-permute-start | bytes 61448 | tf_op jit(solution)/shard_map/ppermute | solution.py:454
  25.9 9.9 %collective-permute-start.9 = (bf16[80,128]{1,0:T(8,128)(2,1)S(1)}, bf16[80,128]{1,0:T(8,128)(2,1)S(1)}, u32[]{:S(2)}, u32[]{:S(2)}) collective-permute-start(bf16[80,128]{1,0:T(8,128)(2,1)S(1)} %get-tuple-element.61.fown), channel_id=1, source_target_pairs={{2,4},{6,0},{4,2},{0,6},{3,5},{7,1},{5,3},{1,7},{10,12},{14,8},{12... | collective-permute-start | bytes 61448 | tf_op jit(solution)/shard_map/ppermute | solution.py:454
  27.3 4.5 %collective-permute-start.11 = (f32[8,128]{1,0:T(8,128)S(1)}, f32[8,128]{1,0:T(8,128)S(1)}, u32[]{:S(2)}, u32[]{:S(2)}) collective-permute-start(f32[8,128]{1,0:T(8,128)S(1)} %get-tuple-element.58.cost), channel_id=1, source_target_pairs={{0,4},{2,6},{4,0},{6,2},{1,5},{3,7},{5,1},{7,3},{8,12},{10,14},{12... | collective-permute-start | bytes 12296 | tf_op jit(solution)/shard_map/ppermute | solution.py:460
  31.8 3.9 %collective-permute-start.12 = (f32[8,128]{1,0:T(8,128)S(1)}, f32[8,128]{1,0:T(8,128)S(1)}, u32[]{:S(2)}, u32[]{:S(2)}) collective-permute-start(f32[8,128]{1,0:T(8,128)S(1)} %collective-permute-done.11.refs_0_), channel_id=1, source_target_pairs={{1,8},{9,16},{17,24},{25,0},{8,1},{16,9},{24,17},{0,25},{3,10},{11... | collective-permute-start | bytes 12296 | tf_op jit(solution)/shard_map/ppermute | solution.py:484
  37.5 6.2 %collective-permute-start.13 = (f32[320,128]{1,0:T(8,128)S(1)}, f32[320,128]{1,0:T(8,128)S(1)}, u32[]{:S(2)}, u32[]{:S(2)}) collective-permute-start(f32[320,128]{1,0:T(8,128)S(1)} %get-tuple-element.64), channel_id=1, source_target_pairs={{0,1},{1,0},{2,3},{3,2},{4,5},{5,4},{6,7},{7,6},{8,9},{9,8},{10,11... | collective-permute-start | bytes 491528 | tf_op jit(solution)/shard_map/ppermute | solution.py:481
  37.6 4.9 %collective-permute-start.14 = (f32[8,128]{1,0:T(8,128)S(1)}, f32[8,128]{1,0:T(8,128)S(1)}, u32[]{:S(2)}, u32[]{:S(2)}) collective-permute-start(f32[8,128]{1,0:T(8,128)S(1)} %shard_map.120.after), channel_id=1, source_target_pairs={{0,16},{8,24},{16,0},{24,8},{1,17},{9,25},{17,1},{25,9},{2,18},{10... | collective-permute-start | bytes 12296 | tf_op jit(solution)/shard_map/ppermute | solution.py:460
  42.5 1.2 %collective-permute-start.15 = (f32[8,128]{1,0:T(8,128)S(1)}, f32[8,128]{1,0:T(8,128)S(1)}, u32[]{:S(2)}, u32[]{:S(2)}) collective-permute-start(f32[8,128]{1,0:T(8,128)S(1)} %add.3.cost), channel_id=1, source_target_pairs={{0,1},{1,0},{2,3},{3,2},{4,5},{5,4},{6,7},{7,6},{8,9},{9,8},{10,11... | collective-permute-start | bytes 12296 | tf_op jit(solution)/shard_map/ppermute | solution.py:481

commit v5 on v4

--- a/solution.py
+++ b/solution.py
@@ -59,17 +59,24 @@
     return jnp.where(lane < B // 2, western, eastern)
 
 
-def from_east(x, side, q):
-    lane = lanes_of(x.shape[0])
-    return jnp.where(lane == B - 1, roll(side, B - 1 - (B // 2 + q * GROUP + 2)), roll(x, -1))
-
-
-def from_west(x, side, q):
-    lane = lanes_of(x.shape[0])
-    return jnp.where(lane == 0, roll(side, -(q * GROUP + 1)), roll(x, 1))
-
-
-def put_split(stack, p, x):
+def both_ends(from_east, from_west):
+    lane = lanes_of(from_east.shape[0])
+    return jnp.where(lane % GROUP == 0, roll(from_east, -(B // 2 + 2)), from_west)
+
+
+def beyond(ends, q):
+    return roll(ends, B - 1 - q * GROUP)
+
+
+def from_east(x, ends):
+    return jnp.where(lanes_of(x.shape[0]) == B - 1, ends, roll(x, -1))
+
+
+def from_west(x, ends):
+    return jnp.where(lanes_of(x.shape[0]) == 0, ends, roll(x, 1))
+
+
+def put(stack, p, x):
     levels = x.shape[0]
     head = x.astype(jnp.bfloat16)
     stack[0:levels, p * B : (p + 1) * B] = head
@@ -205,10 +212,10 @@
     low = lax.axis_index("lev") == 0
     count = win_i.shape[1] // B
     k = 0
-    for main, win, width in ((main_i, win_i, HALO), (main_u, win_u, 1), (main_v, win_v, HALO)):
-        win[:, HALO * B : (count - HALO) * B] = main[...]
+    for main, win, width, scale in ((main_i, win_i, HALO, 1.0), (main_u, win_u, 1, 0.5), (main_v, win_v, HALO, 0.5)):
+        win[:, HALO * B : (count - HALO) * B] = scale * main[...]
         span = slice(k * B, (k + width) * B)
-        fill_halo(win, inner[:, span], edge[:, span].astype(jnp.float32), low, width)
+        fill_halo(win, scale * inner[:, span], scale * edge[:, span].astype(jnp.float32), low, width)
         k += width
     packed[...] = pack_edges(
         [functools.partial(block, win) for win in (win_i, win_u, win_v)], count - 2
@@ -216,12 +223,7 @@
 
 
 def smooth(x, north, south, east, west, diff, u, v):
-    return (
-        x
-        + diff * ((north + south) + (east + west) - 4.0 * x)
-        - 0.5 * u * (east - west)
-        - 0.5 * v * (north - south)
-    )
+    return x + diff * ((north + south) + (east + west) - 4.0 * x) - u * (east - west) - v * (north - south)
 
 
 def forward(
@@ -236,26 +238,27 @@
     count = win_i.shape[1] // B
     rows = count - 2
     half = rows - 2
-    diff = par[:, levels : levels + 1]
+    diff = jnp.broadcast_to(par[:, levels : levels + 1], (levels, B))
     coupling = split_matrix(par[:, :B], levels)
     radiance = par[:, B:].astype(jnp.bfloat16)
     channels = radiance.shape[1]
     scale = weights[:, :1]
     clear_rest(stack, levels)
     sides = [side_block(west, own, east, f, rows) for f in range(3)]
+    ends = both_ends(sides[0], sides[0])
     for q in range(rows):
         p = q + 1
-        x = block(win_i, p)
+        x, here = block(win_i, p), beyond(ends, q)
         s = smooth(
-            x, block(win_i, p + 1), block(win_i, p - 1), from_east(x, sides[0], q), from_west(x, sides[0], q),
+            x, block(win_i, p + 1), block(win_i, p - 1), from_east(x, here), from_west(x, here),
             diff, block(win_u, p), block(win_v, p),
         )
         plain[:, q * B : (q + 1) * B] = s
-        put_split(stack, q, s)
+        put(stack, q, s)
     x = sides[0]
     s = smooth(x, roll(x, -GROUP), roll(x, GROUP), roll(x, -1), roll(x, 1), diff, sides[1], sides[2])
     plain[:, rows * B :] = s
-    put_split(stack, rows, s)
+    put(stack, rows, s)
     state[...] = plain[...] + jnp.dot(coupling, stack[...], preferred_element_type=jnp.float32)
     first, final = (rows - 1) * B, rows * B
     state[:, :B] = jnp.where(is_first, state[:, :B], 0.0)
@@ -273,15 +276,15 @@
         return jnp.sum(misfit * scaled, keepdims=True)
 
     total = observe(state[:, B : (half + 1) * B].astype(jnp.bfloat16), 0, f1)
-    side = state[:, rows * B :]
+    ends = both_ends(state[:, rows * B :], state[:, rows * B :])
     for q in range(1, rows - 1):
-        x = block(state, q)
+        x, here = block(state, q), beyond(ends, q)
         s = smooth(
-            x, block(state, q + 1), block(state, q - 1), from_east(x, side, q), from_west(x, side, q),
+            x, block(state, q + 1), block(state, q - 1), from_east(x, here), from_west(x, here),
             diff, block(win_u, q + 1), block(win_v, q + 1),
         )
         plain[:, (q - 1) * B : q * B] = s
-        put_split(stack, q - 1, s)
+        put(stack, q - 1, s)
     end = plain[:, : half * B] + jnp.dot(coupling, stack[:, : half * B], preferred_element_type=jnp.float32)
     total = total + observe(end.astype(jnp.bfloat16), 1, f2)
     whole = win_i[:, HALO * B : (count - HALO) * B]
@@ -345,7 +348,7 @@
     count = win_i.shape[1] // B
     rows = count - 2
     half = rows - 2
-    diff = par[:, levels : levels + 1]
+    diff = jnp.broadcast_to(par[:, levels : levels + 1], (levels, B))
     middle = 1.0 - 4.0 * diff
     square[...] = jnp.zeros(square.shape, jnp.float32)
     square[:levels, :] = jnp.where(lanes_of(levels) < levels, par[:, :B], 0.0)
@@ -356,26 +359,26 @@
     for p in range(count):
         x = block(win_2, p)
         coupled[:, p * B : (p + 1) * B] = x
-        put_split(stack, p, x)
+        put(stack, p, x)
     coupled[:, count * B :] = f_sides[0]
-    put_split(stack, count, f_sides[0])
+    put(stack, count, f_sides[0])
     coupled[...] = coupled[...] + jnp.dot(coupling, stack[...], preferred_element_type=jnp.float32)
 
-    def spread(p, q, side):
-        x = block(coupled, p)
-        north = (diff + 0.5 * block(win_v, q + 2)) * block(coupled, p + 1)
-        south = (diff - 0.5 * block(win_v, q)) * block(coupled, p - 1)
-        u = 0.5 * block(win_u, q + 1)
-        side_east = (diff + 0.5 * sides[1]) * side
-        side_west = (diff - 0.5 * sides[1]) * side
+    def ends_of(side):
+        return both_ends((diff + sides[1]) * side, (diff - sides[1]) * side)
+
+    def spread(p, q, ends):
+        x, here = block(coupled, p), beyond(ends, q)
+        north = (diff + block(win_v, q + 2)) * block(coupled, p + 1)
+        south = (diff - block(win_v, q)) * block(coupled, p - 1)
+        u = block(win_u, q + 1)
         return (
-            middle * x + north + south + from_east((diff + u) * x, side_east, q)
-            + from_west((diff - u) * x, side_west, q)
+            middle * x + (north + south) + (from_east((diff + u) * x, here) + from_west((diff - u) * x, here))
         )
 
     side = coupled[:, count * B :]
     after = []
-    side_v, side_u = 0.5 * sides[2], 0.5 * sides[1]
+    side_v, side_u = sides[2], sides[1]
     result = (
         middle * side
         + roll((diff + side_v) * side, -GROUP)
@@ -384,22 +387,23 @@
         + roll((diff - side_u) * side, 1)
         + f_sides[1]
     )
+    ends = ends_of(side)
     for q in range(rows):
-        after.append(spread(q + 1, q, side) + block(win_1, q + 1))
+        after.append(spread(q + 1, q, ends) + block(win_1, q + 1))
     after[0] = jnp.where(is_first, after[0], 0.0)
     after[-1] = jnp.where(is_final, after[-1], 0.0)
     for q in range(rows):
         coupled[:, (q + 1) * B : (q + 2) * B] = after[q]
-        put_split(stack, q, after[q])
+        put(stack, q, after[q])
     coupled[:, count * B :] = result
-    put_split(stack, rows, result)
+    put(stack, rows, result)
     mixed = jnp.dot(coupling, stack[:, : (rows + 1) * B], preferred_element_type=jnp.float32)
     coupled[:, B : (rows + 1) * B] = coupled[:, B : (rows + 1) * B] + mixed[:, : rows * B]
-    side = coupled[:, count * B :] + mixed[:, rows * B :]
+    ends = ends_of(coupled[:, count * B :] + mixed[:, rows * B :])
     low = core == 0
     part = levels // 2
     for j in range(half):
-        value = block(win_i, j + HALO) + spread(j + HALO, j + 1, side)
+        value = block(win_i, j + HALO) + spread(j + HALO, j + 1, ends)
         kept[pl.ds(j, part, stride=half), :] = jnp.where(low, value[:part], value[part:])
         sent[pl.ds(j, part, stride=half), :] = jnp.where(low, value[part:], value[:part])
 
@@ -535,7 +539,8 @@
     f_west, f_east = beside(f_own)
     more = []
     if few_points:
-        more = [far_cost, across(far_cost, pairs)]
+        flip = [(i, i ^ 1) for i in range(tiles)]
+        more = [far_cost, lax.ppermute(far_cost, "lat", flip)]
     (total,) = call(add_sides, [scalar], flops=10**7)(total, f_west, f_east, *more)
     more = ring(total, "lat", 2) if tiles > 2 else None
     kept, sent = call(

time: 44.6 us -> 44.1 us (0.989)
  waiting for transfers between devices: 14.3 us -> 12.9 us
  starting transfers between devices: 18.8 us -> 19.9 us
    ppermute x3 -> x2, waiting for transfers between devices: 5.67 us -> 1.74 us  [across(): return lax.ppermute(x, ('lat', 'lev'), which)]
    ppermute x0 -> x1, waiting for transfers between devices: none -> 2.5 us  [body(): more = [far_cost, lax.ppermute(far_cost, 'lat', flip)]]
    ppermute x0 -> x1, starting transfers between devices: none -> 1.1 us  [body(): more = [far_cost, lax.ppermute(far_cost, 'lat', flip)]]
where the time goes in v5:
time: 44.1 us; the launch traced here: 43.9 us
  starting transfers between devices  19.9 us (45%)
  waiting for transfers between devices  12.9 us (29%)
  Pallas kernels  9.72 us (22%)
  between operations  1.42 us (3%)
    pallas_call x11, Pallas kernels, run(): pl.pallas_call(kernel, out_shape=[jax.ShapeDtypeStruct(shape, dtype) for...  9.72 us
    ppermute x7, starting transfers between devices, swap(): return lax.ppermute(x, 'lev', [(0, 1), (1, 0)])  7.44 us
    ppermute x4, starting transfers between devices, beside(): lax.ppermute(x, 'lon', pairs + [(b, a) for a, b in pairs] if count > 2 el...  5.63 us
    ppermute x2, starting transfers between devices, ring(): lax.ppermute(x, axis, [(i, (i + shift) % count) for i in range(count)])  4.96 us
    ppermute x2, waiting for transfers between devices, ring(): lax.ppermute(x, axis, [(i, (i + shift) % count) for i in range(count)])  4.5 us
    ppermute x1, waiting for transfers between devices, body(): more = [far_cost, lax.ppermute(far_cost, 'lat', flip)]  2.5 us
    ppermute x4, waiting for transfers between devices, beside(): lax.ppermute(x, 'lon', pairs + [(b, a) for a, b in pairs] if count > 2 el...  2.45 us
    ppermute x2, waiting for transfers between devices, across(): return lax.ppermute(x, ('lat', 'lev'), which)  1.74 us
  transfers between devices with their start and end apart: 16, of which 9 were waited for; matrix products, arithmetic and copies ran while one was open for 0% of the time, Pallas kernels for 12%

profile of v5, /device:TPU:0, one launch (start us, length us, event | category | flops | bytes accessed | tf_op | source)
XLA Modules:
  0.0 43.9 jit_solution(3748892865549441109)
XLA Ops:
  0.6 0.6 %collective-permute-start = (f32[640,128]{1,0:T(8,128)}, f32[640,128]{1,0:T(8,128)S(1)}, u32[]{:S(2)}, u32[]{:S(2)}) collective-permute-start(f32[640,128]{1,0:T(8,128)} %bitcast.14), channel_id=1, source_target_pairs={{0,1},{1,0},{2,3},{3,2},{4,5},{5,4},{6,7},{7,6},{8,9},{9,8},{10,11... | collective-permute-start | bytes 983048 | tf_op jit(solution)/shard_map/ppermute | solution.py:485
  1.7 1.6 %shard_map.113 = (f32[80,1024]{1,0:T(8,128)S(1)}, f32[80,1024]{1,0:T(8,128)S(1)}, f32[80,1024]{1,0:T(8,128)S(1)}, f32[80,640]{1,0:T(8,128)S(1)}, bf16[80,640]{1,...) custom-call(s32[16,128]{1,0:T(8,128)} %bitcast.21, f32[1,128]{1,0:T(1,128)} %bitcast.22, ...), custom_call_target="tpu_custom_call" | custom-call | flops 1000000000 | tf_op jit(solution)/shard_map/pallas_call | solution.py:439
  3.8 0.7 %collective-permute-start.3 = (bf16[80,640]{1,0:T(8,128)(2,1)S(1)}, bf16[80,640]{1,0:T(8,128)(2,1)S(1)}, u32[]{:S(2)}, u32[]{:S(2)}) collective-permute-start(bf16[80,640]{1,0:T(8,128)(2,1)S(1)} %get-tuple-element.44), channel_id=1, source_target_pairs={{1,8},{9,16},{17,24},{8,1},{16,9},{24,17},{3,10},{11,18},{19,26},{... | collective-permute-start | bytes 307208 | tf_op jit(solution)/shard_map/ppermute | solution.py:488
  4.5 4.3 %collective-permute-start.6 = (f32[40,256]{1,0:T(8,128)S(1)}, f32[40,256]{1,0:T(8,128)S(1)}, u32[]{:S(2)}, u32[]{:S(2)}) collective-permute-start(f32[40,256]{1,0:T(8,128)S(1)} %get-tuple-element.50.own_par), channel_id=1, source_target_pairs={{0,1},{1,0},{2,3},{3,2},{4,5},{5,4},{6,7},{7,6},{8,9},{9,8},{10,11... | collective-permute-start | bytes 122888 | tf_op jit(solution)/shard_map/ppermute | solution.py:485
  9.5 1.2 %shard_map.115.after.hot = bf16[1024,2048]{1,0:T(8,128)(2,1)S(1)} custom-call(s32[1,1]{1,0:T(1,128)S(6)} %copy.24.counts, f32[80,640]{1,0:T(8,128)S(1)} %get-tuple-element.43.after.inner, s32[16,128]{1,0:T(8,128)S(1)} %get-tuple-element.45.places), custom_call_target="tpu_custom_call" | custom-call | flops 1000000000 | tf_op jit(solution)/shard_map/pallas_call | solution.py:439
  11.0 3.7 %collective-permute-start.4 = (bf16[80,128]{1,0:T(8,128)(2,1)S(1)}, bf16[80,128]{1,0:T(8,128)(2,1)S(1)}, u32[]{:S(2)}, u32[]{:S(2)}) collective-permute-start(bf16[80,128]{1,0:T(8,128)(2,1)S(1)} %get-tuple-element.49.after.own), channel_id=1, source_target_pairs={{2,4},{6,0},{4,2},{0,6},{3,5},{7,1},{5,3},{1,7},{10,12},{14,8},{12... | collective-permute-start | bytes 61448 | tf_op jit(solution)/shard_map/ppermute | solution.py:458
  14.7 1.4 %shard_map.117 = (bf16[256,1024]{1,0:T(8,128)(2,1)S(1)}, f32[8,1024]{1,0:T(8,128)S(1)}) custom-call(bf16[80,128]{1,0:T(8,128)(2,1)S(1)} %get-tuple-element.49.after.own, bf16[1024,2048]{1,0:T(8,128)(2,1)S(1)} %shard_map.115.after.hot, bf16[2,16,128,128]{3,2,1,0:T(8,128)(2,1)S(1)} %bitcast.11), custom_call_target="tpu_custom_call" | custom-call | flops 1000000000 | tf_op jit(solution)/shard_map/pallas_call | solution.py:439
  16.1 0.6 %collective-permute-done.4.west = bf16[80,128]{1,0:T(8,128)(2,1)S(1)} collective-permute-done((bf16[80,128]{1,0:T(8,128)(2,1)S(1)}, bf16[80,128]{1,0:T(8,128)(2,1)S(1)}, u32[]{:S(2)}, u32[]{:S(2)}) %collective-permute-start.4) | collective-permute-done | bytes 20512 | tf_op jit(solution)/shard_map/ppermute | solution.py:458
  16.6 1.9 %collective-permute-done.5.east = bf16[80,128]{1,0:T(8,128)(2,1)S(1)} collective-permute-done((bf16[80,128]{1,0:T(8,128)(2,1)S(1)}, bf16[80,128]{1,0:T(8,128)(2,1)S(1)}, u32[]{:S(2)}, u32[]{:S(2)}) %collective-permute-start.5) | collective-permute-done | bytes 20512 | tf_op jit(solution)/shard_map/ppermute | solution.py:458
  18.5 1.9 %shard_map.118 = (bf16[80,1024]{1,0:T(8,128)(2,1)S(1)}, bf16[80,1024]{1,0:T(8,128)(2,1)S(1)}, bf16[96,384]{1,0:T(8,128)(2,1)S(1)}, bf16[80,384]{1,0:T(8,128)(2,1...) custom-call(f32[80,1536]{1,0:T(8,128)S(1)} %get-tuple-element.46.win_i, f32[80,1536]{1,0:T(8,128)S(1)} %get-tuple-element.47.win_u, ...), custom_call_target="tpu_custom_call" | custom-call | flops 1000000000 | tf_op jit(solution)/shard_map/pallas_call | solution.py:439
  20.5 2.0 %collective-permute-start.8 = (bf16[80,384]{1,0:T(8,128)(2,1)S(1)}, bf16[80,384]{1,0:T(8,128)(2,1)S(1)}, u32[]{:S(2)}, u32[]{:S(2)}) collective-permute-start(bf16[80,384]{1,0:T(8,128)(2,1)S(1)} %get-tuple-element.57), channel_id=1, source_target_pairs={{0,1},{1,0},{2,3},{3,2},{4,5},{5,4},{6,7},{7,6},{8,9},{9,8},{10,11... | collective-permute-start | bytes 184328 | tf_op jit(solution)/shard_map/ppermute | solution.py:485
  22.5 0.9 %collective-permute-done.8.inner = bf16[80,384]{1,0:T(8,128)(2,1)S(1)} collective-permute-done((bf16[80,384]{1,0:T(8,128)(2,1)S(1)}, bf16[80,384]{1,0:T(8,128)(2,1)S(1)}, u32[]{:S(2)}, u32[]{:S(2)}) %collective-permute-start.8) | collective-permute-done | bytes 61472 | tf_op jit(solution)/shard_map/ppermute | solution.py:485
  23.4 1.7 %collective-permute-done.7.edge = bf16[96,384]{1,0:T(8,128)(2,1)S(1)} collective-permute-done((bf16[96,384]{1,0:T(8,128)(2,1)S(1)}, bf16[96,384]{1,0:T(8,128)(2,1)S(1)}, u32[]{:S(2)}, u32[]{:S(2)}) %collective-permute-start.7) | collective-permute-done | bytes 73760 | tf_op jit(solution)/shard_map/ppermute | solution.py:488
  25.4 0.5 %collective-permute-start.10 = (bf16[80,128]{1,0:T(8,128)(2,1)S(1)}, bf16[80,128]{1,0:T(8,128)(2,1)S(1)}, u32[]{:S(2)}, u32[]{:S(2)}) collective-permute-start(bf16[80,128]{1,0:T(8,128)(2,1)S(1)} %get-tuple-element.61.fown), channel_id=1, source_target_pairs={{0,2},{4,6},{2,0},{6,4},{1,3},{5,7},{3,1},{7,5},{8,10},{12,14},{10... | collective-permute-start | bytes 61448 | tf_op jit(solution)/shard_map/ppermute | solution.py:458
  25.9 1.4 %collective-permute-start.9 = (bf16[80,128]{1,0:T(8,128)(2,1)S(1)}, bf16[80,128]{1,0:T(8,128)(2,1)S(1)}, u32[]{:S(2)}, u32[]{:S(2)}) collective-permute-start(bf16[80,128]{1,0:T(8,128)(2,1)S(1)} %get-tuple-element.61.fown), channel_id=1, source_target_pairs={{2,4},{6,0},{4,2},{0,6},{3,5},{7,1},{5,3},{1,7},{10,12},{14,8},{12... | collective-permute-start | bytes 61448 | tf_op jit(solution)/shard_map/ppermute | solution.py:458
  27.3 1.6 %collective-permute-start.11 = (f32[8,128]{1,0:T(8,128)S(1)}, f32[8,128]{1,0:T(8,128)S(1)}, u32[]{:S(2)}, u32[]{:S(2)}) collective-permute-start(f32[8,128]{1,0:T(8,128)S(1)} %get-tuple-element.58.cost), channel_id=1, source_target_pairs={{0,4},{2,6},{4,0},{6,2},{1,5},{3,7},{5,1},{7,3},{8,12},{10,14},{12... | collective-permute-start | bytes 12296 | tf_op jit(solution)/shard_map/ppermute | solution.py:464
  28.9 2.9 %collective-permute-done.11.refs_0_ = f32[8,128]{1,0:T(8,128)S(1)} collective-permute-done((f32[8,128]{1,0:T(8,128)S(1)}, f32[8,128]{1,0:T(8,128)S(1)}, u32[]{:S(2)}, u32[]{:S(2)}) %collective-permute-start.11) | collective-permute-done | bytes 4128 | tf_op jit(solution)/shard_map/ppermute | solution.py:464
  31.8 1.1 %collective-permute-start.12 = (f32[8,128]{1,0:T(8,128)S(1)}, f32[8,128]{1,0:T(8,128)S(1)}, u32[]{:S(2)}, u32[]{:S(2)}) collective-permute-start(f32[8,128]{1,0:T(8,128)S(1)} %collective-permute-done.11.refs_0_), channel_id=1, source_target_pairs={{0,8},{8,0},{16,24},{24,16},{1,9},{9,1},{17,25},{25,17},{2,10},{10... | collective-permute-start | bytes 12296 | tf_op jit(solution)/shard_map/ppermute | solution.py:543
  32.9 2.5 %collective-permute-done.12.refs_1_ = f32[8,128]{1,0:T(8,128)S(1)} collective-permute-done((f32[8,128]{1,0:T(8,128)S(1)}, f32[8,128]{1,0:T(8,128)S(1)}, u32[]{:S(2)}, u32[]{:S(2)}) %collective-permute-start.12) | collective-permute-done | bytes 4128 | tf_op jit(solution)/shard_map/ppermute | solution.py:543
  35.5 1.4 %shard_map.121 = (f32[320,128]{1,0:T(8,128)S(1)}, f32[320,128]{1,0:T(8,128)S(1)}) custom-call(f32[80,1536]{1,0:T(8,128)S(1)} %get-tuple-element.59.win_1, f32[80,1536]{1,0:T(8,128)S(1)} %get-tuple-element.60.win_2, bf16[80,128]{1,0:T(8,128)(2,1)S(1)} %collective-permute-done.9.one.fwest, bf16[80,128]{1,0:T(8,128)(2,1)S(1)} %get-tuple-element.61.fown, ...), custom_call_target="tpu_custom_call" | custom-call | flops 1000000000 | tf_op jit(solution)/shard_map/pallas_call | solution.py:439
  37.1 3.4 %collective-permute-start.14 = (f32[8,128]{1,0:T(8,128)S(1)}, f32[8,128]{1,0:T(8,128)S(1)}, u32[]{:S(2)}, u32[]{:S(2)}) collective-permute-start(f32[8,128]{1,0:T(8,128)S(1)} %shard_map.120.after), channel_id=1, source_target_pairs={{0,16},{8,24},{16,0},{24,8},{1,17},{9,25},{17,1},{25,9},{2,18},{10... | collective-permute-start | bytes 12296 | tf_op jit(solution)/shard_map/ppermute | solution.py:464
  40.4 1.6 %collective-permute-done.14 = f32[8,128]{1,0:T(8,128)S(1)} collective-permute-done((f32[8,128]{1,0:T(8,128)S(1)}, f32[8,128]{1,0:T(8,128)S(1)}, u32[]{:S(2)}, u32[]{:S(2)}) %collective-permute-start.14) | collective-permute-done | bytes 4128 | tf_op jit(solution)/shard_map/ppermute | solution.py:464
  42.0 0.7 %shard_map.122.begun = f32[40,16,128]{2,1,0:T(8,128)} custom-call(f32[40,8,128]{2,1,0:T(8,128)S(1)} %bitcast.13), custom_call_target="tpu_custom_call" | custom-call | flops 1000000000 | tf_op jit(solution)/shard_map/pallas_call | solution.py:439
  43.2 0.7 %shard_map.123 = (f32[40,16,128]{2,1,0:T(8,128)}, f32[1,1]{1,0:T(1,128)}) custom-call(f32[40,8,128]{2,1,0:T(8,128)S(1)} %bitcast.12, f32[8,128]{1,0:T(8,128)S(1)} %add.3.cost, f32[8,128]{1,0:T(8,128)S(1)} %collective-permute-done.15.cost_2, f32[40,16,128]{2,1,0:T(8,128)} %shard_map.122.begun), custom_call_target="tpu_custom_call", output_to_operand_aliasing={{0}: (3, {})} | custom-call | flops 1000000000 | tf_op jit(solution)/shard_map/pallas_call | solution.py:439
  (22 shorter events, 2.3 us)
Async XLA Ops:
  0.6 2.7 %collective-permute-start = (f32[640,128]{1,0:T(8,128)}, f32[640,128]{1,0:T(8,128)S(1)}, u32[]{:S(2)}, u32[]{:S(2)}) collective-permute-start(f32[640,128]{1,0:T(8,128)} %bitcast.14), channel_id=1, source_target_pairs={{0,1},{1,0},{2,3},{3,2},{4,5},{5,4},{6,7},{7,6},{8,9},{9,8},{10,11... | collective-permute-start | bytes 983048 | tf_op jit(solution)/shard_map/ppermute | solution.py:485
  1.2 2.1 %collective-permute-start.1 = (f32[640,128]{1,0:T(8,128)}, f32[640,128]{1,0:T(8,128)S(1)}, u32[]{:S(2)}, u32[]{:S(2)}) collective-permute-start(f32[640,128]{1,0:T(8,128)} %bitcast.16), channel_id=1, source_target_pairs={{0,1},{1,0},{2,3},{3,2},{4,5},{5,4},{6,7},{7,6},{8,9},{9,8},{10,11... | collective-permute-start | bytes 983048 | tf_op jit(solution)/shard_map/ppermute | solution.py:485
  1.3 2.3 %collective-permute-start.2 = (f32[640,128]{1,0:T(8,128)}, f32[640,128]{1,0:T(8,128)S(1)}, u32[]{:S(2)}, u32[]{:S(2)}) collective-permute-start(f32[640,128]{1,0:T(8,128)} %bitcast.18), channel_id=1, source_target_pairs={{0,1},{1,0},{2,3},{3,2},{4,5},{5,4},{6,7},{7,6},{8,9},{9,8},{10,11... | collective-permute-start | bytes 983048 | tf_op jit(solution)/shard_map/ppermute | solution.py:485
  3.8 6.8 %collective-permute-start.3 = (bf16[80,640]{1,0:T(8,128)(2,1)S(1)}, bf16[80,640]{1,0:T(8,128)(2,1)S(1)}, u32[]{:S(2)}, u32[]{:S(2)}) collective-permute-start(bf16[80,640]{1,0:T(8,128)(2,1)S(1)} %get-tuple-element.44), channel_id=1, source_target_pairs={{1,8},{9,16},{17,24},{8,1},{16,9},{24,17},{3,10},{11,18},{19,26},{... | collective-permute-start | bytes 307208 | tf_op jit(solution)/shard_map/ppermute | solution.py:488
  4.5 11.5 %collective-permute-start.6 = (f32[40,256]{1,0:T(8,128)S(1)}, f32[40,256]{1,0:T(8,128)S(1)}, u32[]{:S(2)}, u32[]{:S(2)}) collective-permute-start(f32[40,256]{1,0:T(8,128)S(1)} %get-tuple-element.50.own_par), channel_id=1, source_target_pairs={{0,1},{1,0},{2,3},{3,2},{4,5},{5,4},{6,7},{7,6},{8,9},{9,8},{10,11... | collective-permute-start | bytes 122888 | tf_op jit(solution)/shard_map/ppermute | solution.py:485
  9.4 5.2 %copy-start = (bf16[2,1,1,16,128,128]{5,4,3,2,1,0:T(8,128)(2,1)S(1)}, bf16[2,1,1,16,128,128]{5,4,3,2,1,0:T(8,128)(2,1)}, u32[]{:S(2)}) copy-start(bf16[2,1,1,16,128,128]{5,4,3,2,1,0:T(8,128)(2,1)} %param.17) | copy-start | bytes 3145732
  11.0 5.7 %collective-permute-start.4 = (bf16[80,128]{1,0:T(8,128)(2,1)S(1)}, bf16[80,128]{1,0:T(8,128)(2,1)S(1)}, u32[]{:S(2)}, u32[]{:S(2)}) collective-permute-start(bf16[80,128]{1,0:T(8,128)(2,1)S(1)} %get-tuple-element.49.after.own), channel_id=1, source_target_pairs={{2,4},{6,0},{4,2},{0,6},{3,5},{7,1},{5,3},{1,7},{10,12},{14,8},{12... | collective-permute-start | bytes 61448 | tf_op jit(solution)/shard_map/ppermute | solution.py:458
  14.6 3.9 %collective-permute-start.5 = (bf16[80,128]{1,0:T(8,128)(2,1)S(1)}, bf16[80,128]{1,0:T(8,128)(2,1)S(1)}, u32[]{:S(2)}, u32[]{:S(2)}) collective-permute-start(bf16[80,128]{1,0:T(8,128)(2,1)S(1)} %get-tuple-element.49.after.own), channel_id=1, source_target_pairs={{0,2},{4,6},{2,0},{6,4},{1,3},{5,7},{3,1},{7,5},{8,10},{12,14},{10... | collective-permute-start | bytes 61448 | tf_op jit(solution)/shard_map/ppermute | solution.py:458
  20.4 4.7 %collective-permute-start.7 = (bf16[96,384]{1,0:T(8,128)(2,1)S(1)}, bf16[96,384]{1,0:T(8,128)(2,1)S(1)}, u32[]{:S(2)}, u32[]{:S(2)}) collective-permute-start(bf16[96,384]{1,0:T(8,128)(2,1)S(1)} %get-tuple-element.56), channel_id=1, source_target_pairs={{1,8},{9,16},{17,24},{25,0},{8,1},{16,9},{24,17},{0,25},{3,10},{11... | collective-permute-start | bytes 221192 | tf_op jit(solution)/shard_map/ppermute | solution.py:488
  20.5 2.9 %collective-permute-start.8 = (bf16[80,384]{1,0:T(8,128)(2,1)S(1)}, bf16[80,384]{1,0:T(8,128)(2,1)S(1)}, u32[]{:S(2)}, u32[]{:S(2)}) collective-permute-start(bf16[80,384]{1,0:T(8,128)(2,1)S(1)} %get-tuple-element.57), channel_id=1, source_target_pairs={{0,1},{1,0},{2,3},{3,2},{4,5},{5,4},{6,7},{7,6},{8,9},{9,8},{10,11... | collective-permute-start | bytes 184328 | tf_op jit(solution)/shard_map/ppermute | solution.py:485
  25.4 10.1 %collective-permute-start.10 = (bf16[80,128]{1,0:T(8,128)(2,1)S(1)}, bf16[80,128]{1,0:T(8,128)(2,1)S(1)}, u32[]{:S(2)}, u32[]{:S(2)}) collective-permute-start(bf16[80,128]{1,0:T(8,128)(2,1)S(1)} %get-tuple-element.61.fown), channel_id=1, source_target_pairs={{0,2},{4,6},{2,0},{6,4},{1,3},{5,7},{3,1},{7,5},{8,10},{12,14},{10... | collective-permute-start | bytes 61448 | tf_op jit(solution)/shard_map/ppermute | solution.py:458
  25.9 9.6 %collective-permute-start.9 = (bf16[80,128]{1,0:T(8,128)(2,1)S(1)}, bf16[80,128]{1,0:T(8,128)(2,1)S(1)}, u32[]{:S(2)}, u32[]{:S(2)}) collective-permute-start(bf16[80,128]{1,0:T(8,128)(2,1)S(1)} %get-tuple-element.61.fown), channel_id=1, source_target_pairs={{2,4},{6,0},{4,2},{0,6},{3,5},{7,1},{5,3},{1,7},{10,12},{14,8},{12... | collective-permute-start | bytes 61448 | tf_op jit(solution)/shard_map/ppermute | solution.py:458
  27.3 4.5 %collective-permute-start.11 = (f32[8,128]{1,0:T(8,128)S(1)}, f32[8,128]{1,0:T(8,128)S(1)}, u32[]{:S(2)}, u32[]{:S(2)}) collective-permute-start(f32[8,128]{1,0:T(8,128)S(1)} %get-tuple-element.58.cost), channel_id=1, source_target_pairs={{0,4},{2,6},{4,0},{6,2},{1,5},{3,7},{5,1},{7,3},{8,12},{10,14},{12... | collective-permute-start | bytes 12296 | tf_op jit(solution)/shard_map/ppermute | solution.py:464
  31.8 3.6 %collective-permute-start.12 = (f32[8,128]{1,0:T(8,128)S(1)}, f32[8,128]{1,0:T(8,128)S(1)}, u32[]{:S(2)}, u32[]{:S(2)}) collective-permute-start(f32[8,128]{1,0:T(8,128)S(1)} %collective-permute-done.11.refs_0_), channel_id=1, source_target_pairs={{0,8},{8,0},{16,24},{24,16},{1,9},{9,1},{17,25},{25,17},{2,10},{10... | collective-permute-start | bytes 12296 | tf_op jit(solution)/shard_map/ppermute | solution.py:543
  37.0 6.2 %collective-permute-start.13 = (f32[320,128]{1,0:T(8,128)S(1)}, f32[320,128]{1,0:T(8,128)S(1)}, u32[]{:S(2)}, u32[]{:S(2)}) collective-permute-start(f32[320,128]{1,0:T(8,128)S(1)} %get-tuple-element.64), channel_id=1, source_target_pairs={{0,1},{1,0},{2,3},{3,2},{4,5},{5,4},{6,7},{7,6},{8,9},{9,8},{10,11... | collective-permute-start | bytes 491528 | tf_op jit(solution)/shard_map/ppermute | solution.py:485
  37.1 5.0 %collective-permute-start.14 = (f32[8,128]{1,0:T(8,128)S(1)}, f32[8,128]{1,0:T(8,128)S(1)}, u32[]{:S(2)}, u32[]{:S(2)}) collective-permute-start(f32[8,128]{1,0:T(8,128)S(1)} %shard_map.120.after), channel_id=1, source_target_pairs={{0,16},{8,24},{16,0},{24,8},{1,17},{9,25},{17,1},{25,9},{2,18},{10... | collective-permute-start | bytes 12296 | tf_op jit(solution)/shard_map/ppermute | solution.py:464
  42.0 1.2 %collective-permute-start.15 = (f32[8,128]{1,0:T(8,128)S(1)}, f32[8,128]{1,0:T(8,128)S(1)}, u32[]{:S(2)}, u32[]{:S(2)}) collective-permute-start(f32[8,128]{1,0:T(8,128)S(1)} %add.3.cost), channel_id=1, source_target_pairs={{0,1},{1,0},{2,3},{3,2},{4,5},{5,4},{6,7},{7,6},{8,9},{9,8},{10,11... | collective-permute-start | bytes 12296 | tf_op jit(solution)/shard_map/ppermute | solution.py:485

commit v6 on v5

--- a/solution.py
+++ b/solution.py
@@ -26,15 +26,13 @@
     return ref[:, p * B : (p + 1) * B]
 
 
-def pack_edges(fields, rows):
-    packed = None
+def pack_edges(fields, rows, which, packed=None):
     for f, field in enumerate(fields):
-        for q in range(rows):
+        for q in which:
             rolled = roll(field(q + 1), (f * rows + q) * GROUP + 2)
             if packed is None:
-                lane = lanes_of(rolled.shape[0])
                 packed = jnp.zeros_like(rolled)
-            packed = jnp.where(lane // GROUP == f * rows + q, rolled, packed)
+            packed = jnp.where(lanes_of(rolled.shape[0]) // GROUP == f * rows + q, rolled, packed)
     return packed
 
 
@@ -208,7 +206,18 @@
     win[:, (count - HALO) * B : (count - HALO + width) * B] = jnp.where(low, near, far)
 
 
-def windows(main_i, main_u, main_v, inner, edge, after, win_i, win_u, win_v, packed):
+def own_row(main, p):
+    return block(main, p - HALO)
+
+
+def pack_own(rows, main_i, main_u, main_v, packed):
+    scaled = [functools.partial(own_row, main) for main in (main_i, main_u, main_v)]
+    both = pack_edges(scaled, rows, range(1, rows - 1))
+    field = lanes_of(both.shape[0]) // (GROUP * rows)
+    packed[...] = (both * jnp.where(field == 0, 1.0, 0.5)).astype(packed.dtype)
+
+
+def windows(main_i, main_u, main_v, inner, edge, after, own, win_i, win_u, win_v, packed):
     low = lax.axis_index("lev") == 0
     count = win_i.shape[1] // B
     k = 0
@@ -217,8 +226,9 @@
         span = slice(k * B, (k + width) * B)
         fill_halo(win, scale * inner[:, span], scale * edge[:, span].astype(jnp.float32), low, width)
         k += width
+    rows = count - 2
     packed[...] = pack_edges(
-        [functools.partial(block, win) for win in (win_i, win_u, win_v)], count - 2
+        [functools.partial(block, win) for win in (win_i, win_u, win_v)], rows, (0, rows - 1), own[...].astype(jnp.float32)
     ).astype(packed.dtype)
 
 
@@ -319,7 +329,7 @@
         far = jnp.where(inside, edge[:levels, span].astype(jnp.float32), 0.0)
         fill_halo(win, inner[:, span].astype(jnp.float32), far, low, width)
         k += width
-    both = pack_edges([functools.partial(block, win) for win in (win_2, win_1)], count - 2)
+    both = pack_edges([functools.partial(block, win) for win in (win_2, win_1)], count - 2, range(count - 2))
     here = cost[...] + carried_in(edge[levels:, :B].astype(jnp.float32), 0)[: cost.shape[0]]
     total[...] = here
     lane = lanes_of(both.shape[0])
@@ -514,9 +524,10 @@
         aliases={3 + i: i for i in range(5)},
     )(*others, *sorted_rows)
     edge = across(edge, inside)
+    (own,) = call(functools.partial(pack_own, count - 2), [packed])(*mains)
     other_par = swap(own_par)
     (hot,) = call(one_hot, [((columns, slots * B), bf16)], smem=1)(counts, inner, places)
-    win_i, win_u, win_v, own = call(windows, [win] * 3 + [packed])(*mains, inner, edge, hot)
+    win_i, win_u, win_v, own = call(windows, [win] * 3 + [packed])(*mains, inner, edge, hot, own)
     observed, live = call(
         by_column,
         [((steps * channels, columns), bf16), ((8, columns), f32)],

time: 44.1 us -> 44.5 us (level)
  starting transfers between devices: 19.9 us -> 23.1 us
  waiting for transfers between devices: 12.9 us -> 9.87 us
    ppermute x2, waiting for transfers between devices: 1.74 us -> 0.01 us  [across(): return lax.ppermute(x, ('lat', 'lev'), which)]
    ppermute x1, starting transfers between devices: 1.1 us -> 2.8 us  [body(): more = [far_cost, lax.ppermute(far_cost, 'lat', flip)]]
    ppermute x7, starting transfers between devices: 7.44 us -> 6.02 us  [swap(): return lax.ppermute(x, 'lev', [(0, 1), (1, 0)])]
    ppermute x4, starting transfers between devices: 5.63 us -> 7.03 us  [beside(): lax.ppermute(x, 'lon', pairs + [(b, a) for a, b in pairs] if count > 2 el...]
    ppermute x1, waiting for transfers between devices: 2.5 us -> 1.58 us  [body(): more = [far_cost, lax.ppermute(far_cost, 'lat', flip)]]
    ppermute x2, starting transfers between devices: 4.96 us -> 5.79 us  [ring(): lax.ppermute(x, axis, [(i, (i + shift) % count) for i in range(count)])]
    ppermute x2, starting transfers between devices: 0.74 us -> 1.44 us  [across(): return lax.ppermute(x, ('lat', 'lev'), which)]
    pallas_call x11 -> x12, Pallas kernels: 9.72 us -> 9.86 us  [run(): pl.pallas_call(kernel, out_shape=[jax.ShapeDtypeStruct(shape, dtype) for...]
  transfers between devices with their start and end apart: 16 -> 16, of which waited for: 9 -> 7; matrix products, arithmetic and copies ran while one was open for 0% -> 0% of each run, Pallas kernels for 12% -> 12%
where the time goes in v6:
time: 44.5 us; the launch traced here: 44.2 us
  starting transfers between devices  23.1 us (52%)
  waiting for transfers between devices  9.87 us (22%)
  Pallas kernels  9.86 us (22%)
  between operations  1.43 us (3%)
    pallas_call x12, Pallas kernels, run(): pl.pallas_call(kernel, out_shape=[jax.ShapeDtypeStruct(shape, dtype) for...  9.86 us
    ppermute x4, starting transfers between devices, beside(): lax.ppermute(x, 'lon', pairs + [(b, a) for a, b in pairs] if count > 2 el...  7.03 us
    ppermute x7, starting transfers between devices, swap(): return lax.ppermute(x, 'lev', [(0, 1), (1, 0)])  6.02 us
    ppermute x2, starting transfers between devices, ring(): lax.ppermute(x, axis, [(i, (i + shift) % count) for i in range(count)])  5.79 us
    ppermute x2, waiting for transfers between devices, ring(): lax.ppermute(x, axis, [(i, (i + shift) % count) for i in range(count)])  4.49 us
    ppermute x1, starting transfers between devices, body(): more = [far_cost, lax.ppermute(far_cost, 'lat', flip)]  2.8 us
    ppermute x4, waiting for transfers between devices, beside(): lax.ppermute(x, 'lon', pairs + [(b, a) for a, b in pairs] if count > 2 el...  2.4 us
    ppermute x1, waiting for transfers between devices, body(): more = [far_cost, lax.ppermute(far_cost, 'lat', flip)]  1.58 us
  transfers between devices with their start and end apart: 16, of which 7 were waited for; matrix products, arithmetic and copies ran while one was open for 0% of the time, Pallas kernels for 12%

profile of v6, /device:TPU:0, one launch (start us, length us, event | category | flops | bytes accessed | tf_op | source)
XLA Modules:
  0.0 44.2 jit_solution(3892401861503892965)
XLA Ops:
  0.6 0.6 %collective-permute-start = (f32[640,128]{1,0:T(8,128)}, f32[640,128]{1,0:T(8,128)S(1)}, u32[]{:S(2)}, u32[]{:S(2)}) collective-permute-start(f32[640,128]{1,0:T(8,128)} %bitcast.14), channel_id=1, source_target_pairs={{0,1},{1,0},{2,3},{3,2},{4,5},{5,4},{6,7},{7,6},{8,9},{9,8},{10,11... | collective-permute-start | bytes 983048 | tf_op jit(solution)/shard_map/ppermute | solution.py:495
  1.3 0.4 collective-permute-start.2
  1.7 1.6 %shard_map.113 = (f32[80,1024]{1,0:T(8,128)S(1)}, f32[80,1024]{1,0:T(8,128)S(1)}, f32[80,1024]{1,0:T(8,128)S(1)}, f32[80,640]{1,0:T(8,128)S(1)}, bf16[80,640]{1,...) custom-call(s32[16,128]{1,0:T(8,128)} %bitcast.21, f32[1,128]{1,0:T(1,128)} %bitcast.22, ...), custom_call_target="tpu_custom_call" | custom-call | flops 1000000000 | tf_op jit(solution)/shard_map/pallas_call | solution.py:449
  4.4 0.7 %collective-permute-start.3 = (bf16[80,640]{1,0:T(8,128)(2,1)S(1)}, bf16[80,640]{1,0:T(8,128)(2,1)S(1)}, u32[]{:S(2)}, u32[]{:S(2)}) collective-permute-start(bf16[80,640]{1,0:T(8,128)(2,1)S(1)} %get-tuple-element.44), channel_id=1, source_target_pairs={{1,8},{9,16},{17,24},{8,1},{16,9},{24,17},{3,10},{11,18},{19,26},{... | collective-permute-start | bytes 307208 | tf_op jit(solution)/shard_map/ppermute | solution.py:498
  5.4 1.2 %shard_map.115.after.hot = bf16[1024,2048]{1,0:T(8,128)(2,1)S(1)} custom-call(s32[1,1]{1,0:T(1,128)S(6)} %copy.24.counts, f32[80,640]{1,0:T(8,128)S(1)} %get-tuple-element.43.after.inner, s32[16,128]{1,0:T(8,128)S(1)} %get-tuple-element.45.places), custom_call_target="tpu_custom_call" | custom-call | flops 1000000000 | tf_op jit(solution)/shard_map/pallas_call | solution.py:449
  6.7 5.1 %collective-permute-start.4 = (bf16[80,128]{1,0:T(8,128)(2,1)S(1)}, bf16[80,128]{1,0:T(8,128)(2,1)S(1)}, u32[]{:S(2)}, u32[]{:S(2)}) collective-permute-start(bf16[80,128]{1,0:T(8,128)(2,1)S(1)} %get-tuple-element.49.after.own), channel_id=1, source_target_pairs={{2,4},{6,0},{4,2},{0,6},{3,5},{7,1},{5,3},{1,7},{10,12},{14,8},{12... | collective-permute-start | bytes 61448 | tf_op jit(solution)/shard_map/ppermute | solution.py:468
  11.8 1.4 %shard_map.118 = (bf16[256,1024]{1,0:T(8,128)(2,1)S(1)}, f32[8,1024]{1,0:T(8,128)S(1)}) custom-call(bf16[80,128]{1,0:T(8,128)(2,1)S(1)} %get-tuple-element.49.after.own, bf16[1024,2048]{1,0:T(8,128)(2,1)S(1)} %shard_map.115.after.hot, bf16[2,16,128,128]{3,2,1,0:T(8,128)(2,1)S(1)} %bitcast.11), custom_call_target="tpu_custom_call" | custom-call | flops 1000000000 | tf_op jit(solution)/shard_map/pallas_call | solution.py:449
  13.2 0.4 collective-permute-done.4.west
  13.6 2.0 %collective-permute-done.5.east = bf16[80,128]{1,0:T(8,128)(2,1)S(1)} collective-permute-done((bf16[80,128]{1,0:T(8,128)(2,1)S(1)}, bf16[80,128]{1,0:T(8,128)(2,1)S(1)}, u32[]{:S(2)}, u32[]{:S(2)}) %collective-permute-start.5) | collective-permute-done | bytes 20512 | tf_op jit(solution)/shard_map/ppermute | solution.py:468
  15.6 1.9 %shard_map.119 = (bf16[80,1024]{1,0:T(8,128)(2,1)S(1)}, bf16[80,1024]{1,0:T(8,128)(2,1)S(1)}, bf16[96,384]{1,0:T(8,128)(2,1)S(1)}, bf16[80,384]{1,0:T(8,128)(2,1...) custom-call(f32[80,1536]{1,0:T(8,128)S(1)} %get-tuple-element.46.win_i, f32[80,1536]{1,0:T(8,128)S(1)} %get-tuple-element.47.win_u, ...), custom_call_target="tpu_custom_call" | custom-call | flops 1000000000 | tf_op jit(solution)/shard_map/pallas_call | solution.py:449
  17.5 0.8 %collective-permute-start.7 = (bf16[96,384]{1,0:T(8,128)(2,1)S(1)}, bf16[96,384]{1,0:T(8,128)(2,1)S(1)}, u32[]{:S(2)}, u32[]{:S(2)}) collective-permute-start(bf16[96,384]{1,0:T(8,128)(2,1)S(1)} %get-tuple-element.56), channel_id=1, source_target_pairs={{1,8},{9,16},{17,24},{25,0},{8,1},{16,9},{24,17},{0,25},{3,10},{11... | collective-permute-start | bytes 221192 | tf_op jit(solution)/shard_map/ppermute | solution.py:498
  18.3 4.6 %collective-permute-start.8 = (bf16[80,384]{1,0:T(8,128)(2,1)S(1)}, bf16[80,384]{1,0:T(8,128)(2,1)S(1)}, u32[]{:S(2)}, u32[]{:S(2)}) collective-permute-start(bf16[80,384]{1,0:T(8,128)(2,1)S(1)} %get-tuple-element.57), channel_id=1, source_target_pairs={{0,1},{1,0},{2,3},{3,2},{4,5},{5,4},{6,7},{7,6},{8,9},{9,8},{10,11... | collective-permute-start | bytes 184328 | tf_op jit(solution)/shard_map/ppermute | solution.py:495
  22.9 0.9 %collective-permute-done.8.inner = bf16[80,384]{1,0:T(8,128)(2,1)S(1)} collective-permute-done((bf16[80,384]{1,0:T(8,128)(2,1)S(1)}, bf16[80,384]{1,0:T(8,128)(2,1)S(1)}, u32[]{:S(2)}, u32[]{:S(2)}) %collective-permute-start.8) | collective-permute-done | bytes 61472 | tf_op jit(solution)/shard_map/ppermute | solution.py:495
  24.3 1.7 %collective-permute-start.9 = (bf16[80,128]{1,0:T(8,128)(2,1)S(1)}, bf16[80,128]{1,0:T(8,128)(2,1)S(1)}, u32[]{:S(2)}, u32[]{:S(2)}) collective-permute-start(bf16[80,128]{1,0:T(8,128)(2,1)S(1)} %get-tuple-element.61.fown), channel_id=1, source_target_pairs={{2,4},{6,0},{4,2},{0,6},{3,5},{7,1},{5,3},{1,7},{10,12},{14,8},{12... | collective-permute-start | bytes 61448 | tf_op jit(solution)/shard_map/ppermute | solution.py:468
  26.0 1.6 %collective-permute-start.11 = (f32[8,128]{1,0:T(8,128)S(1)}, f32[8,128]{1,0:T(8,128)S(1)}, u32[]{:S(2)}, u32[]{:S(2)}) collective-permute-start(f32[8,128]{1,0:T(8,128)S(1)} %get-tuple-element.58.cost), channel_id=1, source_target_pairs={{0,4},{2,6},{4,0},{6,2},{1,5},{3,7},{5,1},{7,3},{8,12},{10,14},{12... | collective-permute-start | bytes 12296 | tf_op jit(solution)/shard_map/ppermute | solution.py:474
  27.6 2.9 %collective-permute-done.11.refs_0_ = f32[8,128]{1,0:T(8,128)S(1)} collective-permute-done((f32[8,128]{1,0:T(8,128)S(1)}, f32[8,128]{1,0:T(8,128)S(1)}, u32[]{:S(2)}, u32[]{:S(2)}) %collective-permute-start.11) | collective-permute-done | bytes 4128 | tf_op jit(solution)/shard_map/ppermute | solution.py:474
  30.5 2.8 %collective-permute-start.12 = (f32[8,128]{1,0:T(8,128)S(1)}, f32[8,128]{1,0:T(8,128)S(1)}, u32[]{:S(2)}, u32[]{:S(2)}) collective-permute-start(f32[8,128]{1,0:T(8,128)S(1)} %collective-permute-done.11.refs_0_), channel_id=1, source_target_pairs={{0,8},{8,0},{16,24},{24,16},{1,9},{9,1},{17,25},{25,17},{2,10},{10... | collective-permute-start | bytes 12296 | tf_op jit(solution)/shard_map/ppermute | solution.py:554
  33.3 1.6 %collective-permute-done.12.refs_1_ = f32[8,128]{1,0:T(8,128)S(1)} collective-permute-done((f32[8,128]{1,0:T(8,128)S(1)}, f32[8,128]{1,0:T(8,128)S(1)}, u32[]{:S(2)}, u32[]{:S(2)}) %collective-permute-start.12) | collective-permute-done | bytes 4128 | tf_op jit(solution)/shard_map/ppermute | solution.py:554
  35.0 1.4 %shard_map.122 = (f32[320,128]{1,0:T(8,128)S(1)}, f32[320,128]{1,0:T(8,128)S(1)}) custom-call(f32[80,1536]{1,0:T(8,128)S(1)} %get-tuple-element.59.win_1, f32[80,1536]{1,0:T(8,128)S(1)} %get-tuple-element.60.win_2, bf16[80,128]{1,0:T(8,128)(2,1)S(1)} %collective-permute-done.9.one.fwest, bf16[80,128]{1,0:T(8,128)(2,1)S(1)} %get-tuple-element.61.fown, ...), custom_call_target="tpu_custom_call" | custom-call | flops 1000000000 | tf_op jit(solution)/shard_map/pallas_call | solution.py:449
  36.6 4.2 %collective-permute-start.14 = (f32[8,128]{1,0:T(8,128)S(1)}, f32[8,128]{1,0:T(8,128)S(1)}, u32[]{:S(2)}, u32[]{:S(2)}) collective-permute-start(f32[8,128]{1,0:T(8,128)S(1)} %shard_map.121.after), channel_id=1, source_target_pairs={{0,16},{8,24},{16,0},{24,8},{1,17},{9,25},{17,1},{25,9},{2,18},{10... | collective-permute-start | bytes 12296 | tf_op jit(solution)/shard_map/ppermute | solution.py:474
  40.8 1.6 %collective-permute-done.14 = f32[8,128]{1,0:T(8,128)S(1)} collective-permute-done((f32[8,128]{1,0:T(8,128)S(1)}, f32[8,128]{1,0:T(8,128)S(1)}, u32[]{:S(2)}, u32[]{:S(2)}) %collective-permute-start.14) | collective-permute-done | bytes 4128 | tf_op jit(solution)/shard_map/ppermute | solution.py:474
  42.4 0.7 %shard_map.123.begun = f32[40,16,128]{2,1,0:T(8,128)} custom-call(f32[40,8,128]{2,1,0:T(8,128)S(1)} %bitcast.13), custom_call_target="tpu_custom_call" | custom-call | flops 1000000000 | tf_op jit(solution)/shard_map/pallas_call | solution.py:449
  43.1 0.5 %collective-permute-done.15.cost_2 = f32[8,128]{1,0:T(8,128)S(1)} collective-permute-done((f32[8,128]{1,0:T(8,128)S(1)}, f32[8,128]{1,0:T(8,128)S(1)}, u32[]{:S(2)}, u32[]{:S(2)}) %collective-permute-start.15) | collective-permute-done | bytes 4128 | tf_op jit(solution)/shard_map/ppermute | solution.py:495
  43.5 0.7 %shard_map.124 = (f32[40,16,128]{2,1,0:T(8,128)}, f32[1,1]{1,0:T(1,128)}) custom-call(f32[40,8,128]{2,1,0:T(8,128)S(1)} %bitcast.12, f32[8,128]{1,0:T(8,128)S(1)} %add.3.cost, f32[8,128]{1,0:T(8,128)S(1)} %collective-permute-done.15.cost_2, f32[40,16,128]{2,1,0:T(8,128)} %shard_map.123.begun), custom_call_target="tpu_custom_call", output_to_operand_aliasing={{0}: (3, {})} | custom-call | flops 1000000000 | tf_op jit(solution)/shard_map/pallas_call | solution.py:449
  (23 shorter events, 1.7 us)
Async XLA Ops:
  0.6 3.4 %collective-permute-start = (f32[640,128]{1,0:T(8,128)}, f32[640,128]{1,0:T(8,128)S(1)}, u32[]{:S(2)}, u32[]{:S(2)}) collective-permute-start(f32[640,128]{1,0:T(8,128)} %bitcast.14), channel_id=1, source_target_pairs={{0,1},{1,0},{2,3},{3,2},{4,5},{5,4},{6,7},{7,6},{8,9},{9,8},{10,11... | collective-permute-start | bytes 983048 | tf_op jit(solution)/shard_map/ppermute | solution.py:495
  1.2 2.9 %collective-permute-start.1 = (f32[640,128]{1,0:T(8,128)}, f32[640,128]{1,0:T(8,128)S(1)}, u32[]{:S(2)}, u32[]{:S(2)}) collective-permute-start(f32[640,128]{1,0:T(8,128)} %bitcast.16), channel_id=1, source_target_pairs={{0,1},{1,0},{2,3},{3,2},{4,5},{5,4},{6,7},{7,6},{8,9},{9,8},{10,11... | collective-permute-start | bytes 983048 | tf_op jit(solution)/shard_map/ppermute | solution.py:495
  1.3 2.8 %collective-permute-start.2 = (f32[640,128]{1,0:T(8,128)}, f32[640,128]{1,0:T(8,128)S(1)}, u32[]{:S(2)}, u32[]{:S(2)}) collective-permute-start(f32[640,128]{1,0:T(8,128)} %bitcast.18), channel_id=1, source_target_pairs={{0,1},{1,0},{2,3},{3,2},{4,5},{5,4},{6,7},{7,6},{8,9},{9,8},{10,11... | collective-permute-start | bytes 983048 | tf_op jit(solution)/shard_map/ppermute | solution.py:495
  3.3 9.9 %collective-permute-start.6 = (f32[40,256]{1,0:T(8,128)S(1)}, f32[40,256]{1,0:T(8,128)S(1)}, u32[]{:S(2)}, u32[]{:S(2)}) collective-permute-start(f32[40,256]{1,0:T(8,128)S(1)} %get-tuple-element.50.own_par), channel_id=1, source_target_pairs={{0,1},{1,0},{2,3},{3,2},{4,5},{5,4},{6,7},{7,6},{8,9},{9,8},{10,11... | collective-permute-start | bytes 122888 | tf_op jit(solution)/shard_map/ppermute | solution.py:495
  4.4 2.2 %collective-permute-start.3 = (bf16[80,640]{1,0:T(8,128)(2,1)S(1)}, bf16[80,640]{1,0:T(8,128)(2,1)S(1)}, u32[]{:S(2)}, u32[]{:S(2)}) collective-permute-start(bf16[80,640]{1,0:T(8,128)(2,1)S(1)} %get-tuple-element.44), channel_id=1, source_target_pairs={{1,8},{9,16},{17,24},{8,1},{16,9},{24,17},{3,10},{11,18},{19,26},{... | collective-permute-start | bytes 307208 | tf_op jit(solution)/shard_map/ppermute | solution.py:498
  5.4 6.4 %copy-start = (bf16[2,1,1,16,128,128]{5,4,3,2,1,0:T(8,128)(2,1)S(1)}, bf16[2,1,1,16,128,128]{5,4,3,2,1,0:T(8,128)(2,1)}, u32[]{:S(2)}) copy-start(bf16[2,1,1,16,128,128]{5,4,3,2,1,0:T(8,128)(2,1)} %param.17) | copy-start | bytes 3145732
  6.7 6.8 %collective-permute-start.4 = (bf16[80,128]{1,0:T(8,128)(2,1)S(1)}, bf16[80,128]{1,0:T(8,128)(2,1)S(1)}, u32[]{:S(2)}, u32[]{:S(2)}) collective-permute-start(bf16[80,128]{1,0:T(8,128)(2,1)S(1)} %get-tuple-element.49.after.own), channel_id=1, source_target_pairs={{2,4},{6,0},{4,2},{0,6},{3,5},{7,1},{5,3},{1,7},{10,12},{14,8},{12... | collective-permute-start | bytes 61448 | tf_op jit(solution)/shard_map/ppermute | solution.py:468
  11.8 3.8 %collective-permute-start.5 = (bf16[80,128]{1,0:T(8,128)(2,1)S(1)}, bf16[80,128]{1,0:T(8,128)(2,1)S(1)}, u32[]{:S(2)}, u32[]{:S(2)}) collective-permute-start(bf16[80,128]{1,0:T(8,128)(2,1)S(1)} %get-tuple-element.49.after.own), channel_id=1, source_target_pairs={{0,2},{4,6},{2,0},{6,4},{1,3},{5,7},{3,1},{7,5},{8,10},{12,14},{10... | collective-permute-start | bytes 61448 | tf_op jit(solution)/shard_map/ppermute | solution.py:468
  17.5 6.3 %collective-permute-start.7 = (bf16[96,384]{1,0:T(8,128)(2,1)S(1)}, bf16[96,384]{1,0:T(8,128)(2,1)S(1)}, u32[]{:S(2)}, u32[]{:S(2)}) collective-permute-start(bf16[96,384]{1,0:T(8,128)(2,1)S(1)} %get-tuple-element.56), channel_id=1, source_target_pairs={{1,8},{9,16},{17,24},{25,0},{8,1},{16,9},{24,17},{0,25},{3,10},{11... | collective-permute-start | bytes 221192 | tf_op jit(solution)/shard_map/ppermute | solution.py:498
  18.3 5.5 %collective-permute-start.8 = (bf16[80,384]{1,0:T(8,128)(2,1)S(1)}, bf16[80,384]{1,0:T(8,128)(2,1)S(1)}, u32[]{:S(2)}, u32[]{:S(2)}) collective-permute-start(bf16[80,384]{1,0:T(8,128)(2,1)S(1)} %get-tuple-element.57), channel_id=1, source_target_pairs={{0,1},{1,0},{2,3},{3,2},{4,5},{5,4},{6,7},{7,6},{8,9},{9,8},{10,11... | collective-permute-start | bytes 184328 | tf_op jit(solution)/shard_map/ppermute | solution.py:495
  24.0 10.8 %collective-permute-start.10 = (bf16[80,128]{1,0:T(8,128)(2,1)S(1)}, bf16[80,128]{1,0:T(8,128)(2,1)S(1)}, u32[]{:S(2)}, u32[]{:S(2)}) collective-permute-start(bf16[80,128]{1,0:T(8,128)(2,1)S(1)} %get-tuple-element.61.fown), channel_id=1, source_target_pairs={{0,2},{4,6},{2,0},{6,4},{1,3},{5,7},{3,1},{7,5},{8,10},{12,14},{10... | collective-permute-start | bytes 61448 | tf_op jit(solution)/shard_map/ppermute | solution.py:468
  24.3 10.6 %collective-permute-start.9 = (bf16[80,128]{1,0:T(8,128)(2,1)S(1)}, bf16[80,128]{1,0:T(8,128)(2,1)S(1)}, u32[]{:S(2)}, u32[]{:S(2)}) collective-permute-start(bf16[80,128]{1,0:T(8,128)(2,1)S(1)} %get-tuple-element.61.fown), channel_id=1, source_target_pairs={{2,4},{6,0},{4,2},{0,6},{3,5},{7,1},{5,3},{1,7},{10,12},{14,8},{12... | collective-permute-start | bytes 61448 | tf_op jit(solution)/shard_map/ppermute | solution.py:468
  26.0 4.5 %collective-permute-start.11 = (f32[8,128]{1,0:T(8,128)S(1)}, f32[8,128]{1,0:T(8,128)S(1)}, u32[]{:S(2)}, u32[]{:S(2)}) collective-permute-start(f32[8,128]{1,0:T(8,128)S(1)} %get-tuple-element.58.cost), channel_id=1, source_target_pairs={{0,4},{2,6},{4,0},{6,2},{1,5},{3,7},{5,1},{7,3},{8,12},{10,14},{12... | collective-permute-start | bytes 12296 | tf_op jit(solution)/shard_map/ppermute | solution.py:474
  30.5 4.4 %collective-permute-start.12 = (f32[8,128]{1,0:T(8,128)S(1)}, f32[8,128]{1,0:T(8,128)S(1)}, u32[]{:S(2)}, u32[]{:S(2)}) collective-permute-start(f32[8,128]{1,0:T(8,128)S(1)} %collective-permute-done.11.refs_0_), channel_id=1, source_target_pairs={{0,8},{8,0},{16,24},{24,16},{1,9},{9,1},{17,25},{25,17},{2,10},{10... | collective-permute-start | bytes 12296 | tf_op jit(solution)/shard_map/ppermute | solution.py:554
  36.4 7.1 %collective-permute-start.13 = (f32[320,128]{1,0:T(8,128)S(1)}, f32[320,128]{1,0:T(8,128)S(1)}, u32[]{:S(2)}, u32[]{:S(2)}) collective-permute-start(f32[320,128]{1,0:T(8,128)S(1)} %get-tuple-element.64), channel_id=1, source_target_pairs={{0,1},{1,0},{2,3},{3,2},{4,5},{5,4},{6,7},{7,6},{8,9},{9,8},{10,11... | collective-permute-start | bytes 491528 | tf_op jit(solution)/shard_map/ppermute | solution.py:495
  36.6 5.8 %collective-permute-start.14 = (f32[8,128]{1,0:T(8,128)S(1)}, f32[8,128]{1,0:T(8,128)S(1)}, u32[]{:S(2)}, u32[]{:S(2)}) collective-permute-start(f32[8,128]{1,0:T(8,128)S(1)} %shard_map.121.after), channel_id=1, source_target_pairs={{0,16},{8,24},{16,0},{24,8},{1,17},{9,25},{17,1},{25,9},{2,18},{10... | collective-permute-start | bytes 12296 | tf_op jit(solution)/shard_map/ppermute | solution.py:474
  42.4 1.2 %collective-permute-start.15 = (f32[8,128]{1,0:T(8,128)S(1)}, f32[8,128]{1,0:T(8,128)S(1)}, u32[]{:S(2)}, u32[]{:S(2)}) collective-permute-start(f32[8,128]{1,0:T(8,128)S(1)} %add.3.cost), channel_id=1, source_target_pairs={{0,1},{1,0},{2,3},{3,2},{4,5},{5,4},{6,7},{7,6},{8,9},{9,8},{10,11... | collective-permute-start | bytes 12296 | tf_op jit(solution)/shard_map/ppermute | solution.py:495
